TPU v7x, 32 devices: a whole 2x2x4 slice. The times are simulated.
32 devices in a mesh: row: 8 (over y, x, core), col: 4 (over z).
Axes of the slice: x: 2, y: 2, z: 4, core: 2. Of those that a mesh axis runs over, the one named last changes fastest.
Arguments:
- design: bfloat16 [4096, 6144], P(('row', 'col')), may hold values from -0.09375 to 0.09375
- observations: float32 [4096], P(('row', 'col')), may hold values from -6 to 6
- gaps: int32 [4096], P(('row', 'col')), may hold values 0 or 1
- noise_var: float32 [4096], P(('row', 'col')), may hold values from 0.25 to 4
- arc_lengths: int32 [32, 4], P(('row', 'col')), may hold values from 1 to 64, 128 in all within a row
- arc_amp: float32 [32, 4], P(('row', 'col')), may hold values from 0.2 to 2
- arc_decay: float32 [32, 4], P(('row', 'col')), may hold values from 0.3 to 0.95
- plan: int32 [32], P(('row', 'col')), may hold values from 0 to 31, each once
- tile_map: int32 [48], replicated, may hold values from 0 to 47, each once
Outputs:
- gram: float32 [6144, 6144], P('row', 'col')
- normal_rhs: float32 [6144], P('row')
- balanced_obs: float32 [32, 128], P(('row', 'col'))
Inputs may be any that keep to these rules, and one draw needn't show every extreme that they name: `plan`: a permutation of the blocks. `tile_map`: a permutation of the tiles. `arc_lengths`: each block's arc lengths sum to 128; some arc has 64 rows.
All inputs are finite; a program needn't handle non-finite values. No bound on the sum of `gaps` on one device may be relied on, other than what follows from the above.
Results may differ from a plain program's by a relative error of at most 0.004.
Values may be sent and summed in bfloat16 or wider, within the bound.
No kernel may reach another device: no remote copies, remote signals or barrier semaphores. Data moves between devices by JAX's collectives and lax.ppermute only.
A program may use at most 192 MiB of HBM per device.

v0:
```python
import jax
import jax.numpy as jnp
from jax import lax
from jax.experimental import pallas as pl
from jax.experimental.pallas import tpu as pltpu
from jax.sharding import PartitionSpec as P


F32, BF16 = jnp.float32, jnp.bfloat16
ANY = pl.BlockSpec(memory_space=pl.ANY)
VMEM = pl.BlockSpec(memory_space=pltpu.VMEM)
SMEM = pl.BlockSpec(memory_space=pltpu.SMEM)


def factor_math(n, arcs, len_ref, amp_ref, decay_ref, obs_ref, gap_ref, noise_ref):
    lane = lax.broadcasted_iota(jnp.int32, (8, n), 1)
    live = jnp.broadcast_to(gap_ref[...].astype(F32), (8, n))
    noise = jnp.broadcast_to(noise_ref[...], (8, n))
    big_line = lax.broadcasted_iota(jnp.int32, (n, n), 0)
    big_lane = lax.broadcasted_iota(jnp.int32, (n, n), 1)
    arc = jnp.zeros((8, n), jnp.int32)
    first = lane == 0
    arc_line = jnp.zeros((n, n), jnp.int32)
    end = 0
    for k in range(arcs):
        end = end + len_ref[0, k]
        arc = arc + (lane >= end).astype(jnp.int32)
        arc_line = arc_line + (big_line >= end).astype(jnp.int32)
        first = jnp.logical_or(first, lane == end)
    amp = jnp.zeros((8, n), F32)
    decay = jnp.ones((8, n), F32)
    for k in range(arcs):
        amp = jnp.where(arc == k, amp_ref[0, k], amp)
        decay = jnp.where(arc == k, decay_ref[0, k], decay)

    def back(x, shift):
        return pltpu.roll(x, shift, axis=1)

    fresh = (1.0 - decay * decay) * amp
    a = back(decay * decay * noise + fresh * live, 1)
    b = back(fresh * noise, 1)
    c = back(live, 1)
    d = back(noise, 1)
    a = jnp.where(first, 0.0, a)
    b = jnp.where(first, amp, b)
    c = jnp.where(first, 0.0, c)
    d = jnp.where(first, 1.0, d)
    shift = 1
    while shift < n:
        ok = lane >= shift
        pa, pb = jnp.where(ok, back(a, shift), 1.0), jnp.where(ok, back(b, shift), 0.0)
        pc, pd = jnp.where(ok, back(c, shift), 0.0), jnp.where(ok, back(d, shift), 1.0)
        a, b, c, d = a * pa + b * pc, a * pb + b * pd, c * pa + d * pc, c * pb + d * pd
        level = 1.0 / (a + b + c + d)
        a, b, c, d = a * level, b * level, c * level, d * level
        shift *= 2
    variance = b / d
    total = live * variance + noise
    root = 1.0 / jnp.sqrt(total)
    fade = jnp.log(decay * noise / total)
    gain = decay * variance * live / total
    below = big_lane < big_line
    fades = jnp.where(below, jnp.broadcast_to(fade[:1], (n, n)), 0.0)
    mask = below.astype(BF16)
    spans = jnp.zeros((n, n), F32)
    for _ in range(3):
        part = fades.astype(BF16)
        spans = spans + jnp.dot(part, mask, preferred_element_type=F32)
        fades = fades - part.astype(F32)
    diagonal = big_line == big_lane

    def upright(x):
        return jnp.sum(jnp.where(diagonal, jnp.broadcast_to(x[:1], (n, n)), 0.0), axis=1, keepdims=True)

    left = upright(live * root)
    same = jnp.logical_and(below, arc_line == jnp.broadcast_to(arc[:1], (n, n)))
    weight = jnp.where(same, -left * jnp.exp(spans) * jnp.broadcast_to(gain[:1], (n, n)), 0.0)
    weight = jnp.where(diagonal, left, weight)
    white = jnp.sum(weight * jnp.broadcast_to(obs_ref[...], (n, n)), axis=1, keepdims=True)
    white_row = jnp.sum(jnp.where(diagonal, white, 0.0), axis=0, keepdims=True)
    return weight, jnp.broadcast_to(white_row, (8, n))


def factor_kernel(observations, gaps, noise_var, arc_lengths, arc_amp, arc_decay):
    n = observations.shape[0]
    arcs = arc_lengths.shape[1]

    def kernel(len_ref, amp_ref, decay_ref, obs_ref, gap_ref, noise_ref, out_ref):
        out_ref[:n, :], out_ref[n:, :] = factor_math(
            n, arcs, len_ref, amp_ref, decay_ref, obs_ref, gap_ref, noise_ref
        )

    row = (1, n)
    return pl.pallas_call(
        kernel,
        name="factor",
        in_specs=[SMEM] * 3 + [VMEM] * 3,
        out_specs=VMEM,
        out_shape=jax.ShapeDtypeStruct((n + 8, n), F32),
        cost_estimate=pl.CostEstimate(flops=10**8, bytes_accessed=10**5, transcendentals=0),
        compiler_params=pltpu.CompilerParams(vmem_limit_bytes=4 << 20),
    )(
        arc_lengths,
        arc_amp,
        arc_decay,
        observations.reshape(row),
        gaps.reshape(row),
        noise_var.reshape(row),
    )


def split_dot(w, x):
    high = w.astype(BF16)
    low = (w - high.astype(F32)).astype(BF16)
    total = jnp.dot(high, x, preferred_element_type=F32)
    return (total + jnp.dot(low, x, preferred_element_type=F32)).astype(BF16)


def pack(chunk, weight, tile_map, where, rows_axis, cols_axis):
    block_rows, columns = chunk.shape
    tiles = tile_map.shape[0]
    size = columns // tiles
    pairs = rows_axis // 2
    per_row, per_col = tiles // rows_axis, tiles // cols_axis
    wide = (2 * per_row + per_col) * size

    def kernel(map_ref, where_ref, x_ref, *refs):
        outs = refs[-pairs - 1 : -1]
        held = refs[-1]
        row, col = where_ref[0], where_ref[1]

        def fetch(base, count, to):
            for j in range(count):
                at = pl.multiple_of(map_ref[base + j] * size, size)
                held[:, (to + j) * size : (to + j + 1) * size] = x_ref[:, pl.ds(at, size)]

        def finish(start, stop, targets):
            part = held[:, start:stop]
            if weight is not None:
                part = split_dot(refs[0][...], part)
            for target in targets:
                target[:, start:stop] = part

        own = per_row * size
        fetch(col * per_col, per_col, 2 * per_row)
        finish(2 * own, wide, outs)
        for n in range(pairs):
            there = jnp.bitwise_xor(row, 2 * n)
            fetch(there * per_row, per_row, 0)
            fetch(jnp.bitwise_xor(there, 1) * per_row, per_row, per_row)
            finish(0, 2 * own, [outs[n]])

    args = (tile_map, where, chunk) + (() if weight is None else (weight,))
    return pl.pallas_call(
        kernel,
        name="pack",
        in_specs=[SMEM, SMEM] + [VMEM] * (len(args) - 2),
        out_specs=[VMEM] * pairs,
        out_shape=[jax.ShapeDtypeStruct((block_rows, wide), BF16)] * pairs,
        scratch_shapes=[pltpu.VMEM((block_rows, wide), BF16)],
        cost_estimate=pl.CostEstimate(flops=10**9, bytes_accessed=5 * 10**6, transcendentals=0),
        compiler_params=pltpu.CompilerParams(vmem_limit_bytes=24 << 20),
    )(*args)


def gram_first(raw, weights, white, obs, rows_width, cols_width):
    block_rows, wide = raw[0].shape
    count = len(raw) + len(white)
    depth = count * block_rows
    half = rows_width // 2
    step = cols_width // 6 if cols_width % 6 == 0 and (cols_width // 6) % 128 == 0 else 128
    steps = cols_width // step

    def kernel(*refs):
        blocks = refs[:count]
        w_refs = refs[count : count + len(raw)]
        obs_ref = refs[count + len(raw)]
        keep_ref, give_ref, rhs_ref = refs[-7:-4]
        fresh, held, turned, sems = refs[-4:]

        @pl.when(pl.program_id(0) == 0)
        def _():
            copies = []
            for b in range(count):
                to = fresh.at[b] if b < len(raw) else held.at[pl.ds(b * block_rows, block_rows)]
                copies.append(pltpu.make_async_copy(blocks[b], to, sems.at[b]))
                copies[-1].start()
            for b in range(count):
                rows = slice(b * block_rows, (b + 1) * block_rows)
                copies[b].wait()
                if b < len(raw):
                    held[rows, :] = split_dot(w_refs[b][...], fresh[b])
                turned[:, rows] = held[rows, :rows_width].T
            spread = jnp.broadcast_to(obs_ref[...].astype(BF16), (16, depth))
            rhs_ref[...] = jnp.dot(spread, held[:, :rows_width], preferred_element_type=F32)

        at = pl.multiple_of(rows_width + pl.program_id(0) * step, 128)
        right = held[:, pl.ds(at, step)]
        keep_ref[...] = jnp.dot(turned[:half, :], right, preferred_element_type=F32)
        give_ref[...] = jnp.dot(turned[half:, :], right, preferred_element_type=F32)

    tile = pl.BlockSpec((half, step), lambda i: (0, i))
    return pl.pallas_call(
        kernel,
        name="gram_first",
        grid=(steps,),
        in_specs=[ANY] * count + [VMEM] * (len(raw) + 1),
        out_specs=[tile, tile, pl.BlockSpec((16, rows_width), lambda i: (0, 0))],
        out_shape=[jax.ShapeDtypeStruct((half, cols_width), F32)] * 2
        + [jax.ShapeDtypeStruct((16, rows_width), F32)],
        scratch_shapes=[
            pltpu.VMEM((len(raw), block_rows, wide), BF16),
            pltpu.VMEM((depth, wide), BF16),
            pltpu.VMEM((rows_width, depth), BF16),
            pltpu.SemaphoreType.DMA((count,)),
        ],
        cost_estimate=pl.CostEstimate(
            flops=2 * depth * rows_width * cols_width, bytes_accessed=2 * 10**7, transcendentals=0
        ),
        compiler_params=pltpu.CompilerParams(vmem_limit_bytes=48 << 20),
    )(*raw, *white, *weights, obs)


def gram_last(keep, other, mine, theirs, obs, rows_width, cols_width):
    block_rows, wide = mine[0].shape
    count = len(mine) + len(theirs)
    depth = count * block_rows
    half = rows_width // 2
    step = cols_width // 6 if cols_width % 6 == 0 and (cols_width // 6) % 128 == 0 else 128
    steps = cols_width // step

    def kernel(*refs):
        keep_ref, other_ref = refs[:2]
        blocks = refs[2 : 2 + count]
        obs_ref = refs[2 + count]
        out_ref, rhs_ref = refs[-5:-3]
        held, turned, sems = refs[-3:]

        @pl.when(pl.program_id(0) == 0)
        def _():
            copies = []
            for b in range(count):
                to = held.at[pl.ds(b * block_rows, block_rows)]
                copies.append(pltpu.make_async_copy(blocks[b], to, sems.at[b]))
                copies[-1].start()
            total = jnp.zeros((16, half), F32)
            for b in range(count):
                rows = slice(b * block_rows, (b + 1) * block_rows)
                lead = 0 if b < len(mine) else half
                copies[b].wait()
                left = held[rows, lead : lead + half]
                turned[:, rows] = left.T
                spread = jnp.broadcast_to(obs_ref[:, rows].astype(BF16), (16, block_rows))
                total = total + jnp.dot(spread, left, preferred_element_type=F32)
            rhs_ref[...] = total

        at = pl.multiple_of(rows_width + pl.program_id(0) * step, 128)
        right = held[:, pl.ds(at, step)]
        out_ref[...] = (keep_ref[...] + other_ref[...]) + jnp.dot(
            turned[...], right, preferred_element_type=F32
        )

    tile = pl.BlockSpec((half, step), lambda i: (0, i))
    return pl.pallas_call(
        kernel,
        name="gram_last",
        grid=(steps,),
        in_specs=[tile, tile] + [ANY] * count + [VMEM],
        out_specs=[tile, pl.BlockSpec((16, half), lambda i: (0, 0))],
        out_shape=[
            jax.ShapeDtypeStruct((half, cols_width), F32),
            jax.ShapeDtypeStruct((16, half), F32),
        ],
        scratch_shapes=[
            pltpu.VMEM((depth, wide), BF16),
            pltpu.VMEM((half, depth), BF16),
            pltpu.SemaphoreType.DMA((count,)),
        ],
        cost_estimate=pl.CostEstimate(
            flops=2 * depth * half * cols_width, bytes_accessed=2 * 10**7, transcendentals=0
        ),
        compiler_params=pltpu.CompilerParams(vmem_limit_bytes=48 << 20),
    )(keep, other, *mine, *theirs, obs)


def on_device_any(
    rows_axis,
    cols_axis,
    design,
    observations,
    gaps,
    noise_var,
    arc_lengths,
    arc_amp,
    arc_decay,
    plan,
    tile_map,
):
    columns = design.shape[1]
    tiles = tile_map.shape[0]
    size = columns // tiles
    pairs = rows_axis // 2
    rows_width = 2 * (tiles // rows_axis) * size
    cols_width = (tiles // cols_axis) * size
    row, col = lax.axis_index("row"), lax.axis_index("col")
    where = jnp.stack([row, col]).astype(jnp.int32)

    def ring(x, shift):
        return lax.ppermute(x, "col", [(c, (c + shift) % cols_axis) for c in range(cols_axis)])

    def swap(x, mask):
        return lax.ppermute(x, "row", [(r, r ^ mask) for r in range(rows_axis)])

    def spread(parts):
        return [parts[0]] + [swap(parts[n], 2 * n) for n in range(1, pairs)]

    chunks = [design]
    for _ in range(1, cols_axis):
        chunks.append(ring(chunks[-1], 1))

    block_rows = design.shape[0]
    near = factor_kernel(observations, gaps, noise_var, arc_lengths, arc_amp, arc_decay)
    weight = near[:block_rows]
    line = [near] + [ring(near, s) for s in range(1, cols_axis)]
    line_obs = jnp.stack([part[block_rows] for part in line])
    obs_all = jnp.stack([line_obs] + [swap(line_obs, m) for m in range(1, rows_axis)])

    packed = [spread(pack(design, None, tile_map, where, rows_axis, cols_axis))]
    for s in range(1, cols_axis):
        weight_s = line[s][:block_rows]
        packed.append(spread(pack(chunks[s], weight_s, tile_map, where, rows_axis, cols_axis)))

    weights = [weight] + [swap(weight, 2 * n) for n in range(1, pairs)]
    obs_first = obs_all[::2, : cols_axis - 1].swapaxes(0, 1).reshape(1, -1)
    keep, give, rhs_first = gram_first(
        packed[0],
        weights,
        [block for s in range(1, cols_axis - 1) for block in packed[s]],
        obs_first,
        rows_width,
        cols_width,
    )
    half = rows_width // 2
    other = swap(give, 1)
    other_rhs = swap(rhs_first[0, half:], 1)
    theirs = [swap(block, 1) for block in packed[-1]]
    obs_last = jnp.concatenate([obs_all[::2, -1], obs_all[1::2, -1]], axis=0).reshape(1, -1)
    gram, rhs_last = gram_last(
        keep, other, packed[-1], theirs, obs_last, rows_width, cols_width
    )
    normal_rhs = rhs_first[0, :half] + other_rhs + rhs_last[0]
    from_row, from_col = plan // cols_axis, plan % cols_axis
    ahead = (col - from_col + cols_axis) % cols_axis
    place = jnp.bitwise_xor(from_row, row) * cols_axis + ahead
    balanced_obs = jnp.take(obs_all.reshape(-1, block_rows), place, axis=0)
    return (gram, normal_rhs, balanced_obs)


def cut_columns(sizes, fetch, row, outs):
    per_row, per_col, own, half, base = sizes
    across_a, across_b, along_a, along_b, keep = outs
    rows_width = 2 * own

    def rows_of(n, core):
        there = jnp.bitwise_xor(row, 2 * n + core)
        return fetch(there * per_row, per_row)

    part = fetch(base, per_col)
    keep[:, rows_width:] = part
    across_a[:, own:] = part[:, :half]
    along_b[:, rows_width:] = part[:, :half]
    across_b[:, rows_width:] = part[:, half:]
    along_a[:, own:] = part[:, half:]
    across_a[:, :own] = rows_of(3, 0)
    along_a[:, :own] = rows_of(3, 1)
    for n, target in ((1, across_b), (2, along_b), (0, keep)):
        target[:, :own] = rows_of(n, 0)
        target[:, own:rows_width] = rows_of(n, 1)


def cut_widths(own, cols_width):
    half = cols_width // 2
    return [own + half, 2 * own + half, own + half, 2 * own + half, 2 * own + cols_width]


def head(design, small, tables, tile_map, where, rows_axis, cols_axis):
    block_rows, columns = design.shape
    tiles = tile_map.shape[0]
    size = columns // tiles
    per_row, per_col = tiles // rows_axis, tiles // cols_axis
    own, cols_width = per_row * size, per_col * size
    arcs = tables[0].shape[1]

    def kernel(where_ref, *refs):
        sources = refs[:8]
        near_ref = refs[8]
        outs = refs[9:14]
        before_ref = refs[14]
        x_ref, obs_ref, gap_ref, noise_ref, len_ref, amp_ref, decay_ref, map_ref, held, sems = refs[15:]
        targets = (x_ref, obs_ref, gap_ref, noise_ref, len_ref, amp_ref, decay_ref, map_ref)
        copies = [
            pltpu.make_async_copy(source, target, sems.at[k])
            for k, (source, target) in enumerate(zip(sources, targets))
        ]
        for copy in copies[1:] + copies[:1]:
            copy.start()
        for copy in copies[1:]:
            copy.wait()
        weight, white = factor_math(
            block_rows, arcs, len_ref, amp_ref, decay_ref, obs_ref, gap_ref, noise_ref
        )
        near_ref[:block_rows, :] = weight
        near_ref[block_rows:, :] = white
        copies[0].wait()
        row, col = where_ref[0], where_ref[1]

        def fetch(base, count):
            for j in range(count):
                at = pl.multiple_of(map_ref[0, base + j] * size, size)
                held[:, j * size : (j + 1) * size] = x_ref[:, pl.ds(at, size)]
            return split_dot(near_ref[:block_rows, :], held[:, : count * size])

        cut_columns((per_row, per_col, own, cols_width // 2, col * per_col), fetch, row, outs)
        before = jnp.where(col == 0, cols_axis - 1, col - 1)
        before_ref[...] = fetch(before * per_col, per_col)

    line = pltpu.VMEM((1, block_rows), F32)
    outs = [(block_rows + 8, block_rows, F32)]
    outs += [(block_rows, w, BF16) for w in cut_widths(own, cols_width) + [cols_width]]
    return pl.pallas_call(
        kernel,
        name="head",
        in_specs=[SMEM] + [ANY] * 8,
        out_specs=[VMEM] * 7,
        out_shape=[jax.ShapeDtypeStruct((h, w), t) for h, w, t in outs],
        scratch_shapes=[
            pltpu.VMEM((block_rows, columns), BF16),
            line,
            pltpu.VMEM((1, block_rows), jnp.int32),
            line,
            pltpu.SMEM((1, arcs), jnp.int32),
            pltpu.SMEM((1, arcs), F32),
            pltpu.SMEM((1, arcs), F32),
            pltpu.SMEM((1, tiles), jnp.int32),
            pltpu.VMEM((block_rows, max(2 * own, cols_width)), BF16),
            pltpu.SemaphoreType.DMA((8,)),
        ],
        cost_estimate=pl.CostEstimate(flops=10**9, bytes_accessed=5 * 10**6, transcendentals=0),
        compiler_params=pltpu.CompilerParams(vmem_limit_bytes=10 << 20),
    )(where, design, *[v.reshape(1, -1) for v in small], *tables, tile_map.reshape(1, -1))


def pack_cut(chunks, near, tile_map, where, rows_axis, cols_axis, begin):
    height, columns = chunks[-1].shape
    tiles = tile_map.shape[0]
    size = columns // tiles
    per_row, per_col = tiles // rows_axis, tiles // cols_axis
    own, cols_width = per_row * size, per_col * size
    depth = begin + height

    def kernel(map_ref, where_ref, near_ref, *refs):
        raw = refs[: len(chunks)]
        outs = refs[len(chunks) : -1]
        held = refs[-1]
        row, col = where_ref[0], where_ref[1]
        weight = near_ref[begin:depth, :depth]

        def fetch(base, count):
            for j in range(count):
                at = pl.multiple_of(map_ref[base + j] * size, size)
                top = 0
                for piece in raw:
                    end = top + piece.shape[0]
                    held[top:end, j * size : (j + 1) * size] = piece[:, pl.ds(at, size)]
                    top = end
            return split_dot(weight, held[:, : count * size])

        cut_columns((per_row, per_col, own, cols_width // 2, col * per_col), fetch, row, outs)

    return pl.pallas_call(
        kernel,
        name="pack_cut",
        in_specs=[SMEM, SMEM, VMEM] + [VMEM] * len(chunks),
        out_specs=[VMEM] * 5,
        out_shape=[jax.ShapeDtypeStruct((height, w), BF16) for w in cut_widths(own, cols_width)],
        scratch_shapes=[pltpu.VMEM((depth, max(own, cols_width)), BF16)],
        cost_estimate=pl.CostEstimate(flops=10**9, bytes_accessed=5 * 10**6, transcendentals=0),
        compiler_params=pltpu.CompilerParams(vmem_limit_bytes=8 << 20),
    )(tile_map, where, near, *chunks)


def row_parts(keep, xb, yb, fa, fb, own):
    block_rows = keep.shape[0]

    def kernel(keep_ref, xb_ref, yb_ref, fa_ref, fb_ref, lead_ref, rest_ref):
        for n, ref in enumerate((keep_ref, xb_ref, yb_ref)):
            lead_ref[n * block_rows : (n + 1) * block_rows, :] = ref[:, :own]
            rest_ref[n * block_rows : (n + 1) * block_rows, :] = ref[:, own : 2 * own]
        lead_ref[3 * block_rows :, :] = fa_ref[:, :own]
        rest_ref[3 * block_rows :, :] = fb_ref[:, :own]

    return pl.pallas_call(
        kernel,
        name="row_parts",
        in_specs=[VMEM] * 5,
        out_specs=[VMEM] * 2,
        out_shape=[jax.ShapeDtypeStruct((4 * block_rows, own), BF16)] * 2,
        cost_estimate=pl.CostEstimate(flops=10**9, bytes_accessed=5 * 10**6, transcendentals=0),
        compiler_params=pltpu.CompilerParams(vmem_limit_bytes=4 << 20),
    )(keep, xb, yb, fa, fb)


def obs_rows(obs, places, plan, where, cols_axis):
    block_rows = obs[0].shape[1]

    def kernel(plan_ref, where_ref, *refs):
        sources, (rows_ref, picked_ref) = refs[:-2], refs[-2:]
        at = 0
        for m, s, (begin, end) in places:
            line = jnp.broadcast_to(sources[m][s : s + 1, :], (8, block_rows))
            rows_ref[:, at : at + end - begin] = line[:, begin:end]
            at += end - begin
        from_row = lax.div(plan_ref[0], cols_axis)
        from_col = lax.rem(plan_ref[0], cols_axis)
        mask = jnp.bitwise_xor(from_row, where_ref[0])
        step = lax.rem(where_ref[1] - from_col + cols_axis, cols_axis)
        picked = jnp.zeros((1, block_rows), F32)
        for m, source in enumerate(sources):
            picked = jnp.where(mask == m, source[pl.ds(step, 1), :], picked)
        picked_ref[...] = picked

    return pl.pallas_call(
        kernel,
        name="obs_rows",
        in_specs=[SMEM, SMEM] + [VMEM] * len(obs),
        out_specs=[VMEM] * 2,
        out_shape=[
            jax.ShapeDtypeStruct((8, sum(end - begin for _, _, (begin, end) in places)), F32),
            jax.ShapeDtypeStruct((1, block_rows), F32),
        ],
        cost_estimate=pl.CostEstimate(flops=10**7, bytes_accessed=10**5, transcendentals=0),
        compiler_params=pltpu.CompilerParams(vmem_limit_bytes=4 << 20),
    )(plan, where, *obs)


def gram_direct(blocks, operands, rows, at_row, left_width, cols_width, before, halves, out_far):
    count = len(operands)
    width = left_width // halves
    step = cols_width // 6 if cols_width % 6 == 0 and (cols_width // 6) % 128 == 0 else 128
    steps = cols_width // step
    depth = sum(block[0] for block in blocks)

    def kernel(*refs):
        sources = refs[:count]
        rows_ref = refs[count]
        sums = refs[count + 1 : count + 1 + len(before)]
        outs = refs[count + 1 + len(before) : count + 1 + len(before) + 2 * halves]
        scratch = refs[count + 1 + len(before) + 2 * halves :]
        turned = scratch[0]
        total = jnp.zeros((8, left_width), F32)
        top = 0
        for height, lefts, _ in blocks:
            seen = rows_ref[:, at_row + top : at_row + top + height].astype(BF16)
            for which, first, begin, length, to in lefts:
                left = sources[which][first : first + height, begin : begin + length]
                turned[to : to + length, top : top + height] = left.T
            left = jnp.concatenate(
                [
                    sources[which][first : first + height, begin : begin + length]
                    for which, first, begin, length, _ in sorted(lefts, key=lambda p: p[4])
                ],
                axis=1,
            )
            total = total + jnp.dot(seen, left, preferred_element_type=F32)
            top += height
        half_sums = len(before) // 2
        for h in range(halves):
            part = total[:, h * width : (h + 1) * width]
            for extra in sums[half_sums:]:
                part = part + extra[...]
            outs[halves + h][...] = part
        copies = [None, None]
        for t in range(steps):
            begin = t * step
            pieces = []
            for height, _, cols in blocks:
                for which, first, start, length, to in cols:
                    if to <= begin < to + length:
                        at = start + begin - to
                        pieces.append(sources[which][first : first + height, at : at + step])
            right = jnp.concatenate(pieces, axis=0)
            for h in range(halves):
                part = jnp.dot(
                    turned[h * width : (h + 1) * width, :], right, preferred_element_type=F32
                )
                for extra in sums[:half_sums]:
                    part = part + extra[:, begin : begin + step]
                if not out_far:
                    outs[h][:, begin : begin + step] = part
                    continue
                tile, sems = scratch[1:]
                slot = t % 2
                if copies[slot] is not None:
                    copies[slot].wait()
                tile[slot] = part
                copies[slot] = pltpu.make_async_copy(
                    tile.at[slot], outs[0].at[:, pl.ds(begin, step)], sems.at[slot]
                )
                copies[slot].start()
        for copy in copies:
            if copy is not None:
                copy.wait()

    scratch_shapes = [pltpu.VMEM((left_width, depth), BF16)]
    scratch_bytes = 2 * left_width * depth
    if out_far:
        scratch_shapes += [pltpu.VMEM((2, width, step), F32), pltpu.SemaphoreType.DMA((2,))]
        scratch_bytes += 8 * width * step
    return pl.pallas_call(
        kernel,
        in_specs=[VMEM] * (count + 1 + len(before)),
        out_specs=[ANY if out_far else VMEM] * halves + [VMEM] * halves,
        out_shape=[jax.ShapeDtypeStruct((width, cols_width), F32)] * halves
        + [jax.ShapeDtypeStruct((8, width), F32)] * halves,
        scratch_shapes=scratch_shapes,
        cost_estimate=pl.CostEstimate(
            flops=2 * depth * left_width * cols_width, bytes_accessed=2 * 10**7, transcendentals=0
        ),
        compiler_params=pltpu.CompilerParams(vmem_limit_bytes=scratch_bytes + (4 << 20)),
    )(*operands, rows, *before)


def on_device_square(
    rows_axis,
    cols_axis,
    design,
    observations,
    gaps,
    noise_var,
    arc_lengths,
    arc_amp,
    arc_decay,
    plan,
    tile_map,
):
    block_rows, columns = design.shape
    tiles = tile_map.shape[0]
    size = columns // tiles
    own = (tiles // rows_axis) * size
    wide = 2 * own
    cols_width = (tiles // cols_axis) * size
    half = cols_width // 2
    row, col = lax.axis_index("row"), lax.axis_index("col")
    where = jnp.stack([row, col]).astype(jnp.int32)
    last = cols_axis - 1

    def ring(x, shift):
        return lax.ppermute(x, "col", [(c, (c + shift) % cols_axis) for c in range(cols_axis)])

    def swap(x, mask):
        return lax.ppermute(x, "row", [(r, r ^ mask) for r in range(rows_axis)])

    middle = block_rows // 2
    chunks = [design]
    for _ in range(1, last - 1):
        chunks.append(ring(chunks[-1], 1))
    halves = [ring(chunks[-1][:middle], 1), ring(chunks[-1][middle:], 1)]
    near, *parts = head(
        design,
        (observations, gaps, noise_var),
        (arc_lengths, arc_amp, arc_decay),
        tile_map,
        where,
        rows_axis,
        cols_axis,
    )
    line = [near] + [ring(near, s) for s in range(1, cols_axis)]
    line_obs = jnp.stack([part[block_rows] for part in line])
    obs = [line_obs] + [swap(line_obs, m) for m in range(1, rows_axis)]

    def trade(xa, xb, ya, yb, keep):
        xa, ya = swap(xa, 2), swap(ya, 4)
        xb, yb = swap(xb, 2), swap(yb, 4)
        return keep, xa, xb, ya, yb, swap(xa, 4), swap(ya, 2)

    traded = [trade(*parts[:5])]
    for s in range(1, last - 1):
        cut = pack_cut([chunks[s]], line[s], tile_map, where, rows_axis, cols_axis, 0)
        traded.append(trade(*cut))
    for k, begin in enumerate((0, middle)):
        cut = pack_cut(
            halves[: k + 1], line[last - 1], tile_map, where, rows_axis, cols_axis, begin
        )
        traded.append(trade(*cut))

    keep, _, xb, _, yb, fa, fb = traded[0]
    lead, rest = row_parts(keep, xb, yb, fa, fb, own)
    far_cols = ring(parts[5], last)
    far_rest = ring(rest, last)
    far_lead = ring(lead, last)
    x3, y3 = swap(far_cols, 2), swap(far_cols, 4)
    fa3 = swap(x3[:, :half], 4)
    fb3 = swap(y3[:, half:], 2)

    def part_blocks(first, height, left, both):
        wide_left = wide if both else own
        begin = 0 if both else left * own
        blocks = []
        for k in (0, 2, 4):
            blocks.append([height, [(first + k, 0, begin, wide_left, 0)], []])
        corner = [(first + 5 + left, 0, 0, own, 0)]
        if both:
            corner.append((first + 6, 0, 0, own, own))
        blocks.append([height, corner, []])
        for n, k, begin, length, to in (
            (0, 0, wide, cols_width, 0),
            (1, 1, own, half, 0),
            (1, 2, wide, half, half),
            (2, 4, wide, half, 0),
            (2, 3, own, half, half),
            (3, 5, own, half, 0),
            (3, 6, own, half, half),
        ):
            blocks[n][2].append((first + k, 0, begin, length, to))
        return blocks

    def seen(count, core, s, rows):
        return [(2 * n + core, s, rows) for n in range(count)]

    whole = (0, block_rows)
    parts_of = ((0, middle), (middle, block_rows))
    early, mid, late = [], [], []
    for s in range(last - 1):
        early += seen(4, 0, s, whole)
    for rows in parts_of:
        for core in (0, 1):
            mid += seen(4, core, last - 1, rows)
    for core in (0, 1):
        late += seen(4, core, last, whole)
    rows, balanced_obs = obs_rows(obs, early + mid + late, plan, where, cols_axis)

    blocks, operands = [], []
    for s in range(last - 1):
        blocks += part_blocks(len(operands), block_rows, 0, True)
        operands += list(traded[s])
    keep, give, keep_rhs, give_rhs = gram_direct(
        blocks, operands, rows, 0, wide, cols_width, (), 2, False
    )
    other = swap(give, 1)
    other_rhs = swap(give_rhs, 1)

    at_row = 4 * (last - 1) * block_rows
    blocks, operands = [], []
    for k in (last - 1, last):
        mine = list(traded[k])
        theirs = [swap(v, 1) for v in mine]
        blocks += part_blocks(len(operands), middle, 0, False)
        blocks += part_blocks(len(operands) + 7, middle, 1, False)
        operands += mine + theirs
    most, most_rhs = gram_direct(
        blocks,
        operands,
        rows,
        at_row,
        own,
        cols_width,
        (keep, other, keep_rhs, other_rhs),
        1,
        False,
    )
    at_row += 8 * block_rows
    mine = [far_cols, x3, y3, fa3, fb3]
    theirs = [swap(v, 1) for v in mine]
    their_rest = swap(far_rest, 1)
    blocks, operands = [], []
    for left, group in ((far_lead, mine), (their_rest, theirs)):
        first = len(operands)
        operands += [left] + group
        for n in range(4):
            cols = [(first + 1 + n, 0, 0, cols_width, 0)]
            if n == 3:
                cols = [(first + 4, 0, 0, half, 0), (first + 5, 0, 0, half, half)]
            blocks.append((block_rows, [(first, n * block_rows, 0, own, 0)], cols))
    gram, rhs = gram_direct(
        blocks, operands, rows, at_row, own, cols_width, (most, most_rhs), 1, True
    )
    return (gram, rhs[0], balanced_obs)


def solution(mesh):
    placed = (
        P(("row", "col"), None),
        P(("row", "col")),
        P(("row", "col")),
        P(("row", "col")),
        P(("row", "col"), None),
        P(("row", "col"), None),
        P(("row", "col"), None),
        P(("row", "col")),
        P(),
    )
    rows_axis, cols_axis = mesh.shape["row"], mesh.shape["col"]
    square = rows_axis == 2**3 and cols_axis > 2

    def body(*args):
        if not square:
            return on_device_any(rows_axis, cols_axis, *args)
        return on_device_square(rows_axis, cols_axis, *args)

    return jax.shard_map(
        body,
        mesh=mesh,
        in_specs=placed,
        out_specs=(P("row", "col"), P("row"), P(("row", "col"), None)),
        check_vma=False,
    )
```

profile of v0, /device:TPU:0, one launch (start us, length us, event | category | flops | bytes accessed | tf_op | source)
XLA Modules:
  0.0 242.9 jit_solution(3925655173262954391)
XLA Ops:
  0.6 3.1 %collective-permute-start.29 = (bf16[128,6144]{1,0:T(8,128)(2,1)}, bf16[128,6144]{1,0:T(8,128)(2,1)S(1)}, u32[]{:S(2)}, u32[]{:S(2)}) collective-permute-start(bf16[128,6144]{1,0:T(8,128)(2,1)} %refs_0_.1), channel_id=1, source_target_pairs={{0,1},{1,2},{2,3},{3,0},{4,5},{5,6},{6,7},{7,4},{8,9},{9,10},{10,1... | collective-permute-start | bytes 4718600 | tf_op jit(solution)/shard_map/ppermute | solution.py:658
  3.8 1.4 copy-done
  9.8 3.7 %head.1 = (f32[136,128]{1,0:T(8,128)S(1)}, bf16[128,1536]{1,0:T(8,128)(2,1)S(1)}, bf16[128,2304]{1,0:T(8,128)(2,1)S(1)}, bf16[128,1536]{1,0:T(8,128)(2,1)S(1)}, ...) custom-call(s32[2]{0:T(128)S(1)} %pad_add_fusion.where_ref, ...), custom_call_target="tpu_custom_call" | custom-call | flops 1000000000 | bytes 5000000 | tf_op jit(solution)/shard_map/head/pallas_call | solution.py:430
  13.6 2.7 %collective-permute-start.20 = (f32[136,128]{1,0:T(8,128)S(1)}, f32[136,128]{1,0:T(8,128)S(1)}, u32[]{:S(2)}, u32[]{:S(2)}) collective-permute-start(f32[136,128]{1,0:T(8,128)S(1)} %get-tuple-element.45), channel_id=1, source_target_pairs={{0,2},{1,3},{2,0},{3,1},{4,6},{5,7},{6,4},{7,5},{8,10},{9,11},{10,... | collective-permute-start | bytes 208904 | tf_op jit(solution)/shard_map/ppermute | solution.py:658
  16.3 3.8 %collective-permute-start.21 = (f32[136,128]{1,0:T(8,128)S(1)}, f32[136,128]{1,0:T(8,128)S(1)}, u32[]{:S(2)}, u32[]{:S(2)}) collective-permute-start(f32[136,128]{1,0:T(8,128)S(1)} %get-tuple-element.45), channel_id=1, source_target_pairs={{0,3},{1,0},{2,1},{3,2},{4,7},{5,4},{6,5},{7,6},{8,11},{9,8},{10,9... | collective-permute-start | bytes 208904 | tf_op jit(solution)/shard_map/ppermute | solution.py:658
  20.0 24.9 %collective-permute-done.20.near_ref = f32[136,128]{1,0:T(8,128)S(1)} collective-permute-done((f32[136,128]{1,0:T(8,128)S(1)}, f32[136,128]{1,0:T(8,128)S(1)}, u32[]{:S(2)}, u32[]{:S(2)}) %collective-permute-start.20) | collective-permute-done | bytes 69664 | tf_op jit(solution)/shard_map/ppermute | solution.py:658
  45.1 1.6 collective-permute-start.23
  46.9 1.5 collective-permute-start.25
  48.8 2.4 %collective-permute-start.27 = (f32[4,128]{1,0:T(4,128)S(1)}, f32[4,128]{1,0:T(4,128)S(1)}, u32[]{:S(2)}, u32[]{:S(2)}) collective-permute-start(f32[4,128]{1,0:T(4,128)S(1)} %pad_maximum_fusion.refs_0_), channel_id=1, source_target_pairs={{0,24},{4,28},{8,16},{12,20},{16,8},{20,12},{24,0},{28,4},{1,25},{... | collective-permute-start | bytes 6152 | tf_op jit(solution)/shard_map/ppermute | solution.py:661
  51.7 1.5 collective-permute-start
  53.7 1.5 collective-permute-start.4
  55.9 1.9 pack_cut.5
  57.8 5.3 %collective-permute-done.2.refs_1_ = bf16[128,1536]{1,0:T(8,128)(2,1)S(1)} collective-permute-done((bf16[128,1536]{1,0:T(8,128)(2,1)S(1)}, bf16[128,1536]{1,0:T(8,128)(2,1)S(1)}, u32[]{:S(2)}, u32[]{:S(2)}) %collective-permute-start.2) | collective-permute-done | bytes 393248 | tf_op jit(solution)/shard_map/ppermute | solution.py:661
  63.7 10.3 %collective-permute-done.28.refs_7_ = f32[4,128]{1,0:T(4,128)S(1)} collective-permute-done((f32[4,128]{1,0:T(4,128)S(1)}, f32[4,128]{1,0:T(4,128)S(1)}, u32[]{:S(2)}, u32[]{:S(2)}) %collective-permute-start.28) | collective-permute-done | bytes 2080 | tf_op jit(solution)/shard_map/ppermute | solution.py:661
  74.6 3.3 %collective-permute-done.4.refs_3_ = bf16[128,1536]{1,0:T(8,128)(2,1)S(1)} collective-permute-done((bf16[128,1536]{1,0:T(8,128)(2,1)S(1)}, bf16[128,1536]{1,0:T(8,128)(2,1)S(1)}, u32[]{:S(2)}, u32[]{:S(2)}) %collective-permute-start.4) | collective-permute-done | bytes 393248 | tf_op jit(solution)/shard_map/ppermute | solution.py:661
  79.0 1.5 collective-permute-start.61
  80.5 5.9 %collective-permute-done.3.fa_ref.refs_5_ = bf16[128,1536]{1,0:T(8,128)(2,1)S(1)} collective-permute-done((bf16[128,1536]{1,0:T(8,128)(2,1)S(1)}, bf16[128,1536]{1,0:T(8,128)(2,1)S(1)}, u32[]{:S(2)}, u32[]{:S(2)}) %collective-permute-start.3) | collective-permute-done | bytes 393248 | tf_op jit(solution)/shard_map/ppermute | solution.py:661
  87.5 7.2 %collective-permute-done.60.refs_10_ = bf16[128,1536]{1,0:T(8,128)(2,1)S(1)} collective-permute-done((bf16[128,1536]{1,0:T(8,128)(2,1)S(1)}, bf16[128,1536]{1,0:T(8,128)(2,1)S(1)}, u32[]{:S(2)}, u32[]{:S(2)}) %collective-permute-start.60) | collective-permute-done | bytes 393248 | tf_op jit(solution)/shard_map/ppermute | solution.py:661
  95.9 1.1 obs_rows.1
  97.0 10.0 %collective-permute-done.5.fb_ref.refs_6_ = bf16[128,1536]{1,0:T(8,128)(2,1)S(1)} collective-permute-done((bf16[128,1536]{1,0:T(8,128)(2,1)S(1)}, bf16[128,1536]{1,0:T(8,128)(2,1)S(1)}, u32[]{:S(2)}, u32[]{:S(2)}) %collective-permute-start.5) | collective-permute-done | bytes 393248 | tf_op jit(solution)/shard_map/ppermute | solution.py:661
  107.1 2.2 collective-permute-start.7
  109.3 5.1 %collective-permute-done.62.refs_12_ = bf16[128,1536]{1,0:T(8,128)(2,1)S(1)} collective-permute-done((bf16[128,1536]{1,0:T(8,128)(2,1)S(1)}, bf16[128,1536]{1,0:T(8,128)(2,1)S(1)}, u32[]{:S(2)}, u32[]{:S(2)}) %collective-permute-start.62) | collective-permute-done | bytes 393248 | tf_op jit(solution)/shard_map/ppermute | solution.py:661
  115.3 5.6 %shard_map.112 = (f32[768,1536]{1,0:T(8,128)S(1)}, f32[768,1536]{1,0:T(8,128)S(1)}, f32[8,768]{1,0:T(8,128)S(1)}, f32[8,768]{1,0:T(8,128)S(1)}) custom-call(bf16[128,3072]{1,0:T(8,128)(2,1)S(1)} %get-tuple-element.37.keep_ref.refs_0_, bf16[128,1536]{1,0:T(8,128)(2,1)S(1)} %collective-permute-done.2.refs_1_, ...), custom_call_target="tpu_custom_call" | custom-call | flops 4831838208 | bytes 20000000 | tf_op jit(solution)/shard_map/pallas_call | solution.py:619
  121.7 1.5 collective-permute-start.9
  123.3 2.0 collective-permute-start.30
  126.1 6.5 %collective-permute-done.8.refs_2_ = bf16[128,1536]{1,0:T(8,128)(2,1)S(1)} collective-permute-done((bf16[128,1536]{1,0:T(8,128)(2,1)S(1)}, bf16[128,1536]{1,0:T(8,128)(2,1)S(1)}, u32[]{:S(2)}, u32[]{:S(2)}) %collective-permute-start.8) | collective-permute-done | bytes 393248 | tf_op jit(solution)/shard_map/ppermute | solution.py:661
  132.6 2.2 collective-permute-start.12
  134.8 1.6 collective-permute-start.10
  136.4 4.6 %collective-permute-done.10.refs_4_ = bf16[128,768]{1,0:T(8,128)(2,1)S(1)} collective-permute-done((bf16[128,768]{1,0:T(8,128)(2,1)S(1)}, bf16[128,768]{1,0:T(8,128)(2,1)S(1)}, u32[]{:S(2)}, u32[]{:S(2)}) %collective-permute-start.10) | collective-permute-done | bytes 196640 | tf_op jit(solution)/shard_map/ppermute | solution.py:661
  141.0 4.7 %collective-permute-done.30.refs_0_ = bf16[64,6144]{1,0:T(8,128)(2,1)S(1)} collective-permute-done((bf16[64,6144]{1,0:T(8,128)(2,1)S(1)}, bf16[64,6144]{1,0:T(8,128)(2,1)S(1)}, u32[]{:S(2)}, u32[]{:S(2)}) %collective-permute-start.30) | collective-permute-done | bytes 786464 | tf_op jit(solution)/shard_map/ppermute | solution.py:658
  145.7 1.5 collective-permute-start.11
  147.2 15.3 %collective-permute-done.44.refs_1_ = bf16[64,6144]{1,0:T(8,128)(2,1)S(1)} collective-permute-done((bf16[64,6144]{1,0:T(8,128)(2,1)S(1)}, bf16[64,6144]{1,0:T(8,128)(2,1)S(1)}, u32[]{:S(2)}, u32[]{:S(2)}) %collective-permute-start.44) | collective-permute-done | bytes 786464 | tf_op jit(solution)/shard_map/ppermute | solution.py:658
  162.5 1.6 pack_cut.4
  164.1 1.5 collective-permute-start.45
  166.2 1.3 pack_cut.3
  167.5 10.7 %collective-permute-done.12 = bf16[512,768]{1,0:T(8,128)(2,1)S(1)} collective-permute-done((bf16[512,768]{1,0:T(8,128)(2,1)S(1)}, bf16[512,768]{1,0:T(8,128)(2,1)S(1)}, u32[]{:S(2)}, u32[]{:S(2)}) %collective-permute-start.12) | collective-permute-done | bytes 786464 | tf_op jit(solution)/shard_map/ppermute | solution.py:658
  178.2 1.5 collective-permute-start.46
  180.7 1.5 collective-permute-start.33
  182.3 9.1 %collective-permute-done.31.refs_1_ = bf16[64,1536]{1,0:T(8,128)(2,1)S(1)} collective-permute-done((bf16[64,1536]{1,0:T(8,128)(2,1)S(1)}, bf16[64,1536]{1,0:T(8,128)(2,1)S(1)}, u32[]{:S(2)}, u32[]{:S(2)}) %collective-permute-start.31) | collective-permute-done | bytes 196640 | tf_op jit(solution)/shard_map/ppermute | solution.py:661
  191.3 1.2 collective-permute-done.33.refs_3_
  193.8 8.1 %collective-permute-done.32.refs_2_ = bf16[64,2304]{1,0:T(8,128)(2,1)S(1)} collective-permute-done((bf16[64,2304]{1,0:T(8,128)(2,1)S(1)}, bf16[64,2304]{1,0:T(8,128)(2,1)S(1)}, u32[]{:S(2)}, u32[]{:S(2)}) %collective-permute-start.32) | collective-permute-done | bytes 294944 | tf_op jit(solution)/shard_map/ppermute | solution.py:661
  202.5 1.2 collective-permute-start.50
  204.2 4.2 %collective-permute-done.49.refs_19_ = bf16[64,1536]{1,0:T(8,128)(2,1)S(1)} collective-permute-done((bf16[64,1536]{1,0:T(8,128)(2,1)S(1)}, bf16[64,1536]{1,0:T(8,128)(2,1)S(1)}, u32[]{:S(2)}, u32[]{:S(2)}) %collective-permute-start.49) | collective-permute-done | bytes 196640 | tf_op jit(solution)/shard_map/ppermute | solution.py:661
  210.4 3.7 %collective-permute-done.35.refs_5_ = bf16[64,1536]{1,0:T(8,128)(2,1)S(1)} collective-permute-done((bf16[64,1536]{1,0:T(8,128)(2,1)S(1)}, bf16[64,1536]{1,0:T(8,128)(2,1)S(1)}, u32[]{:S(2)}, u32[]{:S(2)}) %collective-permute-start.35) | collective-permute-done | bytes 196640 | tf_op jit(solution)/shard_map/ppermute | solution.py:661
  218.1 2.0 collective-permute-done.42.refs_12_
  220.9 3.9 %shard_map.113 = (f32[768,1536]{1,0:T(8,128)S(1)}, f32[8,768]{1,0:T(8,128)S(1)}) custom-call(bf16[64,3072]{1,0:T(8,128)(2,1)S(1)} %get-tuple-element.47.refs_0_, bf16[64,1536]{1,0:T(8,128)(2,1)S(1)} %collective-permute-done.31.refs_1_, bf16[64,2304]{1,0:T(8,128)(2,1)S(1)} %collective-permute-done.32.refs_2_, ...), custom_call_target="tpu_custom_call" | custom-call | flops 2415919104 | bytes 20000000 | tf_op jit(solution)/shard_map/pallas_call | solution.py:619
  224.8 11.4 %collective-permute-done.6.refs_0_ = bf16[512,768]{1,0:T(8,128)(2,1)S(1)} collective-permute-done((bf16[512,768]{1,0:T(8,128)(2,1)S(1)}, bf16[512,768]{1,0:T(8,128)(2,1)S(1)}, u32[]{:S(2)}, u32[]{:S(2)}) %collective-permute-start.6) | collective-permute-done | bytes 786464 | tf_op jit(solution)/shard_map/ppermute | solution.py:658
  236.2 6.1 %shard_map.114 = (f32[768,1536]{1,0:T(8,128)}, f32[8,768]{1,0:T(8,128)S(1)}) custom-call(bf16[512,768]{1,0:T(8,128)(2,1)S(1)} %collective-permute-done.6.refs_0_, bf16[128,1536]{1,0:T(8,128)(2,1)S(1)} %collective-permute-done.7.refs_1_, bf16[128,1536]{1,0:T(8,128)(2,1)S(1)} %collective-permute-done.8.refs_2_, ...), custom_call_target="tpu_custom_call" | custom-call | flops 2415919104 | bytes 20000000 | tf_op jit(solution)/shard_map/pallas_call | solution.py:619
  (123 shorter events, 24.9 us)
Async XLA Ops:
  0.6 54.6 %collective-permute-start.29 = (bf16[128,6144]{1,0:T(8,128)(2,1)}, bf16[128,6144]{1,0:T(8,128)(2,1)S(1)}, u32[]{:S(2)}, u32[]{:S(2)}) collective-permute-start(bf16[128,6144]{1,0:T(8,128)(2,1)} %refs_0_.1), channel_id=1, source_target_pairs={{0,1},{1,2},{2,3},{3,0},{4,5},{5,6},{6,7},{7,4},{8,9},{9,10},{10,1... | collective-permute-start | bytes 4718600 | tf_op jit(solution)/shard_map/ppermute | solution.py:658
  13.6 31.4 %collective-permute-start.20 = (f32[136,128]{1,0:T(8,128)S(1)}, f32[136,128]{1,0:T(8,128)S(1)}, u32[]{:S(2)}, u32[]{:S(2)}) collective-permute-start(f32[136,128]{1,0:T(8,128)S(1)} %get-tuple-element.45), channel_id=1, source_target_pairs={{0,2},{1,3},{2,0},{3,1},{4,6},{5,7},{6,4},{7,5},{8,10},{9,11},{10,... | collective-permute-start | bytes 208904 | tf_op jit(solution)/shard_map/ppermute | solution.py:658
  16.2 28.8 %collective-permute-start.19 = (f32[136,128]{1,0:T(8,128)S(1)}, f32[136,128]{1,0:T(8,128)S(1)}, u32[]{:S(2)}, u32[]{:S(2)}) collective-permute-start(f32[136,128]{1,0:T(8,128)S(1)} %get-tuple-element.45), channel_id=1, source_target_pairs={{0,1},{1,2},{2,3},{3,0},{4,5},{5,6},{6,7},{7,4},{8,9},{9,10},{10,1... | collective-permute-start | bytes 208904 | tf_op jit(solution)/shard_map/ppermute | solution.py:658
  16.3 28.7 %collective-permute-start.21 = (f32[136,128]{1,0:T(8,128)S(1)}, f32[136,128]{1,0:T(8,128)S(1)}, u32[]{:S(2)}, u32[]{:S(2)}) collective-permute-start(f32[136,128]{1,0:T(8,128)S(1)} %get-tuple-element.45), channel_id=1, source_target_pairs={{0,3},{1,0},{2,1},{3,2},{4,7},{5,4},{6,5},{7,6},{8,11},{9,8},{10,9... | collective-permute-start | bytes 208904 | tf_op jit(solution)/shard_map/ppermute | solution.py:658
  48.8 5.0 %collective-permute-start.27 = (f32[4,128]{1,0:T(4,128)S(1)}, f32[4,128]{1,0:T(4,128)S(1)}, u32[]{:S(2)}, u32[]{:S(2)}) collective-permute-start(f32[4,128]{1,0:T(4,128)S(1)} %pad_maximum_fusion.refs_0_), channel_id=1, source_target_pairs={{0,24},{4,28},{8,16},{12,20},{16,8},{20,12},{24,0},{28,4},{1,25},{... | collective-permute-start | bytes 6152 | tf_op jit(solution)/shard_map/ppermute | solution.py:661
  51.2 12.0 %collective-permute-start.2 = (bf16[128,1536]{1,0:T(8,128)(2,1)S(1)}, bf16[128,1536]{1,0:T(8,128)(2,1)S(1)}, u32[]{:S(2)}, u32[]{:S(2)}) collective-permute-start(bf16[128,1536]{1,0:T(8,128)(2,1)S(1)} %get-tuple-element.40), channel_id=1, source_target_pairs={{0,8},{4,12},{8,0},{12,4},{16,24},{20,28},{24,16},{28,20},{1,9},{5... | collective-permute-start | bytes 1179656 | tf_op jit(solution)/shard_map/ppermute | solution.py:661
  51.7 26.7 %collective-permute-start = (bf16[128,2304]{1,0:T(8,128)(2,1)S(1)}, bf16[128,2304]{1,0:T(8,128)(2,1)S(1)}, u32[]{:S(2)}, u32[]{:S(2)}) collective-permute-start(bf16[128,2304]{1,0:T(8,128)(2,1)S(1)} %get-tuple-element.38), channel_id=1, source_target_pairs={{0,8},{4,12},{8,0},{12,4},{16,24},{20,28},{24,16},{28,20},{1,9},{5... | collective-permute-start | bytes 1769480 | tf_op jit(solution)/shard_map/ppermute | solution.py:661
  53.2 25.7 %collective-permute-start.1 = (bf16[128,2304]{1,0:T(8,128)(2,1)S(1)}, bf16[128,2304]{1,0:T(8,128)(2,1)S(1)}, u32[]{:S(2)}, u32[]{:S(2)}) collective-permute-start(bf16[128,2304]{1,0:T(8,128)(2,1)S(1)} %get-tuple-element.39), channel_id=1, source_target_pairs={{0,16},{4,20},{8,24},{12,28},{16,0},{20,4},{24,8},{28,12},{1,17},{... | collective-permute-start | bytes 1769480 | tf_op jit(solution)/shard_map/ppermute | solution.py:661
  53.7 24.2 %collective-permute-start.4 = (bf16[128,1536]{1,0:T(8,128)(2,1)S(1)}, bf16[128,1536]{1,0:T(8,128)(2,1)S(1)}, u32[]{:S(2)}, u32[]{:S(2)}) collective-permute-start(bf16[128,1536]{1,0:T(8,128)(2,1)S(1)} %get-tuple-element.41), channel_id=1, source_target_pairs={{0,16},{4,20},{8,24},{12,28},{16,0},{20,4},{24,8},{28,12},{1,17},{... | collective-permute-start | bytes 1179656 | tf_op jit(solution)/shard_map/ppermute | solution.py:661
  55.3 18.7 %collective-permute-start.28 = (f32[4,128]{1,0:T(4,128)S(1)}, f32[4,128]{1,0:T(4,128)S(1)}, u32[]{:S(2)}, u32[]{:S(2)}) collective-permute-start(f32[4,128]{1,0:T(4,128)S(1)} %pad_maximum_fusion.refs_0_), channel_id=1, source_target_pairs={{0,28},{4,24},{8,20},{12,16},{16,12},{20,8},{24,4},{28,0},{1,29},{... | collective-permute-start | bytes 6152 | tf_op jit(solution)/shard_map/ppermute | solution.py:661
  63.2 23.1 %collective-permute-start.3 = (bf16[128,1536]{1,0:T(8,128)(2,1)S(1)}, bf16[128,1536]{1,0:T(8,128)(2,1)S(1)}, u32[]{:S(2)}, u32[]{:S(2)}) collective-permute-start(bf16[128,1536]{1,0:T(8,128)(2,1)S(1)} %collective-permute-done.2.refs_1_), channel_id=1, source_target_pairs={{0,16},{4,20},{8,24},{12,28},{16,0},{20,4},{24,8},{28,12},{1,17},{... | collective-permute-start | bytes 1179656 | tf_op jit(solution)/shard_map/ppermute | solution.py:661
  74.0 12.9 %collective-permute-start.58 = (bf16[128,1536]{1,0:T(8,128)(2,1)S(1)}, bf16[128,1536]{1,0:T(8,128)(2,1)S(1)}, u32[]{:S(2)}, u32[]{:S(2)}) collective-permute-start(bf16[128,1536]{1,0:T(8,128)(2,1)S(1)} %get-tuple-element.58), channel_id=1, source_target_pairs={{0,8},{4,12},{8,0},{12,4},{16,24},{20,28},{24,16},{28,20},{1,9},{5... | collective-permute-start | bytes 1179656 | tf_op jit(solution)/shard_map/ppermute | solution.py:661
  77.9 16.9 %collective-permute-start.60 = (bf16[128,1536]{1,0:T(8,128)(2,1)S(1)}, bf16[128,1536]{1,0:T(8,128)(2,1)S(1)}, u32[]{:S(2)}, u32[]{:S(2)}) collective-permute-start(bf16[128,1536]{1,0:T(8,128)(2,1)S(1)} %get-tuple-element.60), channel_id=1, source_target_pairs={{0,16},{4,20},{8,24},{12,28},{16,0},{20,4},{24,8},{28,12},{1,17},{... | collective-permute-start | bytes 1179656 | tf_op jit(solution)/shard_map/ppermute | solution.py:661
  78.4 30.9 %collective-permute-start.59 = (bf16[128,2304]{1,0:T(8,128)(2,1)S(1)}, bf16[128,2304]{1,0:T(8,128)(2,1)S(1)}, u32[]{:S(2)}, u32[]{:S(2)}) collective-permute-start(bf16[128,2304]{1,0:T(8,128)(2,1)S(1)} %get-tuple-element.59), channel_id=1, source_target_pairs={{0,8},{4,12},{8,0},{12,4},{16,24},{20,28},{24,16},{28,20},{1,9},{5... | collective-permute-start | bytes 1769480 | tf_op jit(solution)/shard_map/ppermute | solution.py:661
  79.0 30.3 %collective-permute-start.61 = (bf16[128,2304]{1,0:T(8,128)(2,1)S(1)}, bf16[128,2304]{1,0:T(8,128)(2,1)S(1)}, u32[]{:S(2)}, u32[]{:S(2)}) collective-permute-start(bf16[128,2304]{1,0:T(8,128)(2,1)S(1)} %get-tuple-element.61), channel_id=1, source_target_pairs={{0,16},{4,20},{8,24},{12,28},{16,0},{20,4},{24,8},{28,12},{1,17},{... | collective-permute-start | bytes 1769480 | tf_op jit(solution)/shard_map/ppermute | solution.py:661
  86.3 20.7 %collective-permute-start.5 = (bf16[128,1536]{1,0:T(8,128)(2,1)S(1)}, bf16[128,1536]{1,0:T(8,128)(2,1)S(1)}, u32[]{:S(2)}, u32[]{:S(2)}) collective-permute-start(bf16[128,1536]{1,0:T(8,128)(2,1)S(1)} %collective-permute-done.4.refs_3_), channel_id=1, source_target_pairs={{0,8},{4,12},{8,0},{12,4},{16,24},{20,28},{24,16},{28,20},{1,9},{5... | collective-permute-start | bytes 1179656 | tf_op jit(solution)/shard_map/ppermute | solution.py:661
  86.9 27.5 %collective-permute-start.62 = (bf16[128,1536]{1,0:T(8,128)(2,1)S(1)}, bf16[128,1536]{1,0:T(8,128)(2,1)S(1)}, u32[]{:S(2)}, u32[]{:S(2)}) collective-permute-start(bf16[128,1536]{1,0:T(8,128)(2,1)S(1)} %collective-permute-done.58.refs_8_), channel_id=1, source_target_pairs={{0,16},{4,20},{8,24},{12,28},{16,0},{20,4},{24,8},{28,12},{1,17},{... | collective-permute-start | bytes 1179656 | tf_op jit(solution)/shard_map/ppermute | solution.py:661
  94.8 20.6 %collective-permute-start.63 = (bf16[128,1536]{1,0:T(8,128)(2,1)S(1)}, bf16[128,1536]{1,0:T(8,128)(2,1)S(1)}, u32[]{:S(2)}, u32[]{:S(2)}) collective-permute-start(bf16[128,1536]{1,0:T(8,128)(2,1)S(1)} %collective-permute-done.60.refs_10_), channel_id=1, source_target_pairs={{0,8},{4,12},{8,0},{12,4},{16,24},{20,28},{24,16},{28,20},{1,9},{5... | collective-permute-start | bytes 1179656 | tf_op jit(solution)/shard_map/ppermute | solution.py:661
  107.1 14.0 %collective-permute-start.7 = (bf16[128,1536]{1,0:T(8,128)(2,1)S(1)}, bf16[128,1536]{1,0:T(8,128)(2,1)S(1)}, u32[]{:S(2)}, u32[]{:S(2)}) collective-permute-start(bf16[128,1536]{1,0:T(8,128)(2,1)S(1)} %get-tuple-element.43), channel_id=1, source_target_pairs={{0,3},{1,0},{2,1},{3,2},{4,7},{5,4},{6,5},{7,6},{8,11},{9,8},{10,9... | collective-permute-start | bytes 1179656 | tf_op jit(solution)/shard_map/ppermute | solution.py:658
  121.0 99.6 %collective-permute-start.64 = (f32[768,1536]{1,0:T(8,128)S(1)}, f32[768,1536]{1,0:T(8,128)S(1)}, u32[]{:S(2)}, u32[]{:S(2)}) collective-permute-start(f32[768,1536]{1,0:T(8,128)S(1)} %get-tuple-element.63), channel_id=1, source_target_pairs={{0,4},{4,0},{8,12},{12,8},{16,20},{20,16},{24,28},{28,24},{1,5},{5... | collective-permute-start | bytes 14155784 | tf_op jit(solution)/shard_map/ppermute | solution.py:661
  121.1 11.5 %collective-permute-start.8 = (bf16[128,1536]{1,0:T(8,128)(2,1)S(1)}, bf16[128,1536]{1,0:T(8,128)(2,1)S(1)}, u32[]{:S(2)}, u32[]{:S(2)}) collective-permute-start(bf16[128,1536]{1,0:T(8,128)(2,1)S(1)} %collective-permute-done.7.refs_1_), channel_id=1, source_target_pairs={{0,8},{4,12},{8,0},{12,4},{16,24},{20,28},{24,16},{28,20},{1,9},{5... | collective-permute-start | bytes 1179656 | tf_op jit(solution)/shard_map/ppermute | solution.py:661
  121.7 13.1 %collective-permute-start.9 = (bf16[128,1536]{1,0:T(8,128)(2,1)S(1)}, bf16[128,1536]{1,0:T(8,128)(2,1)S(1)}, u32[]{:S(2)}, u32[]{:S(2)}) collective-permute-start(bf16[128,1536]{1,0:T(8,128)(2,1)S(1)} %collective-permute-done.7.refs_1_), channel_id=1, source_target_pairs={{0,16},{4,20},{8,24},{12,28},{16,0},{20,4},{24,8},{28,12},{1,17},{... | collective-permute-start | bytes 1179656 | tf_op jit(solution)/shard_map/ppermute | solution.py:661
  123.3 22.4 %collective-permute-start.30 = (bf16[64,6144]{1,0:T(8,128)(2,1)S(1)}, bf16[64,6144]{1,0:T(8,128)(2,1)S(1)}, u32[]{:S(2)}, u32[]{:S(2)}) collective-permute-start(bf16[64,6144]{1,0:T(8,128)(2,1)S(1)} %get-tuple-element.72), channel_id=1, source_target_pairs={{0,1},{1,2},{2,3},{3,0},{4,5},{5,6},{6,7},{7,4},{8,9},{9,10},{10,1... | collective-permute-start | bytes 2359304 | tf_op jit(solution)/shard_map/ppermute | solution.py:658
  125.3 37.2 %collective-permute-start.44 = (bf16[64,6144]{1,0:T(8,128)(2,1)S(1)}, bf16[64,6144]{1,0:T(8,128)(2,1)S(1)}, u32[]{:S(2)}, u32[]{:S(2)}) collective-permute-start(bf16[64,6144]{1,0:T(8,128)(2,1)S(1)} %get-tuple-element.71), channel_id=1, source_target_pairs={{0,1},{1,2},{2,3},{3,0},{4,5},{5,6},{6,7},{7,4},{8,9},{9,10},{10,1... | collective-permute-start | bytes 2359304 | tf_op jit(solution)/shard_map/ppermute | solution.py:658
  132.6 45.6 %collective-permute-start.12 = (bf16[512,768]{1,0:T(8,128)(2,1)S(1)}, bf16[512,768]{1,0:T(8,128)(2,1)S(1)}, u32[]{:S(2)}, u32[]{:S(2)}) collective-permute-start(bf16[512,768]{1,0:T(8,128)(2,1)S(1)} %get-tuple-element.44), channel_id=1, source_target_pairs={{0,3},{1,0},{2,1},{3,2},{4,7},{5,4},{6,5},{7,6},{8,11},{9,8},{10,9... | collective-permute-start | bytes 2359304 | tf_op jit(solution)/shard_map/ppermute | solution.py:658
  134.8 6.2 %collective-permute-start.10 = (bf16[128,768]{1,0:T(8,128)(2,1)S(1)}, bf16[128,768]{1,0:T(8,128)(2,1)S(1)}, u32[]{:S(2)}, u32[]{:S(2)}) collective-permute-start(bf16[128,768]{1,0:T(8,128)(2,1)S(1)} %slice.36), channel_id=1, source_target_pairs={{0,16},{4,20},{8,24},{12,28},{16,0},{20,4},{24,8},{28,12},{1,17},{... | collective-permute-start | bytes 589832 | tf_op jit(solution)/shard_map/ppermute | solution.py:661
  141.0 23.1 %collective-permute-start.14 = (bf16[128,1536]{1,0:T(8,128)(2,1)S(1)}, bf16[128,1536]{1,0:T(8,128)(2,1)S(1)}, u32[]{:S(2)}, u32[]{:S(2)}) collective-permute-start(bf16[128,1536]{1,0:T(8,128)(2,1)S(1)} %collective-permute-done.7.refs_1_), channel_id=1, source_target_pairs={{0,4},{4,0},{8,12},{12,8},{16,20},{20,16},{24,28},{28,24},{1,5},{5... | collective-permute-start | bytes 1179656 | tf_op jit(solution)/shard_map/ppermute | solution.py:661
  145.7 20.0 %collective-permute-start.11 = (bf16[128,768]{1,0:T(8,128)(2,1)S(1)}, bf16[128,768]{1,0:T(8,128)(2,1)S(1)}, u32[]{:S(2)}, u32[]{:S(2)}) collective-permute-start(bf16[128,768]{1,0:T(8,128)(2,1)S(1)} %slice.37), channel_id=1, source_target_pairs={{0,8},{4,12},{8,0},{12,4},{16,24},{20,28},{24,16},{28,20},{1,9},{5... | collective-permute-start | bytes 589832 | tf_op jit(solution)/shard_map/ppermute | solution.py:661
  164.1 16.0 %collective-permute-start.45 = (bf16[64,1536]{1,0:T(8,128)(2,1)S(1)}, bf16[64,1536]{1,0:T(8,128)(2,1)S(1)}, u32[]{:S(2)}, u32[]{:S(2)}) collective-permute-start(bf16[64,1536]{1,0:T(8,128)(2,1)S(1)} %get-tuple-element.53), channel_id=1, source_target_pairs={{0,8},{4,12},{8,0},{12,4},{16,24},{20,28},{24,16},{28,20},{1,9},{5... | collective-permute-start | bytes 589832 | tf_op jit(solution)/shard_map/ppermute | solution.py:661
  165.7 15.1 %collective-permute-start.47 = (bf16[64,1536]{1,0:T(8,128)(2,1)S(1)}, bf16[64,1536]{1,0:T(8,128)(2,1)S(1)}, u32[]{:S(2)}, u32[]{:S(2)}) collective-permute-start(bf16[64,1536]{1,0:T(8,128)(2,1)S(1)} %get-tuple-element.55), channel_id=1, source_target_pairs={{0,16},{4,20},{8,24},{12,28},{16,0},{20,4},{24,8},{28,12},{1,17},{... | collective-permute-start | bytes 589832 | tf_op jit(solution)/shard_map/ppermute | solution.py:661
  166.2 13.5 %collective-permute-start.65 = (f32[8,768]{1,0:T(8,128)S(1)}, f32[8,768]{1,0:T(8,128)S(1)}, u32[]{:S(2)}, u32[]{:S(2)}) collective-permute-start(f32[8,768]{1,0:T(8,128)S(1)} %get-tuple-element.65), channel_id=1, source_target_pairs={{0,4},{4,0},{8,12},{12,8},{16,20},{20,16},{24,28},{28,24},{1,5},{5... | collective-permute-start | bytes 73736 | tf_op jit(solution)/shard_map/ppermute | solution.py:661
  178.2 14.3 %collective-permute-start.46 = (bf16[64,2304]{1,0:T(8,128)(2,1)S(1)}, bf16[64,2304]{1,0:T(8,128)(2,1)S(1)}, u32[]{:S(2)}, u32[]{:S(2)}) collective-permute-start(bf16[64,2304]{1,0:T(8,128)(2,1)S(1)} %get-tuple-element.54), channel_id=1, source_target_pairs={{0,8},{4,12},{8,0},{12,4},{16,24},{20,28},{24,16},{28,20},{1,9},{5... | collective-permute-start | bytes 884744 | tf_op jit(solution)/shard_map/ppermute | solution.py:661
  179.7 13.7 %collective-permute-start.48 = (bf16[64,2304]{1,0:T(8,128)(2,1)S(1)}, bf16[64,2304]{1,0:T(8,128)(2,1)S(1)}, u32[]{:S(2)}, u32[]{:S(2)}) collective-permute-start(bf16[64,2304]{1,0:T(8,128)(2,1)S(1)} %get-tuple-element.56), channel_id=1, source_target_pairs={{0,16},{4,20},{8,24},{12,28},{16,0},{20,4},{24,8},{28,12},{1,17},{... | collective-permute-start | bytes 884744 | tf_op jit(solution)/shard_map/ppermute | solution.py:661
  180.2 11.2 %collective-permute-start.31 = (bf16[64,1536]{1,0:T(8,128)(2,1)S(1)}, bf16[64,1536]{1,0:T(8,128)(2,1)S(1)}, u32[]{:S(2)}, u32[]{:S(2)}) collective-permute-start(bf16[64,1536]{1,0:T(8,128)(2,1)S(1)} %get-tuple-element.48), channel_id=1, source_target_pairs={{0,8},{4,12},{8,0},{12,4},{16,24},{20,28},{24,16},{28,20},{1,9},{5... | collective-permute-start | bytes 589832 | tf_op jit(solution)/shard_map/ppermute | solution.py:661
  180.7 11.8 %collective-permute-start.33 = (bf16[64,1536]{1,0:T(8,128)(2,1)S(1)}, bf16[64,1536]{1,0:T(8,128)(2,1)S(1)}, u32[]{:S(2)}, u32[]{:S(2)}) collective-permute-start(bf16[64,1536]{1,0:T(8,128)(2,1)S(1)} %get-tuple-element.50), channel_id=1, source_target_pairs={{0,16},{4,20},{8,24},{12,28},{16,0},{20,4},{24,8},{28,12},{1,17},{... | collective-permute-start | bytes 589832 | tf_op jit(solution)/shard_map/ppermute | solution.py:661
  191.3 12.4 %collective-permute-start.51 = (bf16[64,3072]{1,0:T(8,128)(2,1)S(1)}, bf16[64,3072]{1,0:T(8,128)(2,1)S(1)}, u32[]{:S(2)}, u32[]{:S(2)}) collective-permute-start(bf16[64,3072]{1,0:T(8,128)(2,1)S(1)} %get-tuple-element.52.refs_14_), channel_id=1, source_target_pairs={{0,4},{4,0},{8,12},{12,8},{16,20},{20,16},{24,28},{28,24},{1,5},{5... | collective-permute-start | bytes 1179656 | tf_op jit(solution)/shard_map/ppermute | solution.py:661
  192.5 11.2 %collective-permute-start.37 = (bf16[64,3072]{1,0:T(8,128)(2,1)S(1)}, bf16[64,3072]{1,0:T(8,128)(2,1)S(1)}, u32[]{:S(2)}, u32[]{:S(2)}) collective-permute-start(bf16[64,3072]{1,0:T(8,128)(2,1)S(1)} %get-tuple-element.47.refs_0_), channel_id=1, source_target_pairs={{0,4},{4,0},{8,12},{12,8},{16,20},{20,16},{24,28},{28,24},{1,5},{5... | collective-permute-start | bytes 1179656 | tf_op jit(solution)/shard_map/ppermute | solution.py:661
  192.5 9.4 %collective-permute-start.32 = (bf16[64,2304]{1,0:T(8,128)(2,1)S(1)}, bf16[64,2304]{1,0:T(8,128)(2,1)S(1)}, u32[]{:S(2)}, u32[]{:S(2)}) collective-permute-start(bf16[64,2304]{1,0:T(8,128)(2,1)S(1)} %get-tuple-element.49), channel_id=1, source_target_pairs={{0,8},{4,12},{8,0},{12,4},{16,24},{20,28},{24,16},{28,20},{1,9},{5... | collective-permute-start | bytes 884744 | tf_op jit(solution)/shard_map/ppermute | solution.py:661
  193.3 9.1 %collective-permute-start.34 = (bf16[64,2304]{1,0:T(8,128)(2,1)S(1)}, bf16[64,2304]{1,0:T(8,128)(2,1)S(1)}, u32[]{:S(2)}, u32[]{:S(2)}) collective-permute-start(bf16[64,2304]{1,0:T(8,128)(2,1)S(1)} %get-tuple-element.51), channel_id=1, source_target_pairs={{0,16},{4,20},{8,24},{12,28},{16,0},{20,4},{24,8},{28,12},{1,17},{... | collective-permute-start | bytes 884744 | tf_op jit(solution)/shard_map/ppermute | solution.py:661
  202.0 6.5 %collective-permute-start.49 = (bf16[64,1536]{1,0:T(8,128)(2,1)S(1)}, bf16[64,1536]{1,0:T(8,128)(2,1)S(1)}, u32[]{:S(2)}, u32[]{:S(2)}) collective-permute-start(bf16[64,1536]{1,0:T(8,128)(2,1)S(1)} %collective-permute-done.45.refs_15_), channel_id=1, source_target_pairs={{0,16},{4,20},{8,24},{12,28},{16,0},{20,4},{24,8},{28,12},{1,17},{... | collective-permute-start | bytes 589832 | tf_op jit(solution)/shard_map/ppermute | solution.py:661
  202.5 6.5 %collective-permute-start.50 = (bf16[64,1536]{1,0:T(8,128)(2,1)S(1)}, bf16[64,1536]{1,0:T(8,128)(2,1)S(1)}, u32[]{:S(2)}, u32[]{:S(2)}) collective-permute-start(bf16[64,1536]{1,0:T(8,128)(2,1)S(1)} %collective-permute-done.47.refs_17_), channel_id=1, source_target_pairs={{0,8},{4,12},{8,0},{12,4},{16,24},{20,28},{24,16},{28,20},{1,9},{5... | collective-permute-start | bytes 589832 | tf_op jit(solution)/shard_map/ppermute | solution.py:661
  203.7 6.2 %collective-permute-start.52 = (bf16[64,1536]{1,0:T(8,128)(2,1)S(1)}, bf16[64,1536]{1,0:T(8,128)(2,1)S(1)}, u32[]{:S(2)}, u32[]{:S(2)}) collective-permute-start(bf16[64,1536]{1,0:T(8,128)(2,1)S(1)} %collective-permute-done.45.refs_15_), channel_id=1, source_target_pairs={{0,4},{4,0},{8,12},{12,8},{16,20},{20,16},{24,28},{28,24},{1,5},{5... | collective-permute-start | bytes 589832 | tf_op jit(solution)/shard_map/ppermute | solution.py:661
  203.7 6.2 %collective-permute-start.54 = (bf16[64,1536]{1,0:T(8,128)(2,1)S(1)}, bf16[64,1536]{1,0:T(8,128)(2,1)S(1)}, u32[]{:S(2)}, u32[]{:S(2)}) collective-permute-start(bf16[64,1536]{1,0:T(8,128)(2,1)S(1)} %collective-permute-done.47.refs_17_), channel_id=1, source_target_pairs={{0,4},{4,0},{8,12},{12,8},{16,20},{20,16},{24,28},{28,24},{1,5},{5... | collective-permute-start | bytes 589832 | tf_op jit(solution)/shard_map/ppermute | solution.py:661
  208.4 5.7 %collective-permute-start.35 = (bf16[64,1536]{1,0:T(8,128)(2,1)S(1)}, bf16[64,1536]{1,0:T(8,128)(2,1)S(1)}, u32[]{:S(2)}, u32[]{:S(2)}) collective-permute-start(bf16[64,1536]{1,0:T(8,128)(2,1)S(1)} %collective-permute-done.31.refs_1_), channel_id=1, source_target_pairs={{0,16},{4,20},{8,24},{12,28},{16,0},{20,4},{24,8},{28,12},{1,17},{... | collective-permute-start | bytes 589832 | tf_op jit(solution)/shard_map/ppermute | solution.py:661
  208.9 5.7 %collective-permute-start.36 = (bf16[64,1536]{1,0:T(8,128)(2,1)S(1)}, bf16[64,1536]{1,0:T(8,128)(2,1)S(1)}, u32[]{:S(2)}, u32[]{:S(2)}) collective-permute-start(bf16[64,1536]{1,0:T(8,128)(2,1)S(1)} %collective-permute-done.33.refs_3_), channel_id=1, source_target_pairs={{0,8},{4,12},{8,0},{12,4},{16,24},{20,28},{24,16},{28,20},{1,9},{5... | collective-permute-start | bytes 589832 | tf_op jit(solution)/shard_map/ppermute | solution.py:661
  209.9 5.2 %collective-permute-start.40 = (bf16[64,1536]{1,0:T(8,128)(2,1)S(1)}, bf16[64,1536]{1,0:T(8,128)(2,1)S(1)}, u32[]{:S(2)}, u32[]{:S(2)}) collective-permute-start(bf16[64,1536]{1,0:T(8,128)(2,1)S(1)} %collective-permute-done.33.refs_3_), channel_id=1, source_target_pairs={{0,4},{4,0},{8,12},{12,8},{16,20},{20,16},{24,28},{28,24},{1,5},{5... | collective-permute-start | bytes 589832 | tf_op jit(solution)/shard_map/ppermute | solution.py:661
  216.6 19.6 %collective-permute-start.6 = (bf16[512,768]{1,0:T(8,128)(2,1)S(1)}, bf16[512,768]{1,0:T(8,128)(2,1)S(1)}, u32[]{:S(2)}, u32[]{:S(2)}) collective-permute-start(bf16[512,768]{1,0:T(8,128)(2,1)S(1)} %get-tuple-element.42), channel_id=1, source_target_pairs={{0,3},{1,0},{2,1},{3,2},{4,7},{5,4},{6,5},{7,6},{8,11},{9,8},{10,9... | collective-permute-start | bytes 2359304 | tf_op jit(solution)/shard_map/ppermute | solution.py:658
  217.5 18.7 %collective-permute-start.13 = (bf16[512,768]{1,0:T(8,128)(2,1)S(1)}, bf16[512,768]{1,0:T(8,128)(2,1)S(1)}, u32[]{:S(2)}, u32[]{:S(2)}) collective-permute-start(bf16[512,768]{1,0:T(8,128)(2,1)S(1)} %collective-permute-done.12), channel_id=1, source_target_pairs={{0,4},{4,0},{8,12},{12,8},{16,20},{20,16},{24,28},{28,24},{1,5},{5... | collective-permute-start | bytes 2359304 | tf_op jit(solution)/shard_map/ppermute | solution.py:661
  (28 other events, 107.3 us)
where the time goes:
time: 243 us
  waiting for transfers between devices  156 us (64%)
  starting transfers between devices  52.1 us (21%)
  Pallas kernels  25.4 us (10%)
  local copies, waits for them, and re-layouts  7.39 us (3%)
    ppermute x57, waiting for transfers between devices, swap(): return lax.ppermute(x, 'row', [(r, r ^ mask) for r in range(rows_axis)])  89.4 us
    ppermute x9, waiting for transfers between devices, ring(): lax.ppermute(x, 'col', [(c, (c + shift) % cols_axis) for c in range(cols_...  67 us
    ppermute x57, starting transfers between devices, swap(): return lax.ppermute(x, 'row', [(r, r ^ mask) for r in range(rows_axis)])  34.5 us
    ppermute x9, starting transfers between devices, ring(): lax.ppermute(x, 'col', [(c, (c + shift) % cols_axis) for c in range(cols_...  17.6 us
    pallas_call x3, Pallas kernels, gram_direct(): pl.pallas_call(kernel, in_specs=[VMEM] * (count + 1 + len(before)), out_s...  15.6 us
    unnamed x20, local copies, waits for them, and re-layouts  6.65 us
  transfers between devices with their start and end apart: 66, of which 27 were waited for; matrix products, arithmetic and copies ran while one was open for 0% of the time, Pallas kernels for 8%

commit v1 on v0

--- a/solution.py
+++ b/solution.py
@@ -10,6 +10,8 @@
 ANY = pl.BlockSpec(memory_space=pl.ANY)
 VMEM = pl.BlockSpec(memory_space=pltpu.VMEM)
 SMEM = pl.BlockSpec(memory_space=pltpu.SMEM)
+HBM = pl.BlockSpec(memory_space=pltpu.HBM)
+SPLITS = 1
 
 
 def factor_math(n, arcs, len_ref, amp_ref, decay_ref, obs_ref, gap_ref, noise_ref):
@@ -430,7 +432,7 @@
     return pl.pallas_call(
         kernel,
         name="head",
-        in_specs=[SMEM] + [ANY] * 8,
+        in_specs=[SMEM] + [HBM] * 8,
         out_specs=[VMEM] * 7,
         out_shape=[jax.ShapeDtypeStruct((h, w), t) for h, w, t in outs],
         scratch_shapes=[
@@ -514,20 +516,22 @@
     block_rows = obs[0].shape[1]
 
     def kernel(plan_ref, where_ref, *refs):
-        sources, (rows_ref, picked_ref) = refs[:-2], refs[-2:]
+        sources, (rows_ref, picked_ref, held) = refs[:-3], refs[-3:]
+        at = 0
+        for source in sources:
+            held[at : at + source.shape[0], :] = source[...]
+            at += source.shape[0]
         at = 0
         for m, s, (begin, end) in places:
-            line = jnp.broadcast_to(sources[m][s : s + 1, :], (8, block_rows))
-            rows_ref[:, at : at + end - begin] = line[:, begin:end]
+            line = m * cols_axis + s
+            wide = jnp.broadcast_to(held[line : line + 1, :], (8, block_rows))
+            rows_ref[:, at : at + end - begin] = wide[:, begin:end]
             at += end - begin
         from_row = lax.div(plan_ref[0], cols_axis)
         from_col = lax.rem(plan_ref[0], cols_axis)
         mask = jnp.bitwise_xor(from_row, where_ref[0])
         step = lax.rem(where_ref[1] - from_col + cols_axis, cols_axis)
-        picked = jnp.zeros((1, block_rows), F32)
-        for m, source in enumerate(sources):
-            picked = jnp.where(mask == m, source[pl.ds(step, 1), :], picked)
-        picked_ref[...] = picked
+        picked_ref[...] = held[pl.ds(mask * cols_axis + step, 1), :]
 
     return pl.pallas_call(
         kernel,
@@ -538,6 +542,7 @@
             jax.ShapeDtypeStruct((8, sum(end - begin for _, _, (begin, end) in places)), F32),
             jax.ShapeDtypeStruct((1, block_rows), F32),
         ],
+        scratch_shapes=[pltpu.VMEM((sum(v.shape[0] for v in obs), block_rows), F32)],
         cost_estimate=pl.CostEstimate(flops=10**7, bytes_accessed=10**5, transcendentals=0),
         compiler_params=pltpu.CompilerParams(vmem_limit_bytes=4 << 20),
     )(plan, where, *obs)
@@ -660,11 +665,11 @@
     def swap(x, mask):
         return lax.ppermute(x, "row", [(r, r ^ mask) for r in range(rows_axis)])
 
-    middle = block_rows // 2
+    cuts = [(k * block_rows // SPLITS, (k + 1) * block_rows // SPLITS) for k in range(SPLITS)]
     chunks = [design]
     for _ in range(1, last - 1):
         chunks.append(ring(chunks[-1], 1))
-    halves = [ring(chunks[-1][:middle], 1), ring(chunks[-1][middle:], 1)]
+    pieces = [ring(chunks[-1][a:b], 1) for a, b in cuts]
     near, *parts = head(
         design,
         (observations, gaps, noise_var),
@@ -676,7 +681,11 @@
     )
     line = [near] + [ring(near, s) for s in range(1, cols_axis)]
     line_obs = jnp.stack([part[block_rows] for part in line])
-    obs = [line_obs] + [swap(line_obs, m) for m in range(1, rows_axis)]
+    obs = [line_obs]
+    mask = 1
+    while mask < rows_axis:
+        obs.append(swap(jnp.concatenate(obs, axis=0), mask))
+        mask *= 2
 
     def trade(xa, xb, ya, yb, keep):
         xa, ya = swap(xa, 2), swap(ya, 4)
@@ -687,9 +696,9 @@
     for s in range(1, last - 1):
         cut = pack_cut([chunks[s]], line[s], tile_map, where, rows_axis, cols_axis, 0)
         traded.append(trade(*cut))
-    for k, begin in enumerate((0, middle)):
+    for k, (begin, _) in enumerate(cuts):
         cut = pack_cut(
-            halves[: k + 1], line[last - 1], tile_map, where, rows_axis, cols_axis, begin
+            pieces[: k + 1], line[last - 1], tile_map, where, rows_axis, cols_axis, begin
         )
         traded.append(trade(*cut))
 
@@ -728,11 +737,10 @@
         return [(2 * n + core, s, rows) for n in range(count)]
 
     whole = (0, block_rows)
-    parts_of = ((0, middle), (middle, block_rows))
     early, mid, late = [], [], []
     for s in range(last - 1):
         early += seen(4, 0, s, whole)
-    for rows in parts_of:
+    for rows in cuts:
         for core in (0, 1):
             mid += seen(4, core, last - 1, rows)
     for core in (0, 1):
@@ -751,11 +759,12 @@
 
     at_row = 4 * (last - 1) * block_rows
     blocks, operands = [], []
-    for k in (last - 1, last):
+    for k in range(last - 1, len(traded)):
         mine = list(traded[k])
+        height = block_rows // SPLITS
         theirs = [swap(v, 1) for v in mine]
-        blocks += part_blocks(len(operands), middle, 0, False)
-        blocks += part_blocks(len(operands) + 7, middle, 1, False)
+        blocks += part_blocks(len(operands), height, 0, False)
+        blocks += part_blocks(len(operands) + 7, height, 1, False)
         operands += mine + theirs
     most, most_rhs = gram_direct(
         blocks,

time: 243 us -> 252 us (1.037)
  waiting for transfers between devices: 156 us -> 164 us
  local copies, waits for them, and re-layouts: 7.39 us -> 10.8 us
  starting transfers between devices: 52.1 us -> 49.3 us
    ppermute x9 -> x8, waiting for transfers between devices: 67 us -> 78.1 us  [ring(): lax.ppermute(x, 'col', [(c, (c + shift) % cols_axis) for c in range(cols_...]
    unnamed x20 -> x30, local copies, waits for them, and re-layouts: 6.65 us -> 10.2 us
    ppermute x57 -> x40, waiting for transfers between devices: 89.4 us -> 86.2 us  [swap(): return lax.ppermute(x, 'row', [(r, r ^ mask) for r in range(rows_axis)])]
    ppermute x57 -> x40, starting transfers between devices: 34.5 us -> 32.7 us  [swap(): return lax.ppermute(x, 'row', [(r, r ^ mask) for r in range(rows_axis)])]
    ppermute x9 -> x8, starting transfers between devices: 17.6 us -> 16.6 us  [ring(): lax.ppermute(x, 'col', [(c, (c + shift) % cols_axis) for c in range(cols_...]
  transfers between devices with their start and end apart: 66 -> 48, of which waited for: 27 -> 20; matrix products, arithmetic and copies ran while one was open for 0% -> 0% of each run, Pallas kernels for 8% -> 5%
where the time goes in v1:
time: 252 us; the launch traced here: 251 us
  waiting for transfers between devices  164 us (65%)
  starting transfers between devices  49.3 us (20%)
  Pallas kernels  25.4 us (10%)
  local copies, waits for them, and re-layouts  10.8 us (4%)
    ppermute x40, waiting for transfers between devices, swap(): return lax.ppermute(x, 'row', [(r, r ^ mask) for r in range(rows_axis)])  86.2 us
    ppermute x8, waiting for transfers between devices, ring(): lax.ppermute(x, 'col', [(c, (c + shift) % cols_axis) for c in range(cols_...  78.1 us
    ppermute x40, starting transfers between devices, swap(): return lax.ppermute(x, 'row', [(r, r ^ mask) for r in range(rows_axis)])  32.7 us
    ppermute x8, starting transfers between devices, ring(): lax.ppermute(x, 'col', [(c, (c + shift) % cols_axis) for c in range(cols_...  16.6 us
    pallas_call x3, Pallas kernels, gram_direct(): pl.pallas_call(kernel, in_specs=[VMEM] * (count + 1 + len(before)), out_s...  16 us
    unnamed x30, local copies, waits for them, and re-layouts  10.2 us
  transfers between devices with their start and end apart: 48, of which 20 were waited for; matrix products, arithmetic and copies ran while one was open for 0% of the time, Pallas kernels for 5%

profile of v1, /device:TPU:0, one launch (start us, length us, event | category | flops | bytes accessed | tf_op | source)
XLA Modules:
  0.0 251.4 jit_solution(3918238787110118569)
XLA Ops:
  0.6 3.1 %collective-permute-start.25 = (bf16[128,6144]{1,0:T(8,128)(2,1)}, bf16[128,6144]{1,0:T(8,128)(2,1)S(1)}, u32[]{:S(2)}, u32[]{:S(2)}) collective-permute-start(bf16[128,6144]{1,0:T(8,128)(2,1)} %refs_0_.1), channel_id=1, source_target_pairs={{0,1},{1,2},{2,3},{3,0},{4,5},{5,6},{6,7},{7,4},{8,9},{9,10},{10,1... | collective-permute-start | bytes 4718600 | tf_op jit(solution)/shard_map/ppermute | solution.py:663
  3.8 1.4 copy-done
  9.8 4.4 %head.1 = (f32[136,128]{1,0:T(8,128)S(1)}, bf16[128,1536]{1,0:T(8,128)(2,1)}, bf16[128,2304]{1,0:T(8,128)(2,1)}, bf16[128,1536]{1,0:T(8,128)(2,1)S(1)}, bf16[128...) custom-call(s32[2]{0:T(128)S(1)} %pad_add_fusion.where_ref, ...), custom_call_target="tpu_custom_call" | custom-call | flops 1000000000 | bytes 5000000 | tf_op jit(solution)/shard_map/head/pallas_call | solution.py:432
  16.6 1.6 collective-permute-start.19
  19.2 2.9 %collective-permute-start.21 = (f32[136,128]{1,0:T(8,128)S(1)}, f32[136,128]{1,0:T(8,128)S(1)}, u32[]{:S(2)}, u32[]{:S(2)}) collective-permute-start(f32[136,128]{1,0:T(8,128)S(1)} %get-tuple-element.40), channel_id=1, source_target_pairs={{0,3},{1,0},{2,1},{3,2},{4,7},{5,4},{6,5},{7,6},{8,11},{9,8},{10,9... | collective-permute-start | bytes 208904 | tf_op jit(solution)/shard_map/ppermute | solution.py:663
  22.1 1.5 collective-permute-start.2
  23.6 19.2 %collective-permute-done.19.near_ref = f32[136,128]{1,0:T(8,128)S(1)} collective-permute-done((f32[136,128]{1,0:T(8,128)S(1)}, f32[136,128]{1,0:T(8,128)S(1)}, u32[]{:S(2)}, u32[]{:S(2)}) %collective-permute-start.19) | collective-permute-done | bytes 69664 | tf_op jit(solution)/shard_map/ppermute | solution.py:663
  42.8 2.2 collective-permute-done.20.near_ref
  46.3 1.5 collective-permute-start.23
  48.3 1.5 collective-permute-start.1
  49.9 1.5 collective-permute-start.4
  52.0 1.5 collective-permute-start.3
  54.2 1.9 pack_cut.3
  56.1 17.0 %collective-permute-done.24.refs_3_ = f32[16,128]{1,0:T(8,128)S(1)} collective-permute-done((f32[16,128]{1,0:T(8,128)S(1)}, f32[16,128]{1,0:T(8,128)S(1)}, u32[]{:S(2)}, u32[]{:S(2)}) %collective-permute-start.24) | collective-permute-done | bytes 8224 | tf_op jit(solution)/shard_map/ppermute | solution.py:666
  73.1 1.5 collective-permute-start.40
  74.6 1.5 collective-permute-start.42
  77.2 4.4 %collective-permute-done.3.fa_ref.refs_5_ = bf16[128,1536]{1,0:T(8,128)(2,1)S(1)} collective-permute-done((bf16[128,1536]{1,0:T(8,128)(2,1)}, bf16[128,1536]{1,0:T(8,128)(2,1)S(1)}, u32[]{:S(2)}, u32[]{:S(2)}) %collective-permute-start.3) | collective-permute-done | bytes 393248 | tf_op jit(solution)/shard_map/ppermute | solution.py:666
  81.6 1.5 collective-permute-start.5
  83.1 2.1 collective-permute-done.40.refs_8_
  85.1 1.5 collective-permute-start.44
  86.6 3.3 %collective-permute-done.42.refs_10_ = bf16[128,1536]{1,0:T(8,128)(2,1)S(1)} collective-permute-done((bf16[128,1536]{1,0:T(8,128)(2,1)S(1)}, bf16[128,1536]{1,0:T(8,128)(2,1)S(1)}, u32[]{:S(2)}, u32[]{:S(2)}) %collective-permute-start.42) | collective-permute-done | bytes 393248 | tf_op jit(solution)/shard_map/ppermute | solution.py:666
  90.0 1.5 collective-permute-start.45
  93.2 13.0 %collective-permute-done.5.fb_ref.refs_6_ = bf16[128,1536]{1,0:T(8,128)(2,1)S(1)} collective-permute-done((bf16[128,1536]{1,0:T(8,128)(2,1)}, bf16[128,1536]{1,0:T(8,128)(2,1)S(1)}, u32[]{:S(2)}, u32[]{:S(2)}) %collective-permute-start.5) | collective-permute-done | bytes 393248 | tf_op jit(solution)/shard_map/ppermute | solution.py:666
  106.2 3.5 %collective-permute-done.44.refs_12_ = bf16[128,1536]{1,0:T(8,128)(2,1)S(1)} collective-permute-done((bf16[128,1536]{1,0:T(8,128)(2,1)S(1)}, bf16[128,1536]{1,0:T(8,128)(2,1)S(1)}, u32[]{:S(2)}, u32[]{:S(2)}) %collective-permute-start.44) | collective-permute-done | bytes 393248 | tf_op jit(solution)/shard_map/ppermute | solution.py:666
  109.7 1.4 collective-permute-done.45.refs_13_
  112.3 6.8 %shard_map.112 = (f32[768,1536]{1,0:T(8,128)S(1)}, f32[768,1536]{1,0:T(8,128)S(1)}, f32[8,768]{1,0:T(8,128)S(1)}, f32[8,768]{1,0:T(8,128)S(1)}) custom-call(bf16[128,3072]{1,0:T(8,128)(2,1)S(1)} %copy-done.14, bf16[128,1536]{1,0:T(8,128)(2,1)} %collective-permute-done.2.refs_1_, bf16[128,2304]{1,0:T(8,128)(2,1)S(1)} %collective-permute-done.xb_ref.refs_2_, ...), custom_call_target="tpu_custom_call" | custom-call | flops 4831838208 | bytes 20000000 | tf_op jit(solution)/shard_map/pallas_call | solution.py:624
  119.2 2.0 collective-permute-start.26
  121.2 1.9 collective-permute-start.7
  123.0 43.0 %collective-permute-done.7.refs_1_ = bf16[128,1536]{1,0:T(8,128)(2,1)S(1)} collective-permute-done((bf16[128,1536]{1,0:T(8,128)(2,1)S(1)}, bf16[128,1536]{1,0:T(8,128)(2,1)S(1)}, u32[]{:S(2)}, u32[]{:S(2)}) %collective-permute-start.7) | collective-permute-done | bytes 393248 | tf_op jit(solution)/shard_map/ppermute | solution.py:663
  166.1 1.5 collective-permute-start.8
  167.5 1.5 collective-permute-start.9
  169.2 2.3 collective-permute-start.12
  171.5 5.5 %collective-permute-done.8.refs_2_ = bf16[128,1536]{1,0:T(8,128)(2,1)S(1)} collective-permute-done((bf16[128,1536]{1,0:T(8,128)(2,1)S(1)}, bf16[128,1536]{1,0:T(8,128)(2,1)S(1)}, u32[]{:S(2)}, u32[]{:S(2)}) %collective-permute-start.8) | collective-permute-done | bytes 393248 | tf_op jit(solution)/shard_map/ppermute | solution.py:666
  178.2 1.5 collective-permute-start.10
  180.3 4.1 %collective-permute-done.10.refs_4_ = bf16[128,768]{1,0:T(8,128)(2,1)S(1)} collective-permute-done((bf16[128,768]{1,0:T(8,128)(2,1)S(1)}, bf16[128,768]{1,0:T(8,128)(2,1)S(1)}, u32[]{:S(2)}, u32[]{:S(2)}) %collective-permute-start.10) | collective-permute-done | bytes 196640 | tf_op jit(solution)/shard_map/ppermute | solution.py:666
  184.9 2.0 pack_cut.2
  186.9 1.5 collective-permute-start.28
  188.4 1.5 collective-permute-start.30
  191.0 19.6 %collective-permute-done.27.refs_1_ = bf16[128,1536]{1,0:T(8,128)(2,1)S(1)} collective-permute-done((bf16[128,1536]{1,0:T(8,128)(2,1)S(1)}, bf16[128,1536]{1,0:T(8,128)(2,1)S(1)}, u32[]{:S(2)}, u32[]{:S(2)}) %collective-permute-start.27) | collective-permute-done | bytes 393248 | tf_op jit(solution)/shard_map/ppermute | solution.py:666
  210.6 1.5 collective-permute-start.31
  212.1 1.5 collective-permute-start.32
  214.1 6.6 %collective-permute-done.31.refs_5_ = bf16[128,1536]{1,0:T(8,128)(2,1)S(1)} collective-permute-done((bf16[128,1536]{1,0:T(8,128)(2,1)S(1)}, bf16[128,1536]{1,0:T(8,128)(2,1)S(1)}, u32[]{:S(2)}, u32[]{:S(2)}) %collective-permute-start.31) | collective-permute-done | bytes 393248 | tf_op jit(solution)/shard_map/ppermute | solution.py:666
  220.8 1.2 collective-permute-done.32.refs_6_
  222.5 2.1 collective-permute-done.36.refs_10_
  225.0 1.8 collective-permute-start.6
  227.9 3.0 %shard_map.113 = (f32[768,1536]{1,0:T(8,128)S(1)}, f32[8,768]{1,0:T(8,128)S(1)}) custom-call(bf16[128,3072]{1,0:T(8,128)(2,1)S(1)} %get-tuple-element.42.refs_0_, bf16[128,1536]{1,0:T(8,128)(2,1)S(1)} %collective-permute-done.27.refs_1_, bf16[128,2304]{1,0:T(8,128)(2,1)S(1)} %collective-permute-done.28.refs_2_, ...), custom_call_target="tpu_custom_call" | custom-call | flops 2415919104 | bytes 20000000 | tf_op jit(solution)/shard_map/pallas_call | solution.py:624
  230.9 13.7 %collective-permute-done.6.refs_0_ = bf16[512,768]{1,0:T(8,128)(2,1)S(1)} collective-permute-done((bf16[512,768]{1,0:T(8,128)(2,1)S(1)}, bf16[512,768]{1,0:T(8,128)(2,1)S(1)}, u32[]{:S(2)}, u32[]{:S(2)}) %collective-permute-start.6) | collective-permute-done | bytes 786464 | tf_op jit(solution)/shard_map/ppermute | solution.py:663
  244.6 6.1 %shard_map.114 = (f32[768,1536]{1,0:T(8,128)}, f32[8,768]{1,0:T(8,128)S(1)}) custom-call(bf16[512,768]{1,0:T(8,128)(2,1)S(1)} %collective-permute-done.6.refs_0_, bf16[128,1536]{1,0:T(8,128)(2,1)S(1)} %collective-permute-done.7.refs_1_, bf16[128,1536]{1,0:T(8,128)(2,1)S(1)} %collective-permute-done.8.refs_2_, ...), custom_call_target="tpu_custom_call" | custom-call | flops 2415919104 | bytes 20000000 | tf_op jit(solution)/shard_map/pallas_call | solution.py:624
  (97 shorter events, 21.2 us)
Async XLA Ops:
  0.6 51.4 %collective-permute-start.25 = (bf16[128,6144]{1,0:T(8,128)(2,1)}, bf16[128,6144]{1,0:T(8,128)(2,1)S(1)}, u32[]{:S(2)}, u32[]{:S(2)}) collective-permute-start(bf16[128,6144]{1,0:T(8,128)(2,1)} %refs_0_.1), channel_id=1, source_target_pairs={{0,1},{1,2},{2,3},{3,0},{4,5},{5,6},{6,7},{7,4},{8,9},{9,10},{10,1... | collective-permute-start | bytes 4718600 | tf_op jit(solution)/shard_map/ppermute | solution.py:663
  16.6 26.2 %collective-permute-start.19 = (f32[136,128]{1,0:T(8,128)S(1)}, f32[136,128]{1,0:T(8,128)S(1)}, u32[]{:S(2)}, u32[]{:S(2)}) collective-permute-start(f32[136,128]{1,0:T(8,128)S(1)} %get-tuple-element.40), channel_id=1, source_target_pairs={{0,1},{1,2},{2,3},{3,0},{4,5},{5,6},{6,7},{7,4},{8,9},{9,10},{10,1... | collective-permute-start | bytes 208904 | tf_op jit(solution)/shard_map/ppermute | solution.py:663
  18.1 26.9 %collective-permute-start.20 = (f32[136,128]{1,0:T(8,128)S(1)}, f32[136,128]{1,0:T(8,128)S(1)}, u32[]{:S(2)}, u32[]{:S(2)}) collective-permute-start(f32[136,128]{1,0:T(8,128)S(1)} %get-tuple-element.40), channel_id=1, source_target_pairs={{0,2},{1,3},{2,0},{3,1},{4,6},{5,7},{6,4},{7,5},{8,10},{9,11},{10,... | collective-permute-start | bytes 208904 | tf_op jit(solution)/shard_map/ppermute | solution.py:663
  19.2 25.8 %collective-permute-start.21 = (f32[136,128]{1,0:T(8,128)S(1)}, f32[136,128]{1,0:T(8,128)S(1)}, u32[]{:S(2)}, u32[]{:S(2)}) collective-permute-start(f32[136,128]{1,0:T(8,128)S(1)} %get-tuple-element.40), channel_id=1, source_target_pairs={{0,3},{1,0},{2,1},{3,2},{4,7},{5,4},{6,5},{7,6},{8,11},{9,8},{10,9... | collective-permute-start | bytes 208904 | tf_op jit(solution)/shard_map/ppermute | solution.py:663
  22.1 29.4 %collective-permute-start.2 = (bf16[128,1536]{1,0:T(8,128)(2,1)}, bf16[128,1536]{1,0:T(8,128)(2,1)}, u32[]{:S(2)}, u32[]{:S(2)}) collective-permute-start(bf16[128,1536]{1,0:T(8,128)(2,1)} %get-tuple-element.35), channel_id=1, source_target_pairs={{0,8},{4,12},{8,0},{12,4},{16,24},{20,28},{24,16},{28,20},{1,9},{5... | collective-permute-start | bytes 1179656 | tf_op jit(solution)/shard_map/ppermute | solution.py:666
  45.0 1.2 collective-permute-start.22
  46.3 3.7 %collective-permute-start.23 = (f32[8,128]{1,0:T(8,128)S(1)}, f32[8,128]{1,0:T(8,128)S(1)}, u32[]{:S(2)}, u32[]{:S(2)}) collective-permute-start(f32[8,128]{1,0:T(8,128)S(1)} %concatenate.8), channel_id=1, source_target_pairs={{0,8},{4,12},{8,0},{12,4},{16,24},{20,28},{24,16},{28,20},{1,9},{5... | collective-permute-start | bytes 12296 | tf_op jit(solution)/shard_map/ppermute | solution.py:666
  47.8 28.4 %collective-permute-start = (bf16[128,2304]{1,0:T(8,128)(2,1)}, bf16[128,2304]{1,0:T(8,128)(2,1)S(1)}, u32[]{:S(2)}, u32[]{:S(2)}) collective-permute-start(bf16[128,2304]{1,0:T(8,128)(2,1)} %get-tuple-element.33), channel_id=1, source_target_pairs={{0,8},{4,12},{8,0},{12,4},{16,24},{20,28},{24,16},{28,20},{1,9},{5... | collective-permute-start | bytes 1769480 | tf_op jit(solution)/shard_map/ppermute | solution.py:666
  48.3 28.4 %collective-permute-start.1 = (bf16[128,2304]{1,0:T(8,128)(2,1)S(1)}, bf16[128,2304]{1,0:T(8,128)(2,1)S(1)}, u32[]{:S(2)}, u32[]{:S(2)}) collective-permute-start(bf16[128,2304]{1,0:T(8,128)(2,1)S(1)} %get-tuple-element.34), channel_id=1, source_target_pairs={{0,16},{4,20},{8,24},{12,28},{16,0},{20,4},{24,8},{28,12},{1,17},{... | collective-permute-start | bytes 1769480 | tf_op jit(solution)/shard_map/ppermute | solution.py:666
  49.9 24.7 %collective-permute-start.4 = (bf16[128,1536]{1,0:T(8,128)(2,1)}, bf16[128,1536]{1,0:T(8,128)(2,1)}, u32[]{:S(2)}, u32[]{:S(2)}) collective-permute-start(bf16[128,1536]{1,0:T(8,128)(2,1)} %copy-done.3), channel_id=1, source_target_pairs={{0,16},{4,20},{8,24},{12,28},{16,0},{20,4},{24,8},{28,12},{1,17},{... | collective-permute-start | bytes 1179656 | tf_op jit(solution)/shard_map/ppermute | solution.py:666
  51.5 21.7 %collective-permute-start.24 = (f32[16,128]{1,0:T(8,128)S(1)}, f32[16,128]{1,0:T(8,128)S(1)}, u32[]{:S(2)}, u32[]{:S(2)}) collective-permute-start(f32[16,128]{1,0:T(8,128)S(1)} %concatenate.9), channel_id=1, source_target_pairs={{0,16},{4,20},{8,24},{12,28},{16,0},{20,4},{24,8},{28,12},{1,17},{... | collective-permute-start | bytes 24584 | tf_op jit(solution)/shard_map/ppermute | solution.py:666
  52.0 29.5 %collective-permute-start.3 = (bf16[128,1536]{1,0:T(8,128)(2,1)}, bf16[128,1536]{1,0:T(8,128)(2,1)S(1)}, u32[]{:S(2)}, u32[]{:S(2)}) collective-permute-start(bf16[128,1536]{1,0:T(8,128)(2,1)} %collective-permute-done.2.refs_1_), channel_id=1, source_target_pairs={{0,16},{4,20},{8,24},{12,28},{16,0},{20,4},{24,8},{28,12},{1,17},{... | collective-permute-start | bytes 1179656 | tf_op jit(solution)/shard_map/ppermute | solution.py:666
  73.1 12.0 %collective-permute-start.40 = (bf16[128,1536]{1,0:T(8,128)(2,1)S(1)}, bf16[128,1536]{1,0:T(8,128)(2,1)S(1)}, u32[]{:S(2)}, u32[]{:S(2)}) collective-permute-start(bf16[128,1536]{1,0:T(8,128)(2,1)S(1)} %get-tuple-element.48), channel_id=1, source_target_pairs={{0,8},{4,12},{8,0},{12,4},{16,24},{20,28},{24,16},{28,20},{1,9},{5... | collective-permute-start | bytes 1179656 | tf_op jit(solution)/shard_map/ppermute | solution.py:666
  74.6 15.4 %collective-permute-start.42 = (bf16[128,1536]{1,0:T(8,128)(2,1)S(1)}, bf16[128,1536]{1,0:T(8,128)(2,1)S(1)}, u32[]{:S(2)}, u32[]{:S(2)}) collective-permute-start(bf16[128,1536]{1,0:T(8,128)(2,1)S(1)} %get-tuple-element.50), channel_id=1, source_target_pairs={{0,16},{4,20},{8,24},{12,28},{16,0},{20,4},{24,8},{28,12},{1,17},{... | collective-permute-start | bytes 1179656 | tf_op jit(solution)/shard_map/ppermute | solution.py:666
  76.2 30.0 %collective-permute-start.41 = (bf16[128,2304]{1,0:T(8,128)(2,1)S(1)}, bf16[128,2304]{1,0:T(8,128)(2,1)S(1)}, u32[]{:S(2)}, u32[]{:S(2)}) collective-permute-start(bf16[128,2304]{1,0:T(8,128)(2,1)S(1)} %get-tuple-element.49), channel_id=1, source_target_pairs={{0,8},{4,12},{8,0},{12,4},{16,24},{20,28},{24,16},{28,20},{1,9},{5... | collective-permute-start | bytes 1769480 | tf_op jit(solution)/shard_map/ppermute | solution.py:666
  76.7 29.5 %collective-permute-start.43 = (bf16[128,2304]{1,0:T(8,128)(2,1)S(1)}, bf16[128,2304]{1,0:T(8,128)(2,1)S(1)}, u32[]{:S(2)}, u32[]{:S(2)}) collective-permute-start(bf16[128,2304]{1,0:T(8,128)(2,1)S(1)} %get-tuple-element.51), channel_id=1, source_target_pairs={{0,16},{4,20},{8,24},{12,28},{16,0},{20,4},{24,8},{28,12},{1,17},{... | collective-permute-start | bytes 1769480 | tf_op jit(solution)/shard_map/ppermute | solution.py:666
  81.6 24.6 %collective-permute-start.5 = (bf16[128,1536]{1,0:T(8,128)(2,1)}, bf16[128,1536]{1,0:T(8,128)(2,1)S(1)}, u32[]{:S(2)}, u32[]{:S(2)}) collective-permute-start(bf16[128,1536]{1,0:T(8,128)(2,1)} %collective-permute-done.4.refs_3_), channel_id=1, source_target_pairs={{0,8},{4,12},{8,0},{12,4},{16,24},{20,28},{24,16},{28,20},{1,9},{5... | collective-permute-start | bytes 1179656 | tf_op jit(solution)/shard_map/ppermute | solution.py:666
  85.1 24.6 %collective-permute-start.44 = (bf16[128,1536]{1,0:T(8,128)(2,1)S(1)}, bf16[128,1536]{1,0:T(8,128)(2,1)S(1)}, u32[]{:S(2)}, u32[]{:S(2)}) collective-permute-start(bf16[128,1536]{1,0:T(8,128)(2,1)S(1)} %collective-permute-done.40.refs_8_), channel_id=1, source_target_pairs={{0,16},{4,20},{8,24},{12,28},{16,0},{20,4},{24,8},{28,12},{1,17},{... | collective-permute-start | bytes 1179656 | tf_op jit(solution)/shard_map/ppermute | solution.py:666
  90.0 21.2 %collective-permute-start.45 = (bf16[128,1536]{1,0:T(8,128)(2,1)S(1)}, bf16[128,1536]{1,0:T(8,128)(2,1)S(1)}, u32[]{:S(2)}, u32[]{:S(2)}) collective-permute-start(bf16[128,1536]{1,0:T(8,128)(2,1)S(1)} %collective-permute-done.42.refs_10_), channel_id=1, source_target_pairs={{0,8},{4,12},{8,0},{12,4},{16,24},{20,28},{24,16},{28,20},{1,9},{5... | collective-permute-start | bytes 1179656 | tf_op jit(solution)/shard_map/ppermute | solution.py:666
  119.1 108.4 %collective-permute-start.46 = (f32[768,1536]{1,0:T(8,128)S(1)}, f32[768,1536]{1,0:T(8,128)S(1)}, u32[]{:S(2)}, u32[]{:S(2)}) collective-permute-start(f32[768,1536]{1,0:T(8,128)S(1)} %get-tuple-element.53), channel_id=1, source_target_pairs={{0,4},{4,0},{8,12},{12,8},{16,20},{20,16},{24,28},{28,24},{1,5},{5... | collective-permute-start | bytes 14155784 | tf_op jit(solution)/shard_map/ppermute | solution.py:666
  119.2 65.2 %collective-permute-start.26 = (bf16[128,6144]{1,0:T(8,128)(2,1)S(1)}, bf16[128,6144]{1,0:T(8,128)(2,1)S(1)}, u32[]{:S(2)}, u32[]{:S(2)}) collective-permute-start(bf16[128,6144]{1,0:T(8,128)(2,1)S(1)} %collective-permute-done.25.refs_0_), channel_id=1, source_target_pairs={{0,1},{1,2},{2,3},{3,0},{4,5},{5,6},{6,7},{7,4},{8,9},{9,10},{10,1... | collective-permute-start | bytes 4718600 | tf_op jit(solution)/shard_map/ppermute | solution.py:663
  121.2 44.9 %collective-permute-start.7 = (bf16[128,1536]{1,0:T(8,128)(2,1)S(1)}, bf16[128,1536]{1,0:T(8,128)(2,1)S(1)}, u32[]{:S(2)}, u32[]{:S(2)}) collective-permute-start(bf16[128,1536]{1,0:T(8,128)(2,1)S(1)} %copy-done.2), channel_id=1, source_target_pairs={{0,3},{1,0},{2,1},{3,2},{4,7},{5,4},{6,5},{7,6},{8,11},{9,8},{10,9... | collective-permute-start | bytes 1179656 | tf_op jit(solution)/shard_map/ppermute | solution.py:663
  166.1 10.9 %collective-permute-start.8 = (bf16[128,1536]{1,0:T(8,128)(2,1)S(1)}, bf16[128,1536]{1,0:T(8,128)(2,1)S(1)}, u32[]{:S(2)}, u32[]{:S(2)}) collective-permute-start(bf16[128,1536]{1,0:T(8,128)(2,1)S(1)} %collective-permute-done.7.refs_1_), channel_id=1, source_target_pairs={{0,8},{4,12},{8,0},{12,4},{16,24},{20,28},{24,16},{28,20},{1,9},{5... | collective-permute-start | bytes 1179656 | tf_op jit(solution)/shard_map/ppermute | solution.py:666
  167.5 10.6 %collective-permute-start.9 = (bf16[128,1536]{1,0:T(8,128)(2,1)S(1)}, bf16[128,1536]{1,0:T(8,128)(2,1)S(1)}, u32[]{:S(2)}, u32[]{:S(2)}) collective-permute-start(bf16[128,1536]{1,0:T(8,128)(2,1)S(1)} %collective-permute-done.7.refs_1_), channel_id=1, source_target_pairs={{0,16},{4,20},{8,24},{12,28},{16,0},{20,4},{24,8},{28,12},{1,17},{... | collective-permute-start | bytes 1179656 | tf_op jit(solution)/shard_map/ppermute | solution.py:666
  169.2 20.7 %collective-permute-start.12 = (bf16[512,768]{1,0:T(8,128)(2,1)S(1)}, bf16[512,768]{1,0:T(8,128)(2,1)S(1)}, u32[]{:S(2)}, u32[]{:S(2)}) collective-permute-start(bf16[512,768]{1,0:T(8,128)(2,1)S(1)} %get-tuple-element.39), channel_id=1, source_target_pairs={{0,3},{1,0},{2,1},{3,2},{4,7},{5,4},{6,5},{7,6},{8,11},{9,8},{10,9... | collective-permute-start | bytes 2359304 | tf_op jit(solution)/shard_map/ppermute | solution.py:663
  177.0 2.7 %collective-permute-start.14 = (bf16[128,1536]{1,0:T(8,128)(2,1)S(1)}, bf16[128,1536]{1,0:T(8,128)(2,1)S(1)}, u32[]{:S(2)}, u32[]{:S(2)}) collective-permute-start(bf16[128,1536]{1,0:T(8,128)(2,1)S(1)} %collective-permute-done.7.refs_1_), channel_id=1, source_target_pairs={{0,4},{4,0},{8,12},{12,8},{16,20},{20,16},{24,28},{28,24},{1,5},{5... | collective-permute-start | bytes 1179656 | tf_op jit(solution)/shard_map/ppermute | solution.py:666
  178.2 6.2 %collective-permute-start.10 = (bf16[128,768]{1,0:T(8,128)(2,1)S(1)}, bf16[128,768]{1,0:T(8,128)(2,1)S(1)}, u32[]{:S(2)}, u32[]{:S(2)}) collective-permute-start(bf16[128,768]{1,0:T(8,128)(2,1)S(1)} %slice.28), channel_id=1, source_target_pairs={{0,16},{4,20},{8,24},{12,28},{16,0},{20,4},{24,8},{28,12},{1,17},{... | collective-permute-start | bytes 589832 | tf_op jit(solution)/shard_map/ppermute | solution.py:666
  179.7 7.1 %collective-permute-start.11 = (bf16[128,768]{1,0:T(8,128)(2,1)S(1)}, bf16[128,768]{1,0:T(8,128)(2,1)S(1)}, u32[]{:S(2)}, u32[]{:S(2)}) collective-permute-start(bf16[128,768]{1,0:T(8,128)(2,1)S(1)} %slice.29), channel_id=1, source_target_pairs={{0,8},{4,12},{8,0},{12,4},{16,24},{20,28},{24,16},{28,20},{1,9},{5... | collective-permute-start | bytes 589832 | tf_op jit(solution)/shard_map/ppermute | solution.py:666
  184.4 4.0 %collective-permute-start.17 = (bf16[128,768]{1,0:T(8,128)(2,1)S(1)}, bf16[128,768]{1,0:T(8,128)(2,1)S(1)}, u32[]{:S(2)}, u32[]{:S(2)}) collective-permute-start(bf16[128,768]{1,0:T(8,128)(2,1)S(1)} %collective-permute-done.10.refs_4_), channel_id=1, source_target_pairs={{0,4},{4,0},{8,12},{12,8},{16,20},{20,16},{24,28},{28,24},{1,5},{5... | collective-permute-start | bytes 589832 | tf_op jit(solution)/shard_map/ppermute | solution.py:666
  184.4 6.1 %collective-permute-start.47 = (f32[8,768]{1,0:T(8,128)S(1)}, f32[8,768]{1,0:T(8,128)S(1)}, u32[]{:S(2)}, u32[]{:S(2)}) collective-permute-start(f32[8,768]{1,0:T(8,128)S(1)} %get-tuple-element.55), channel_id=1, source_target_pairs={{0,4},{4,0},{8,12},{12,8},{16,20},{20,16},{24,28},{28,24},{1,5},{5... | collective-permute-start | bytes 73736 | tf_op jit(solution)/shard_map/ppermute | solution.py:666
  186.9 26.7 %collective-permute-start.28 = (bf16[128,2304]{1,0:T(8,128)(2,1)S(1)}, bf16[128,2304]{1,0:T(8,128)(2,1)S(1)}, u32[]{:S(2)}, u32[]{:S(2)}) collective-permute-start(bf16[128,2304]{1,0:T(8,128)(2,1)S(1)} %get-tuple-element.44), channel_id=1, source_target_pairs={{0,8},{4,12},{8,0},{12,4},{16,24},{20,28},{24,16},{28,20},{1,9},{5... | collective-permute-start | bytes 1769480 | tf_op jit(solution)/shard_map/ppermute | solution.py:666
  188.4 25.2 %collective-permute-start.30 = (bf16[128,2304]{1,0:T(8,128)(2,1)S(1)}, bf16[128,2304]{1,0:T(8,128)(2,1)S(1)}, u32[]{:S(2)}, u32[]{:S(2)}) collective-permute-start(bf16[128,2304]{1,0:T(8,128)(2,1)S(1)} %get-tuple-element.46), channel_id=1, source_target_pairs={{0,16},{4,20},{8,24},{12,28},{16,0},{20,4},{24,8},{28,12},{1,17},{... | collective-permute-start | bytes 1769480 | tf_op jit(solution)/shard_map/ppermute | solution.py:666
  189.9 20.7 %collective-permute-start.27 = (bf16[128,1536]{1,0:T(8,128)(2,1)S(1)}, bf16[128,1536]{1,0:T(8,128)(2,1)S(1)}, u32[]{:S(2)}, u32[]{:S(2)}) collective-permute-start(bf16[128,1536]{1,0:T(8,128)(2,1)S(1)} %get-tuple-element.43), channel_id=1, source_target_pairs={{0,8},{4,12},{8,0},{12,4},{16,24},{20,28},{24,16},{28,20},{1,9},{5... | collective-permute-start | bytes 1179656 | tf_op jit(solution)/shard_map/ppermute | solution.py:666
  190.5 21.6 %collective-permute-start.29 = (bf16[128,1536]{1,0:T(8,128)(2,1)S(1)}, bf16[128,1536]{1,0:T(8,128)(2,1)S(1)}, u32[]{:S(2)}, u32[]{:S(2)}) collective-permute-start(bf16[128,1536]{1,0:T(8,128)(2,1)S(1)} %get-tuple-element.45), channel_id=1, source_target_pairs={{0,16},{4,20},{8,24},{12,28},{16,0},{20,4},{24,8},{28,12},{1,17},{... | collective-permute-start | bytes 1179656 | tf_op jit(solution)/shard_map/ppermute | solution.py:666
  210.6 10.2 %collective-permute-start.31 = (bf16[128,1536]{1,0:T(8,128)(2,1)S(1)}, bf16[128,1536]{1,0:T(8,128)(2,1)S(1)}, u32[]{:S(2)}, u32[]{:S(2)}) collective-permute-start(bf16[128,1536]{1,0:T(8,128)(2,1)S(1)} %collective-permute-done.27.refs_1_), channel_id=1, source_target_pairs={{0,16},{4,20},{8,24},{12,28},{16,0},{20,4},{24,8},{28,12},{1,17},{... | collective-permute-start | bytes 1179656 | tf_op jit(solution)/shard_map/ppermute | solution.py:666
  212.1 9.9 %collective-permute-start.32 = (bf16[128,1536]{1,0:T(8,128)(2,1)S(1)}, bf16[128,1536]{1,0:T(8,128)(2,1)S(1)}, u32[]{:S(2)}, u32[]{:S(2)}) collective-permute-start(bf16[128,1536]{1,0:T(8,128)(2,1)S(1)} %collective-permute-done.29.refs_3_), channel_id=1, source_target_pairs={{0,8},{4,12},{8,0},{12,4},{16,24},{20,28},{24,16},{28,20},{1,9},{5... | collective-permute-start | bytes 1179656 | tf_op jit(solution)/shard_map/ppermute | solution.py:666
  213.6 8.4 %collective-permute-start.34 = (bf16[128,1536]{1,0:T(8,128)(2,1)S(1)}, bf16[128,1536]{1,0:T(8,128)(2,1)S(1)}, u32[]{:S(2)}, u32[]{:S(2)}) collective-permute-start(bf16[128,1536]{1,0:T(8,128)(2,1)S(1)} %collective-permute-done.27.refs_1_), channel_id=1, source_target_pairs={{0,4},{4,0},{8,12},{12,8},{16,20},{20,16},{24,28},{28,24},{1,5},{5... | collective-permute-start | bytes 1179656 | tf_op jit(solution)/shard_map/ppermute | solution.py:666
  213.6 11.1 %collective-permute-start.33 = (bf16[128,3072]{1,0:T(8,128)(2,1)S(1)}, bf16[128,3072]{1,0:T(8,128)(2,1)S(1)}, u32[]{:S(2)}, u32[]{:S(2)}) collective-permute-start(bf16[128,3072]{1,0:T(8,128)(2,1)S(1)} %get-tuple-element.42.refs_0_), channel_id=1, source_target_pairs={{0,4},{4,0},{8,12},{12,8},{16,20},{20,16},{24,28},{28,24},{1,5},{5... | collective-permute-start | bytes 2359304 | tf_op jit(solution)/shard_map/ppermute | solution.py:666
  220.7 4.3 %collective-permute-start.35 = (bf16[128,2304]{1,0:T(8,128)(2,1)S(1)}, bf16[128,2304]{1,0:T(8,128)(2,1)S(1)}, u32[]{:S(2)}, u32[]{:S(2)}) collective-permute-start(bf16[128,2304]{1,0:T(8,128)(2,1)S(1)} %collective-permute-done.28.refs_2_), channel_id=1, source_target_pairs={{0,4},{4,0},{8,12},{12,8},{16,20},{20,16},{24,28},{28,24},{1,5},{5... | collective-permute-start | bytes 1769480 | tf_op jit(solution)/shard_map/ppermute | solution.py:666
  222.0 4.9 %collective-permute-start.37 = (bf16[128,2304]{1,0:T(8,128)(2,1)S(1)}, bf16[128,2304]{1,0:T(8,128)(2,1)S(1)}, u32[]{:S(2)}, u32[]{:S(2)}) collective-permute-start(bf16[128,2304]{1,0:T(8,128)(2,1)S(1)} %collective-permute-done.30.refs_4_), channel_id=1, source_target_pairs={{0,4},{4,0},{8,12},{12,8},{16,20},{20,16},{24,28},{28,24},{1,5},{5... | collective-permute-start | bytes 1769480 | tf_op jit(solution)/shard_map/ppermute | solution.py:666
  222.0 2.6 %collective-permute-start.36 = (bf16[128,1536]{1,0:T(8,128)(2,1)S(1)}, bf16[128,1536]{1,0:T(8,128)(2,1)S(1)}, u32[]{:S(2)}, u32[]{:S(2)}) collective-permute-start(bf16[128,1536]{1,0:T(8,128)(2,1)S(1)} %collective-permute-done.29.refs_3_), channel_id=1, source_target_pairs={{0,4},{4,0},{8,12},{12,8},{16,20},{20,16},{24,28},{28,24},{1,5},{5... | collective-permute-start | bytes 1179656 | tf_op jit(solution)/shard_map/ppermute | solution.py:666
  224.5 2.3 collective-permute-start.38
  224.7 2.7 %collective-permute-start.39 = (bf16[128,1536]{1,0:T(8,128)(2,1)S(1)}, bf16[128,1536]{1,0:T(8,128)(2,1)S(1)}, u32[]{:S(2)}, u32[]{:S(2)}) collective-permute-start(bf16[128,1536]{1,0:T(8,128)(2,1)S(1)} %collective-permute-done.32.refs_6_), channel_id=1, source_target_pairs={{0,4},{4,0},{8,12},{12,8},{16,20},{20,16},{24,28},{28,24},{1,5},{5... | collective-permute-start | bytes 1179656 | tf_op jit(solution)/shard_map/ppermute | solution.py:666
  225.0 19.6 %collective-permute-start.6 = (bf16[512,768]{1,0:T(8,128)(2,1)S(1)}, bf16[512,768]{1,0:T(8,128)(2,1)S(1)}, u32[]{:S(2)}, u32[]{:S(2)}) collective-permute-start(bf16[512,768]{1,0:T(8,128)(2,1)S(1)} %get-tuple-element.37), channel_id=1, source_target_pairs={{0,3},{1,0},{2,1},{3,2},{4,7},{5,4},{6,5},{7,6},{8,11},{9,8},{10,9... | collective-permute-start | bytes 2359304 | tf_op jit(solution)/shard_map/ppermute | solution.py:663
  226.8 17.8 %collective-permute-start.13 = (bf16[512,768]{1,0:T(8,128)(2,1)S(1)}, bf16[512,768]{1,0:T(8,128)(2,1)S(1)}, u32[]{:S(2)}, u32[]{:S(2)}) collective-permute-start(bf16[512,768]{1,0:T(8,128)(2,1)S(1)} %collective-permute-done.12), channel_id=1, source_target_pairs={{0,4},{4,0},{8,12},{12,8},{16,20},{20,16},{24,28},{28,24},{1,5},{5... | collective-permute-start | bytes 2359304 | tf_op jit(solution)/shard_map/ppermute | solution.py:666
  226.8 4.1 %collective-permute-start.15 = (bf16[128,1536]{1,0:T(8,128)(2,1)S(1)}, bf16[128,1536]{1,0:T(8,128)(2,1)S(1)}, u32[]{:S(2)}, u32[]{:S(2)}) collective-permute-start(bf16[128,1536]{1,0:T(8,128)(2,1)S(1)} %collective-permute-done.8.refs_2_), channel_id=1, source_target_pairs={{0,4},{4,0},{8,12},{12,8},{16,20},{20,16},{24,28},{28,24},{1,5},{5... | collective-permute-start | bytes 1179656 | tf_op jit(solution)/shard_map/ppermute | solution.py:666
  227.4 3.6 %collective-permute-start.16 = (bf16[128,1536]{1,0:T(8,128)(2,1)S(1)}, bf16[128,1536]{1,0:T(8,128)(2,1)S(1)}, u32[]{:S(2)}, u32[]{:S(2)}) collective-permute-start(bf16[128,1536]{1,0:T(8,128)(2,1)S(1)} %collective-permute-done.9.refs_3_), channel_id=1, source_target_pairs={{0,4},{4,0},{8,12},{12,8},{16,20},{20,16},{24,28},{28,24},{1,5},{5... | collective-permute-start | bytes 1179656 | tf_op jit(solution)/shard_map/ppermute | solution.py:666
  227.4 3.5 %collective-permute-start.18 = (bf16[128,768]{1,0:T(8,128)(2,1)S(1)}, bf16[128,768]{1,0:T(8,128)(2,1)S(1)}, u32[]{:S(2)}, u32[]{:S(2)}) collective-permute-start(bf16[128,768]{1,0:T(8,128)(2,1)S(1)} %collective-permute-done.11.refs_5_), channel_id=1, source_target_pairs={{0,4},{4,0},{8,12},{12,8},{16,20},{20,16},{24,28},{28,24},{1,5},{5... | collective-permute-start | bytes 589832 | tf_op jit(solution)/shard_map/ppermute | solution.py:666
  (15 other events, 91.7 us)

commit v2 on v1

--- a/solution.py
+++ b/solution.py
@@ -10,8 +10,6 @@
 ANY = pl.BlockSpec(memory_space=pl.ANY)
 VMEM = pl.BlockSpec(memory_space=pltpu.VMEM)
 SMEM = pl.BlockSpec(memory_space=pltpu.SMEM)
-HBM = pl.BlockSpec(memory_space=pltpu.HBM)
-SPLITS = 1
 
 
 def factor_math(n, arcs, len_ref, amp_ref, decay_ref, obs_ref, gap_ref, noise_ref):
@@ -432,7 +430,7 @@
     return pl.pallas_call(
         kernel,
         name="head",
-        in_specs=[SMEM] + [HBM] * 8,
+        in_specs=[SMEM] + [ANY] * 8,
         out_specs=[VMEM] * 7,
         out_shape=[jax.ShapeDtypeStruct((h, w), t) for h, w, t in outs],
         scratch_shapes=[
@@ -452,29 +450,22 @@
     )(where, design, *[v.reshape(1, -1) for v in small], *tables, tile_map.reshape(1, -1))
 
 
-def pack_cut(chunks, near, tile_map, where, rows_axis, cols_axis, begin):
-    height, columns = chunks[-1].shape
+def pack_cut(chunk, near, tile_map, where, rows_axis, cols_axis):
+    block_rows, columns = chunk.shape
     tiles = tile_map.shape[0]
     size = columns // tiles
     per_row, per_col = tiles // rows_axis, tiles // cols_axis
     own, cols_width = per_row * size, per_col * size
-    depth = begin + height
-
-    def kernel(map_ref, where_ref, near_ref, *refs):
-        raw = refs[: len(chunks)]
-        outs = refs[len(chunks) : -1]
-        held = refs[-1]
+
+    def kernel(map_ref, where_ref, near_ref, x_ref, *refs):
+        outs, held = refs[:-1], refs[-1]
         row, col = where_ref[0], where_ref[1]
-        weight = near_ref[begin:depth, :depth]
+        weight = near_ref[:block_rows, :]
 
         def fetch(base, count):
             for j in range(count):
                 at = pl.multiple_of(map_ref[base + j] * size, size)
-                top = 0
-                for piece in raw:
-                    end = top + piece.shape[0]
-                    held[top:end, j * size : (j + 1) * size] = piece[:, pl.ds(at, size)]
-                    top = end
+                held[:, j * size : (j + 1) * size] = x_ref[:, pl.ds(at, size)]
             return split_dot(weight, held[:, : count * size])
 
         cut_columns((per_row, per_col, own, cols_width // 2, col * per_col), fetch, row, outs)
@@ -482,13 +473,15 @@
     return pl.pallas_call(
         kernel,
         name="pack_cut",
-        in_specs=[SMEM, SMEM, VMEM] + [VMEM] * len(chunks),
+        in_specs=[SMEM, SMEM, VMEM, VMEM],
         out_specs=[VMEM] * 5,
-        out_shape=[jax.ShapeDtypeStruct((height, w), BF16) for w in cut_widths(own, cols_width)],
-        scratch_shapes=[pltpu.VMEM((depth, max(own, cols_width)), BF16)],
+        out_shape=[
+            jax.ShapeDtypeStruct((block_rows, w), BF16) for w in cut_widths(own, cols_width)
+        ],
+        scratch_shapes=[pltpu.VMEM((block_rows, max(own, cols_width)), BF16)],
         cost_estimate=pl.CostEstimate(flops=10**9, bytes_accessed=5 * 10**6, transcendentals=0),
         compiler_params=pltpu.CompilerParams(vmem_limit_bytes=8 << 20),
-    )(tile_map, where, near, *chunks)
+    )(tile_map, where, near, chunk)
 
 
 def row_parts(keep, xb, yb, fa, fb, own):
@@ -496,17 +489,17 @@
 
     def kernel(keep_ref, xb_ref, yb_ref, fa_ref, fb_ref, lead_ref, rest_ref):
         for n, ref in enumerate((keep_ref, xb_ref, yb_ref)):
-            lead_ref[n * block_rows : (n + 1) * block_rows, :] = ref[:, :own]
-            rest_ref[n * block_rows : (n + 1) * block_rows, :] = ref[:, own : 2 * own]
-        lead_ref[3 * block_rows :, :] = fa_ref[:, :own]
-        rest_ref[3 * block_rows :, :] = fb_ref[:, :own]
+            lead_ref[:, n * block_rows : (n + 1) * block_rows] = ref[:, :own].T
+            rest_ref[:, n * block_rows : (n + 1) * block_rows] = ref[:, own : 2 * own].T
+        lead_ref[:, 3 * block_rows :] = fa_ref[:, :own].T
+        rest_ref[:, 3 * block_rows :] = fb_ref[:, :own].T
 
     return pl.pallas_call(
         kernel,
         name="row_parts",
         in_specs=[VMEM] * 5,
         out_specs=[VMEM] * 2,
-        out_shape=[jax.ShapeDtypeStruct((4 * block_rows, own), BF16)] * 2,
+        out_shape=[jax.ShapeDtypeStruct((own, 4 * block_rows), BF16)] * 2,
         cost_estimate=pl.CostEstimate(flops=10**9, bytes_accessed=5 * 10**6, transcendentals=0),
         compiler_params=pltpu.CompilerParams(vmem_limit_bytes=4 << 20),
     )(keep, xb, yb, fa, fb)
@@ -522,11 +515,12 @@
             held[at : at + source.shape[0], :] = source[...]
             at += source.shape[0]
         at = 0
-        for m, s, (begin, end) in places:
+        for m, s in places:
             line = m * cols_axis + s
-            wide = jnp.broadcast_to(held[line : line + 1, :], (8, block_rows))
-            rows_ref[:, at : at + end - begin] = wide[:, begin:end]
-            at += end - begin
+            rows_ref[:, at : at + block_rows] = jnp.broadcast_to(
+                held[line : line + 1, :], (8, block_rows)
+            )
+            at += block_rows
         from_row = lax.div(plan_ref[0], cols_axis)
         from_col = lax.rem(plan_ref[0], cols_axis)
         mask = jnp.bitwise_xor(from_row, where_ref[0])
@@ -539,7 +533,7 @@
         in_specs=[SMEM, SMEM] + [VMEM] * len(obs),
         out_specs=[VMEM] * 2,
         out_shape=[
-            jax.ShapeDtypeStruct((8, sum(end - begin for _, _, (begin, end) in places)), F32),
+            jax.ShapeDtypeStruct((8, len(places) * block_rows), F32),
             jax.ShapeDtypeStruct((1, block_rows), F32),
         ],
         scratch_shapes=[pltpu.VMEM((sum(v.shape[0] for v in obs), block_rows), F32)],
@@ -548,12 +542,15 @@
     )(plan, where, *obs)
 
 
-def gram_direct(blocks, operands, rows, at_row, left_width, cols_width, before, halves, out_far):
+def gram_direct(
+    blocks, ready, operands, rows, at_row, left_width, cols_width, before, halves, out_far
+):
     count = len(operands)
     width = left_width // halves
     step = cols_width // 6 if cols_width % 6 == 0 and (cols_width // 6) % 128 == 0 else 128
     steps = cols_width // step
     depth = sum(block[0] for block in blocks)
+    total_depth = depth + sum(part[0] for _, group in ready for part in group)
 
     def kernel(*refs):
         sources = refs[:count]
@@ -578,6 +575,13 @@
             )
             total = total + jnp.dot(seen, left, preferred_element_type=F32)
             top += height
+        for which, group in ready:
+            height = sum(part[0] for part in group)
+            seen = rows_ref[:, at_row + top : at_row + top + height].astype(BF16)
+            total = total + lax.dot_general(
+                seen, sources[which][...], (((1,), (1,)), ((), ())), preferred_element_type=F32
+            )
+            top += height
         half_sums = len(before) // 2
         for h in range(halves):
             part = total[:, h * width : (h + 1) * width]
@@ -587,17 +591,26 @@
         copies = [None, None]
         for t in range(steps):
             begin = t * step
-            pieces = []
-            for height, _, cols in blocks:
-                for which, first, start, length, to in cols:
-                    if to <= begin < to + length:
-                        at = start + begin - to
-                        pieces.append(sources[which][first : first + height, at : at + step])
-            right = jnp.concatenate(pieces, axis=0)
+
+            def cut(group):
+                pieces = []
+                for height, cols in group:
+                    for which, first, start, length, to in cols:
+                        if to <= begin < to + length:
+                            at = start + begin - to
+                            pieces.append(sources[which][first : first + height, at : at + step])
+                return jnp.concatenate(pieces, axis=0)
+
+            right = cut([(height, cols) for height, _, cols in blocks])
+            rights = [(which, cut(group)) for which, group in ready]
             for h in range(halves):
                 part = jnp.dot(
                     turned[h * width : (h + 1) * width, :], right, preferred_element_type=F32
                 )
+                for which, other in rights:
+                    part = part + jnp.dot(
+                        sources[which][...], other, preferred_element_type=F32
+                    )
                 for extra in sums[:half_sums]:
                     part = part + extra[:, begin : begin + step]
                 if not out_far:
@@ -629,7 +642,9 @@
         + [jax.ShapeDtypeStruct((8, width), F32)] * halves,
         scratch_shapes=scratch_shapes,
         cost_estimate=pl.CostEstimate(
-            flops=2 * depth * left_width * cols_width, bytes_accessed=2 * 10**7, transcendentals=0
+            flops=2 * total_depth * left_width * cols_width,
+            bytes_accessed=2 * 10**7,
+            transcendentals=0,
         ),
         compiler_params=pltpu.CompilerParams(vmem_limit_bytes=scratch_bytes + (4 << 20)),
     )(*operands, rows, *before)
@@ -665,11 +680,9 @@
     def swap(x, mask):
         return lax.ppermute(x, "row", [(r, r ^ mask) for r in range(rows_axis)])
 
-    cuts = [(k * block_rows // SPLITS, (k + 1) * block_rows // SPLITS) for k in range(SPLITS)]
     chunks = [design]
-    for _ in range(1, last - 1):
+    for _ in range(1, last):
         chunks.append(ring(chunks[-1], 1))
-    pieces = [ring(chunks[-1][a:b], 1) for a, b in cuts]
     near, *parts = head(
         design,
         (observations, gaps, noise_var),
@@ -681,11 +694,7 @@
     )
     line = [near] + [ring(near, s) for s in range(1, cols_axis)]
     line_obs = jnp.stack([part[block_rows] for part in line])
-    obs = [line_obs]
-    mask = 1
-    while mask < rows_axis:
-        obs.append(swap(jnp.concatenate(obs, axis=0), mask))
-        mask *= 2
+    obs = [line_obs] + [swap(line_obs, m) for m in range(1, rows_axis)]
 
     def trade(xa, xb, ya, yb, keep):
         xa, ya = swap(xa, 2), swap(ya, 4)
@@ -693,13 +702,8 @@
         return keep, xa, xb, ya, yb, swap(xa, 4), swap(ya, 2)
 
     traded = [trade(*parts[:5])]
-    for s in range(1, last - 1):
-        cut = pack_cut([chunks[s]], line[s], tile_map, where, rows_axis, cols_axis, 0)
-        traded.append(trade(*cut))
-    for k, (begin, _) in enumerate(cuts):
-        cut = pack_cut(
-            pieces[: k + 1], line[last - 1], tile_map, where, rows_axis, cols_axis, begin
-        )
+    for s in range(1, last):
+        cut = pack_cut(chunks[s], line[s], tile_map, where, rows_axis, cols_axis)
         traded.append(trade(*cut))
 
     keep, _, xb, _, yb, fa, fb = traded[0]
@@ -733,18 +737,10 @@
             blocks[n][2].append((first + k, 0, begin, length, to))
         return blocks
 
-    def seen(count, core, s, rows):
-        return [(2 * n + core, s, rows) for n in range(count)]
-
-    whole = (0, block_rows)
-    early, mid, late = [], [], []
-    for s in range(last - 1):
-        early += seen(4, 0, s, whole)
-    for rows in cuts:
-        for core in (0, 1):
-            mid += seen(4, core, last - 1, rows)
-    for core in (0, 1):
-        late += seen(4, core, last, whole)
+    early = [(2 * n, s) for s in range(last - 1) for n in range(4)]
+    mid = [(2 * n + core, last - 1) for core in (0, 1) for n in range(3)]
+    late = [(6 + core, last - 1) for core in (0, 1)]
+    late += [(2 * n + core, last) for core in (0, 1) for n in range(4)]
     rows, balanced_obs = obs_rows(obs, early + mid + late, plan, where, cols_axis)
 
     blocks, operands = [], []
@@ -752,23 +748,19 @@
         blocks += part_blocks(len(operands), block_rows, 0, True)
         operands += list(traded[s])
     keep, give, keep_rhs, give_rhs = gram_direct(
-        blocks, operands, rows, 0, wide, cols_width, (), 2, False
+        blocks, [], operands, rows, 0, wide, cols_width, (), 2, False
     )
     other = swap(give, 1)
     other_rhs = swap(give_rhs, 1)
 
-    at_row = 4 * (last - 1) * block_rows
-    blocks, operands = [], []
-    for k in range(last - 1, len(traded)):
-        mine = list(traded[k])
-        height = block_rows // SPLITS
-        theirs = [swap(v, 1) for v in mine]
-        blocks += part_blocks(len(operands), height, 0, False)
-        blocks += part_blocks(len(operands) + 7, height, 1, False)
-        operands += mine + theirs
+    mine = list(traded[last - 1])
+    theirs = [swap(v, 1) for v in mine]
+    sides = [part_blocks(0, block_rows, 0, False), part_blocks(5, block_rows, 1, False)]
+    at_row = len(early) * block_rows
     most, most_rhs = gram_direct(
-        blocks,
-        operands,
+        sides[0][:3] + sides[1][:3],
+        [],
+        mine[:5] + theirs[:5],
         rows,
         at_row,
         own,
@@ -777,21 +769,24 @@
         1,
         False,
     )
-    at_row += 8 * block_rows
-    mine = [far_cols, x3, y3, fa3, fb3]
-    theirs = [swap(v, 1) for v in mine]
+    at_row += len(mid) * block_rows
+    mine_far = [far_cols, x3, y3, fa3, fb3]
+    theirs_far = [swap(v, 1) for v in mine_far]
     their_rest = swap(far_rest, 1)
-    blocks, operands = [], []
-    for left, group in ((far_lead, mine), (their_rest, theirs)):
+    corners, ready = [], []
+    operands = []
+    for core, group in enumerate((mine, theirs)):
+        cols = [(len(operands), 0, own, half, 0), (len(operands) + 1, 0, own, half, half)]
+        corners.append((block_rows, [(len(operands) + core, 0, 0, own, 0)], cols))
+        operands += group[5:]
+    for left, group in ((far_lead, mine_far), (their_rest, theirs_far)):
         first = len(operands)
         operands += [left] + group
-        for n in range(4):
-            cols = [(first + 1 + n, 0, 0, cols_width, 0)]
-            if n == 3:
-                cols = [(first + 4, 0, 0, half, 0), (first + 5, 0, 0, half, half)]
-            blocks.append((block_rows, [(first, n * block_rows, 0, own, 0)], cols))
+        plain = [(block_rows, [(first + 1 + n, 0, 0, cols_width, 0)]) for n in range(3)]
+        plain.append((block_rows, [(first + 4, 0, 0, half, 0), (first + 5, 0, 0, half, half)]))
+        ready.append((first, plain))
     gram, rhs = gram_direct(
-        blocks, operands, rows, at_row, own, cols_width, (most, most_rhs), 1, True
+        corners, ready, operands, rows, at_row, own, cols_width, (most, most_rhs), 1, True
     )
     return (gram, rhs[0], balanced_obs)
 

time: 252 us -> 252 us (level)
  waiting for transfers between devices: 164 us -> 172 us
  local copies, waits for them, and re-layouts: 10.8 us -> 6.63 us
  starting transfers between devices: 49.3 us -> 46.6 us
    ppermute x8, waiting for transfers between devices: 78.1 us -> 85.7 us  [ring(): lax.ppermute(x, 'col', [(c, (c + shift) % cols_axis) for c in range(cols_...]
    unnamed x30 -> x18, local copies, waits for them, and re-layouts: 10.2 us -> 5.99 us
    ppermute x40 -> x44, starting transfers between devices: 32.7 us -> 30.5 us  [swap(): return lax.ppermute(x, 'row', [(r, r ^ mask) for r in range(rows_axis)])]
    ppermute x40 -> x44, waiting for transfers between devices: 86.2 us -> 86.6 us  [swap(): return lax.ppermute(x, 'row', [(r, r ^ mask) for r in range(rows_axis)])]
  transfers between devices with their start and end apart: 48 -> 52, of which waited for: 20 -> 23; matrix products, arithmetic and copies ran while one was open for 0% -> 0% of each run, Pallas kernels for 5% -> 5%
where the time goes in v2:
time: 252 us; the launch traced here: 251 us
  waiting for transfers between devices  172 us (68%)
  starting transfers between devices  46.6 us (18%)
  Pallas kernels  24.2 us (10%)
  local copies, waits for them, and re-layouts  6.63 us (3%)
    ppermute x44, waiting for transfers between devices, swap(): return lax.ppermute(x, 'row', [(r, r ^ mask) for r in range(rows_axis)])  86.6 us
    ppermute x8, waiting for transfers between devices, ring(): lax.ppermute(x, 'col', [(c, (c + shift) % cols_axis) for c in range(cols_...  85.7 us
    ppermute x44, starting transfers between devices, swap(): return lax.ppermute(x, 'row', [(r, r ^ mask) for r in range(rows_axis)])  30.5 us
    ppermute x8, starting transfers between devices, ring(): lax.ppermute(x, 'col', [(c, (c + shift) % cols_axis) for c in range(cols_...  16.1 us
    pallas_call x3, Pallas kernels, gram_direct(): pl.pallas_call(kernel, in_specs=[VMEM] * (count + 1 + len(before)), out_s...  15.1 us
    unnamed x18, local copies, waits for them, and re-layouts  5.99 us
  transfers between devices with their start and end apart: 52, of which 23 were waited for; matrix products, arithmetic and copies ran while one was open for 0% of the time, Pallas kernels for 5%

profile of v2, /device:TPU:0, one launch (start us, length us, event | category | flops | bytes accessed | tf_op | source)
XLA Modules:
  0.0 251.3 jit_solution(12253224158564357541)
XLA Ops:
  0.6 3.1 %collective-permute-start.1 = (bf16[128,6144]{1,0:T(8,128)(2,1)}, bf16[128,6144]{1,0:T(8,128)(2,1)S(1)}, u32[]{:S(2)}, u32[]{:S(2)}) collective-permute-start(bf16[128,6144]{1,0:T(8,128)(2,1)} %refs_0_.1), channel_id=1, source_target_pairs={{0,1},{1,2},{2,3},{3,0},{4,5},{5,6},{6,7},{7,4},{8,9},{9,10},{10,1... | collective-permute-start | bytes 4718600 | tf_op jit(solution)/shard_map/ppermute | solution.py:678
  3.8 1.4 copy-done
  9.8 3.8 %head.1 = (f32[136,128]{1,0:T(8,128)S(1)}, bf16[128,1536]{1,0:T(8,128)(2,1)S(1)}, bf16[128,2304]{1,0:T(8,128)(2,1)S(1)}, bf16[128,1536]{1,0:T(8,128)(2,1)S(1)}, ...) custom-call(s32[2]{0:T(128)S(1)} %pad_add_fusion.where_ref, ...), custom_call_target="tpu_custom_call" | custom-call | flops 1000000000 | bytes 5000000 | tf_op jit(solution)/shard_map/head/pallas_call | solution.py:430
  13.6 1.6 collective-permute-start.28
  16.3 2.8 %collective-permute-start.29 = (f32[136,128]{1,0:T(8,128)S(1)}, f32[136,128]{1,0:T(8,128)S(1)}, u32[]{:S(2)}, u32[]{:S(2)}) collective-permute-start(f32[136,128]{1,0:T(8,128)S(1)} %get-tuple-element.32), channel_id=1, source_target_pairs={{0,3},{1,0},{2,1},{3,2},{4,7},{5,4},{6,5},{7,6},{8,11},{9,8},{10,9... | collective-permute-start | bytes 208904 | tf_op jit(solution)/shard_map/ppermute | solution.py:678
  19.1 23.7 %collective-permute-done.28.near_ref = f32[136,128]{1,0:T(8,128)S(1)} collective-permute-done((f32[136,128]{1,0:T(8,128)S(1)}, f32[136,128]{1,0:T(8,128)S(1)}, u32[]{:S(2)}, u32[]{:S(2)}) %collective-permute-start.28) | collective-permute-done | bytes 69664 | tf_op jit(solution)/shard_map/ppermute | solution.py:678
  42.8 2.2 collective-permute-done.near_ref
  45.1 1.6 collective-permute-start.31
  46.9 1.5 collective-permute-start.33
  48.7 2.4 collective-permute-start.35
  52.2 1.5 collective-permute-start.9
  53.7 1.5 collective-permute-start.13
  55.3 1.9 pack_cut.3
  57.2 6.0 %collective-permute-done.11.refs_1_ = bf16[128,1536]{1,0:T(8,128)(2,1)S(1)} collective-permute-done((bf16[128,1536]{1,0:T(8,128)(2,1)S(1)}, bf16[128,1536]{1,0:T(8,128)(2,1)S(1)}, u32[]{:S(2)}, u32[]{:S(2)}) %collective-permute-start.11) | collective-permute-done | bytes 393248 | tf_op jit(solution)/shard_map/ppermute | solution.py:681
  63.7 10.3 %collective-permute-done.36.refs_7_ = f32[4,128]{1,0:T(4,128)S(1)} collective-permute-done((f32[4,128]{1,0:T(4,128)S(1)}, f32[4,128]{1,0:T(4,128)S(1)}, u32[]{:S(2)}, u32[]{:S(2)}) %collective-permute-start.36) | collective-permute-done | bytes 2080 | tf_op jit(solution)/shard_map/ppermute | solution.py:681
  74.6 1.8 collective-permute-done.13.refs_3_
  76.9 1.5 collective-permute-start.45
  78.4 1.5 collective-permute-start.47
  79.9 4.9 %collective-permute-done.12.fa_ref.refs_5_ = bf16[128,1536]{1,0:T(8,128)(2,1)S(1)} collective-permute-done((bf16[128,1536]{1,0:T(8,128)(2,1)S(1)}, bf16[128,1536]{1,0:T(8,128)(2,1)S(1)}, u32[]{:S(2)}, u32[]{:S(2)}) %collective-permute-start.12) | collective-permute-done | bytes 393248 | tf_op jit(solution)/shard_map/ppermute | solution.py:681
  84.8 1.5 collective-permute-start.14
  87.5 5.7 %collective-permute-done.46.refs_10_ = bf16[128,1536]{1,0:T(8,128)(2,1)S(1)} collective-permute-done((bf16[128,1536]{1,0:T(8,128)(2,1)S(1)}, bf16[128,1536]{1,0:T(8,128)(2,1)S(1)}, u32[]{:S(2)}, u32[]{:S(2)}) %collective-permute-start.46) | collective-permute-done | bytes 393248 | tf_op jit(solution)/shard_map/ppermute | solution.py:681
  93.2 1.5 collective-permute-start.49
  96.5 10.6 %collective-permute-done.14.fb_ref.refs_6_ = bf16[128,1536]{1,0:T(8,128)(2,1)S(1)} collective-permute-done((bf16[128,1536]{1,0:T(8,128)(2,1)S(1)}, bf16[128,1536]{1,0:T(8,128)(2,1)S(1)}, u32[]{:S(2)}, u32[]{:S(2)}) %collective-permute-start.14) | collective-permute-done | bytes 393248 | tf_op jit(solution)/shard_map/ppermute | solution.py:681
  107.1 6.1 %collective-permute-done.48.refs_12_ = bf16[128,1536]{1,0:T(8,128)(2,1)S(1)} collective-permute-done((bf16[128,1536]{1,0:T(8,128)(2,1)S(1)}, bf16[128,1536]{1,0:T(8,128)(2,1)S(1)}, u32[]{:S(2)}, u32[]{:S(2)}) %collective-permute-start.48) | collective-permute-done | bytes 393248 | tf_op jit(solution)/shard_map/ppermute | solution.py:681
  113.1 2.2 collective-permute-done.49.refs_13_
  115.3 5.6 %shard_map.112 = (f32[768,1536]{1,0:T(8,128)S(1)}, f32[768,1536]{1,0:T(8,128)S(1)}, f32[8,768]{1,0:T(8,128)S(1)}, f32[8,768]{1,0:T(8,128)S(1)}) custom-call(bf16[128,3072]{1,0:T(8,128)(2,1)S(1)} %get-tuple-element.35.keep_ref.refs_0_, bf16[128,1536]{1,0:T(8,128)(2,1)S(1)} %collective-permute-done.11.refs_1_, ...), custom_call_target="tpu_custom_call" | custom-call | flops 4831838208 | bytes 20000000 | tf_op jit(solution)/shard_map/pallas_call | solution.py:637
  121.0 2.0 collective-permute-start.2
  123.0 1.9 collective-permute-start.16
  124.9 43.0 %collective-permute-done.16.refs_5_ = bf16[128,1536]{1,0:T(8,128)(2,1)S(1)} collective-permute-done((bf16[128,1536]{1,0:T(8,128)(2,1)S(1)}, bf16[128,1536]{1,0:T(8,128)(2,1)S(1)}, u32[]{:S(2)}, u32[]{:S(2)}) %collective-permute-start.16) | collective-permute-done | bytes 393248 | tf_op jit(solution)/shard_map/ppermute | solution.py:678
  168.5 1.5 collective-permute-start.18
  170.4 8.4 %collective-permute-done.17.refs_6_ = bf16[128,1536]{1,0:T(8,128)(2,1)S(1)} collective-permute-done((bf16[128,1536]{1,0:T(8,128)(2,1)S(1)}, bf16[128,1536]{1,0:T(8,128)(2,1)S(1)}, u32[]{:S(2)}, u32[]{:S(2)}) %collective-permute-start.17) | collective-permute-done | bytes 393248 | tf_op jit(solution)/shard_map/ppermute | solution.py:681
  178.8 1.8 collective-permute-start.21
  180.6 1.6 collective-permute-start.19
  182.9 3.5 %collective-permute-done.19.refs_8_ = bf16[128,768]{1,0:T(8,128)(2,1)S(1)} collective-permute-done((bf16[128,768]{1,0:T(8,128)(2,1)S(1)}, bf16[128,768]{1,0:T(8,128)(2,1)S(1)}, u32[]{:S(2)}, u32[]{:S(2)}) %collective-permute-start.19) | collective-permute-done | bytes 196640 | tf_op jit(solution)/shard_map/ppermute | solution.py:681
  186.4 1.6 collective-permute-done.20.refs_9_
  188.5 1.9 pack_cut.2
  191.1 1.5 collective-permute-start.37
  193.0 4.3 %collective-permute-done.21 = bf16[768,512]{1,0:T(8,128)(2,1)S(1)} collective-permute-done((bf16[768,512]{1,0:T(8,128)(2,1)S(1)}, bf16[768,512]{1,0:T(8,128)(2,1)S(1)}, u32[]{:S(2)}, u32[]{:S(2)}) %collective-permute-start.21) | collective-permute-done | bytes 786464 | tf_op jit(solution)/shard_map/ppermute | solution.py:678
  198.5 1.5 collective-permute-start.38
  200.0 2.5 collective-permute-done.3.refs_1_
  202.5 2.0 collective-permute-done.5.refs_3_
  204.5 9.7 %collective-permute-done.37.refs_2_ = bf16[128,2304]{1,0:T(8,128)(2,1)S(1)} collective-permute-done((bf16[128,2304]{1,0:T(8,128)(2,1)S(1)}, bf16[128,2304]{1,0:T(8,128)(2,1)S(1)}, u32[]{:S(2)}, u32[]{:S(2)}) %collective-permute-start.37) | collective-permute-done | bytes 589856 | tf_op jit(solution)/shard_map/ppermute | solution.py:681
  214.2 1.5 collective-permute-done.38.refs_4_
  217.2 8.5 %collective-permute-done.4.refs_0_ = bf16[128,1536]{1,0:T(8,128)(2,1)S(1)} collective-permute-done((bf16[128,1536]{1,0:T(8,128)(2,1)S(1)}, bf16[128,1536]{1,0:T(8,128)(2,1)S(1)}, u32[]{:S(2)}, u32[]{:S(2)}) %collective-permute-start.4) | collective-permute-done | bytes 393248 | tf_op jit(solution)/shard_map/ppermute | solution.py:681
  225.7 1.8 collective-permute-start.15
  228.5 2.2 shard_map.113
  230.8 12.6 %collective-permute-done.15.refs_4_ = bf16[768,512]{1,0:T(8,128)(2,1)S(1)} collective-permute-done((bf16[768,512]{1,0:T(8,128)(2,1)S(1)}, bf16[768,512]{1,0:T(8,128)(2,1)S(1)}, u32[]{:S(2)}, u32[]{:S(2)}) %collective-permute-start.15) | collective-permute-done | bytes 786464 | tf_op jit(solution)/shard_map/ppermute | solution.py:678
  243.4 7.3 %shard_map.114 = (f32[768,1536]{1,0:T(8,128)}, f32[8,768]{1,0:T(8,128)S(1)}) custom-call(bf16[128,1536]{1,0:T(8,128)(2,1)S(1)} %collective-permute-done.4.refs_0_, bf16[128,1536]{1,0:T(8,128)(2,1)S(1)} %collective-permute-done.6.refs_1_, bf16[128,1536]{1,0:T(8,128)(2,1)S(1)} %collective-permute-done.7.refs_2_, ...), custom_call_target="tpu_custom_call" | custom-call | flops 3019898880 | bytes 20000000 | tf_op jit(solution)/shard_map/pallas_call | solution.py:637
  (91 shorter events, 19.2 us)
Async XLA Ops:
  0.6 54.6 %collective-permute-start.1 = (bf16[128,6144]{1,0:T(8,128)(2,1)}, bf16[128,6144]{1,0:T(8,128)(2,1)S(1)}, u32[]{:S(2)}, u32[]{:S(2)}) collective-permute-start(bf16[128,6144]{1,0:T(8,128)(2,1)} %refs_0_.1), channel_id=1, source_target_pairs={{0,1},{1,2},{2,3},{3,0},{4,5},{5,6},{6,7},{7,4},{8,9},{9,10},{10,1... | collective-permute-start | bytes 4718600 | tf_op jit(solution)/shard_map/ppermute | solution.py:678
  13.6 29.2 %collective-permute-start.28 = (f32[136,128]{1,0:T(8,128)S(1)}, f32[136,128]{1,0:T(8,128)S(1)}, u32[]{:S(2)}, u32[]{:S(2)}) collective-permute-start(f32[136,128]{1,0:T(8,128)S(1)} %get-tuple-element.32), channel_id=1, source_target_pairs={{0,1},{1,2},{2,3},{3,0},{4,5},{5,6},{6,7},{7,4},{8,9},{9,10},{10,1... | collective-permute-start | bytes 208904 | tf_op jit(solution)/shard_map/ppermute | solution.py:678
  15.2 29.8 %collective-permute-start = (f32[136,128]{1,0:T(8,128)S(1)}, f32[136,128]{1,0:T(8,128)S(1)}, u32[]{:S(2)}, u32[]{:S(2)}) collective-permute-start(f32[136,128]{1,0:T(8,128)S(1)} %get-tuple-element.32), channel_id=1, source_target_pairs={{0,2},{1,3},{2,0},{3,1},{4,6},{5,7},{6,4},{7,5},{8,10},{9,11},{10,... | collective-permute-start | bytes 208904 | tf_op jit(solution)/shard_map/ppermute | solution.py:678
  16.3 28.7 %collective-permute-start.29 = (f32[136,128]{1,0:T(8,128)S(1)}, f32[136,128]{1,0:T(8,128)S(1)}, u32[]{:S(2)}, u32[]{:S(2)}) collective-permute-start(f32[136,128]{1,0:T(8,128)S(1)} %get-tuple-element.32), channel_id=1, source_target_pairs={{0,3},{1,0},{2,1},{3,2},{4,7},{5,4},{6,5},{7,6},{8,11},{9,8},{10,9... | collective-permute-start | bytes 208904 | tf_op jit(solution)/shard_map/ppermute | solution.py:678
  45.0 3.5 %collective-permute-start.30 = (f32[4,128]{1,0:T(4,128)S(1)}, f32[4,128]{1,0:T(4,128)S(1)}, u32[]{:S(2)}, u32[]{:S(2)}) collective-permute-start(f32[4,128]{1,0:T(4,128)S(1)} %pad_maximum_fusion.refs_0_), channel_id=1, source_target_pairs={{0,4},{4,0},{8,12},{12,8},{16,20},{20,16},{24,28},{28,24},{1,5},{5... | collective-permute-start | bytes 6152 | tf_op jit(solution)/shard_map/ppermute | solution.py:681
  45.1 3.7 %collective-permute-start.31 = (f32[4,128]{1,0:T(4,128)S(1)}, f32[4,128]{1,0:T(4,128)S(1)}, u32[]{:S(2)}, u32[]{:S(2)}) collective-permute-start(f32[4,128]{1,0:T(4,128)S(1)} %pad_maximum_fusion.refs_0_), channel_id=1, source_target_pairs={{0,8},{4,12},{8,0},{12,4},{16,24},{20,28},{24,16},{28,20},{1,9},{5... | collective-permute-start | bytes 6152 | tf_op jit(solution)/shard_map/ppermute | solution.py:681
  46.6 4.5 %collective-permute-start.32 = (f32[4,128]{1,0:T(4,128)S(1)}, f32[4,128]{1,0:T(4,128)S(1)}, u32[]{:S(2)}, u32[]{:S(2)}) collective-permute-start(f32[4,128]{1,0:T(4,128)S(1)} %pad_maximum_fusion.refs_0_), channel_id=1, source_target_pairs={{0,12},{4,8},{8,4},{12,0},{16,28},{20,24},{24,20},{28,16},{1,13},{... | collective-permute-start | bytes 6152 | tf_op jit(solution)/shard_map/ppermute | solution.py:681
  46.9 4.8 %collective-permute-start.33 = (f32[4,128]{1,0:T(4,128)S(1)}, f32[4,128]{1,0:T(4,128)S(1)}, u32[]{:S(2)}, u32[]{:S(2)}) collective-permute-start(f32[4,128]{1,0:T(4,128)S(1)} %pad_maximum_fusion.refs_0_), channel_id=1, source_target_pairs={{0,16},{4,20},{8,24},{12,28},{16,0},{20,4},{24,8},{28,12},{1,17},{... | collective-permute-start | bytes 6152 | tf_op jit(solution)/shard_map/ppermute | solution.py:681
  48.5 3.8 %collective-permute-start.34 = (f32[4,128]{1,0:T(4,128)S(1)}, f32[4,128]{1,0:T(4,128)S(1)}, u32[]{:S(2)}, u32[]{:S(2)}) collective-permute-start(f32[4,128]{1,0:T(4,128)S(1)} %pad_maximum_fusion.refs_0_), channel_id=1, source_target_pairs={{0,20},{4,16},{8,28},{12,24},{16,4},{20,0},{24,12},{28,8},{1,21},{... | collective-permute-start | bytes 6152 | tf_op jit(solution)/shard_map/ppermute | solution.py:681
  48.7 5.0 %collective-permute-start.35 = (f32[4,128]{1,0:T(4,128)S(1)}, f32[4,128]{1,0:T(4,128)S(1)}, u32[]{:S(2)}, u32[]{:S(2)}) collective-permute-start(f32[4,128]{1,0:T(4,128)S(1)} %pad_maximum_fusion.refs_0_), channel_id=1, source_target_pairs={{0,24},{4,28},{8,16},{12,20},{16,8},{20,12},{24,0},{28,4},{1,25},{... | collective-permute-start | bytes 6152 | tf_op jit(solution)/shard_map/ppermute | solution.py:681
  51.2 12.0 %collective-permute-start.11 = (bf16[128,1536]{1,0:T(8,128)(2,1)S(1)}, bf16[128,1536]{1,0:T(8,128)(2,1)S(1)}, u32[]{:S(2)}, u32[]{:S(2)}) collective-permute-start(bf16[128,1536]{1,0:T(8,128)(2,1)S(1)} %get-tuple-element.38), channel_id=1, source_target_pairs={{0,8},{4,12},{8,0},{12,4},{16,24},{20,28},{24,16},{28,20},{1,9},{5... | collective-permute-start | bytes 1179656 | tf_op jit(solution)/shard_map/ppermute | solution.py:681
  51.7 25.2 %collective-permute-start.10 = (bf16[128,2304]{1,0:T(8,128)(2,1)S(1)}, bf16[128,2304]{1,0:T(8,128)(2,1)S(1)}, u32[]{:S(2)}, u32[]{:S(2)}) collective-permute-start(bf16[128,2304]{1,0:T(8,128)(2,1)S(1)} %get-tuple-element.37), channel_id=1, source_target_pairs={{0,16},{4,20},{8,24},{12,28},{16,0},{20,4},{24,8},{28,12},{1,17},{... | collective-permute-start | bytes 1769480 | tf_op jit(solution)/shard_map/ppermute | solution.py:681
  52.2 26.2 %collective-permute-start.9 = (bf16[128,2304]{1,0:T(8,128)(2,1)S(1)}, bf16[128,2304]{1,0:T(8,128)(2,1)S(1)}, u32[]{:S(2)}, u32[]{:S(2)}) collective-permute-start(bf16[128,2304]{1,0:T(8,128)(2,1)S(1)} %get-tuple-element.36), channel_id=1, source_target_pairs={{0,8},{4,12},{8,0},{12,4},{16,24},{20,28},{24,16},{28,20},{1,9},{5... | collective-permute-start | bytes 1769480 | tf_op jit(solution)/shard_map/ppermute | solution.py:681
  53.7 22.7 %collective-permute-start.13 = (bf16[128,1536]{1,0:T(8,128)(2,1)S(1)}, bf16[128,1536]{1,0:T(8,128)(2,1)S(1)}, u32[]{:S(2)}, u32[]{:S(2)}) collective-permute-start(bf16[128,1536]{1,0:T(8,128)(2,1)S(1)} %get-tuple-element.39), channel_id=1, source_target_pairs={{0,16},{4,20},{8,24},{12,28},{16,0},{20,4},{24,8},{28,12},{1,17},{... | collective-permute-start | bytes 1179656 | tf_op jit(solution)/shard_map/ppermute | solution.py:681
  55.2 18.7 %collective-permute-start.36 = (f32[4,128]{1,0:T(4,128)S(1)}, f32[4,128]{1,0:T(4,128)S(1)}, u32[]{:S(2)}, u32[]{:S(2)}) collective-permute-start(f32[4,128]{1,0:T(4,128)S(1)} %pad_maximum_fusion.refs_0_), channel_id=1, source_target_pairs={{0,28},{4,24},{8,20},{12,16},{16,12},{20,8},{24,4},{28,0},{1,29},{... | collective-permute-start | bytes 6152 | tf_op jit(solution)/shard_map/ppermute | solution.py:681
  63.2 21.6 %collective-permute-start.12 = (bf16[128,1536]{1,0:T(8,128)(2,1)S(1)}, bf16[128,1536]{1,0:T(8,128)(2,1)S(1)}, u32[]{:S(2)}, u32[]{:S(2)}) collective-permute-start(bf16[128,1536]{1,0:T(8,128)(2,1)S(1)} %collective-permute-done.11.refs_1_), channel_id=1, source_target_pairs={{0,16},{4,20},{8,24},{12,28},{16,0},{20,4},{24,8},{28,12},{1,17},{... | collective-permute-start | bytes 1179656 | tf_op jit(solution)/shard_map/ppermute | solution.py:681
  74.0 12.3 %collective-permute-start.44 = (bf16[128,1536]{1,0:T(8,128)(2,1)S(1)}, bf16[128,1536]{1,0:T(8,128)(2,1)S(1)}, u32[]{:S(2)}, u32[]{:S(2)}) collective-permute-start(bf16[128,1536]{1,0:T(8,128)(2,1)S(1)} %get-tuple-element.48), channel_id=1, source_target_pairs={{0,8},{4,12},{8,0},{12,4},{16,24},{20,28},{24,16},{28,20},{1,9},{5... | collective-permute-start | bytes 1179656 | tf_op jit(solution)/shard_map/ppermute | solution.py:681
  76.4 16.9 %collective-permute-start.46 = (bf16[128,1536]{1,0:T(8,128)(2,1)S(1)}, bf16[128,1536]{1,0:T(8,128)(2,1)S(1)}, u32[]{:S(2)}, u32[]{:S(2)}) collective-permute-start(bf16[128,1536]{1,0:T(8,128)(2,1)S(1)} %get-tuple-element.50), channel_id=1, source_target_pairs={{0,16},{4,20},{8,24},{12,28},{16,0},{20,4},{24,8},{28,12},{1,17},{... | collective-permute-start | bytes 1179656 | tf_op jit(solution)/shard_map/ppermute | solution.py:681
  76.9 30.1 %collective-permute-start.45 = (bf16[128,2304]{1,0:T(8,128)(2,1)S(1)}, bf16[128,2304]{1,0:T(8,128)(2,1)S(1)}, u32[]{:S(2)}, u32[]{:S(2)}) collective-permute-start(bf16[128,2304]{1,0:T(8,128)(2,1)S(1)} %get-tuple-element.49), channel_id=1, source_target_pairs={{0,8},{4,12},{8,0},{12,4},{16,24},{20,28},{24,16},{28,20},{1,9},{5... | collective-permute-start | bytes 1769480 | tf_op jit(solution)/shard_map/ppermute | solution.py:681
  78.4 28.7 %collective-permute-start.47 = (bf16[128,2304]{1,0:T(8,128)(2,1)S(1)}, bf16[128,2304]{1,0:T(8,128)(2,1)S(1)}, u32[]{:S(2)}, u32[]{:S(2)}) collective-permute-start(bf16[128,2304]{1,0:T(8,128)(2,1)S(1)} %get-tuple-element.51), channel_id=1, source_target_pairs={{0,16},{4,20},{8,24},{12,28},{16,0},{20,4},{24,8},{28,12},{1,17},{... | collective-permute-start | bytes 1769480 | tf_op jit(solution)/shard_map/ppermute | solution.py:681
  84.8 22.2 %collective-permute-start.14 = (bf16[128,1536]{1,0:T(8,128)(2,1)S(1)}, bf16[128,1536]{1,0:T(8,128)(2,1)S(1)}, u32[]{:S(2)}, u32[]{:S(2)}) collective-permute-start(bf16[128,1536]{1,0:T(8,128)(2,1)S(1)} %collective-permute-done.13.refs_3_), channel_id=1, source_target_pairs={{0,8},{4,12},{8,0},{12,4},{16,24},{20,28},{24,16},{28,20},{1,9},{5... | collective-permute-start | bytes 1179656 | tf_op jit(solution)/shard_map/ppermute | solution.py:681
  86.3 26.8 %collective-permute-start.48 = (bf16[128,1536]{1,0:T(8,128)(2,1)S(1)}, bf16[128,1536]{1,0:T(8,128)(2,1)S(1)}, u32[]{:S(2)}, u32[]{:S(2)}) collective-permute-start(bf16[128,1536]{1,0:T(8,128)(2,1)S(1)} %collective-permute-done.44.refs_8_), channel_id=1, source_target_pairs={{0,16},{4,20},{8,24},{12,28},{16,0},{20,4},{24,8},{28,12},{1,17},{... | collective-permute-start | bytes 1179656 | tf_op jit(solution)/shard_map/ppermute | solution.py:681
  93.2 22.1 %collective-permute-start.49 = (bf16[128,1536]{1,0:T(8,128)(2,1)S(1)}, bf16[128,1536]{1,0:T(8,128)(2,1)S(1)}, u32[]{:S(2)}, u32[]{:S(2)}) collective-permute-start(bf16[128,1536]{1,0:T(8,128)(2,1)S(1)} %collective-permute-done.46.refs_10_), channel_id=1, source_target_pairs={{0,8},{4,12},{8,0},{12,4},{16,24},{20,28},{24,16},{28,20},{1,9},{5... | collective-permute-start | bytes 1179656 | tf_op jit(solution)/shard_map/ppermute | solution.py:681
  120.9 107.2 %collective-permute-start.50 = (f32[768,1536]{1,0:T(8,128)S(1)}, f32[768,1536]{1,0:T(8,128)S(1)}, u32[]{:S(2)}, u32[]{:S(2)}) collective-permute-start(f32[768,1536]{1,0:T(8,128)S(1)} %get-tuple-element.53), channel_id=1, source_target_pairs={{0,4},{4,0},{8,12},{12,8},{16,20},{20,16},{24,28},{28,24},{1,5},{5... | collective-permute-start | bytes 14155784 | tf_op jit(solution)/shard_map/ppermute | solution.py:681
  121.0 67.0 %collective-permute-start.2 = (bf16[128,6144]{1,0:T(8,128)(2,1)S(1)}, bf16[128,6144]{1,0:T(8,128)(2,1)S(1)}, u32[]{:S(2)}, u32[]{:S(2)}) collective-permute-start(bf16[128,6144]{1,0:T(8,128)(2,1)S(1)} %collective-permute-done.1.x_ref), channel_id=1, source_target_pairs={{0,1},{1,2},{2,3},{3,0},{4,5},{5,6},{6,7},{7,4},{8,9},{9,10},{10,1... | collective-permute-start | bytes 4718600 | tf_op jit(solution)/shard_map/ppermute | solution.py:678
  123.0 44.9 %collective-permute-start.16 = (bf16[128,1536]{1,0:T(8,128)(2,1)S(1)}, bf16[128,1536]{1,0:T(8,128)(2,1)S(1)}, u32[]{:S(2)}, u32[]{:S(2)}) collective-permute-start(bf16[128,1536]{1,0:T(8,128)(2,1)S(1)} %get-tuple-element.41), channel_id=1, source_target_pairs={{0,3},{1,0},{2,1},{3,2},{4,7},{5,4},{6,5},{7,6},{8,11},{9,8},{10,9... | collective-permute-start | bytes 1179656 | tf_op jit(solution)/shard_map/ppermute | solution.py:678
  167.9 10.9 %collective-permute-start.17 = (bf16[128,1536]{1,0:T(8,128)(2,1)S(1)}, bf16[128,1536]{1,0:T(8,128)(2,1)S(1)}, u32[]{:S(2)}, u32[]{:S(2)}) collective-permute-start(bf16[128,1536]{1,0:T(8,128)(2,1)S(1)} %collective-permute-done.16.refs_5_), channel_id=1, source_target_pairs={{0,8},{4,12},{8,0},{12,4},{16,24},{20,28},{24,16},{28,20},{1,9},{5... | collective-permute-start | bytes 1179656 | tf_op jit(solution)/shard_map/ppermute | solution.py:681
  168.5 12.1 %collective-permute-start.18 = (bf16[128,1536]{1,0:T(8,128)(2,1)S(1)}, bf16[128,1536]{1,0:T(8,128)(2,1)S(1)}, u32[]{:S(2)}, u32[]{:S(2)}) collective-permute-start(bf16[128,1536]{1,0:T(8,128)(2,1)S(1)} %collective-permute-done.16.refs_5_), channel_id=1, source_target_pairs={{0,16},{4,20},{8,24},{12,28},{16,0},{20,4},{24,8},{28,12},{1,17},{... | collective-permute-start | bytes 1179656 | tf_op jit(solution)/shard_map/ppermute | solution.py:681
  170.0 12.2 %collective-permute-start.23 = (bf16[128,1536]{1,0:T(8,128)(2,1)S(1)}, bf16[128,1536]{1,0:T(8,128)(2,1)S(1)}, u32[]{:S(2)}, u32[]{:S(2)}) collective-permute-start(bf16[128,1536]{1,0:T(8,128)(2,1)S(1)} %collective-permute-done.16.refs_5_), channel_id=1, source_target_pairs={{0,4},{4,0},{8,12},{12,8},{16,20},{20,16},{24,28},{28,24},{1,5},{5... | collective-permute-start | bytes 1179656 | tf_op jit(solution)/shard_map/ppermute | solution.py:681
  178.8 18.5 %collective-permute-start.21 = (bf16[768,512]{1,0:T(8,128)(2,1)S(1)}, bf16[768,512]{1,0:T(8,128)(2,1)S(1)}, u32[]{:S(2)}, u32[]{:S(2)}) collective-permute-start(bf16[768,512]{1,0:T(8,128)(2,1)S(1)} %get-tuple-element.42), channel_id=1, source_target_pairs={{0,3},{1,0},{2,1},{3,2},{4,7},{5,4},{6,5},{7,6},{8,11},{9,8},{10,9... | collective-permute-start | bytes 2359304 | tf_op jit(solution)/shard_map/ppermute | solution.py:678
  180.6 5.7 %collective-permute-start.19 = (bf16[128,768]{1,0:T(8,128)(2,1)S(1)}, bf16[128,768]{1,0:T(8,128)(2,1)S(1)}, u32[]{:S(2)}, u32[]{:S(2)}) collective-permute-start(bf16[128,768]{1,0:T(8,128)(2,1)S(1)} %slice.28), channel_id=1, source_target_pairs={{0,16},{4,20},{8,24},{12,28},{16,0},{20,4},{24,8},{28,12},{1,17},{... | collective-permute-start | bytes 589832 | tf_op jit(solution)/shard_map/ppermute | solution.py:681
  182.2 5.7 %collective-permute-start.20 = (bf16[128,768]{1,0:T(8,128)(2,1)S(1)}, bf16[128,768]{1,0:T(8,128)(2,1)S(1)}, u32[]{:S(2)}, u32[]{:S(2)}) collective-permute-start(bf16[128,768]{1,0:T(8,128)(2,1)S(1)} %slice.29), channel_id=1, source_target_pairs={{0,8},{4,12},{8,0},{12,4},{16,24},{20,28},{24,16},{28,20},{1,9},{5... | collective-permute-start | bytes 589832 | tf_op jit(solution)/shard_map/ppermute | solution.py:681
  186.4 4.1 %collective-permute-start.26 = (bf16[128,768]{1,0:T(8,128)(2,1)S(1)}, bf16[128,768]{1,0:T(8,128)(2,1)S(1)}, u32[]{:S(2)}, u32[]{:S(2)}) collective-permute-start(bf16[128,768]{1,0:T(8,128)(2,1)S(1)} %collective-permute-done.19.refs_8_), channel_id=1, source_target_pairs={{0,4},{4,0},{8,12},{12,8},{16,20},{20,16},{24,28},{28,24},{1,5},{5... | collective-permute-start | bytes 589832 | tf_op jit(solution)/shard_map/ppermute | solution.py:681
  188.0 4.5 %collective-permute-start.24 = (bf16[128,1536]{1,0:T(8,128)(2,1)S(1)}, bf16[128,1536]{1,0:T(8,128)(2,1)S(1)}, u32[]{:S(2)}, u32[]{:S(2)}) collective-permute-start(bf16[128,1536]{1,0:T(8,128)(2,1)S(1)} %collective-permute-done.17.refs_6_), channel_id=1, source_target_pairs={{0,4},{4,0},{8,12},{12,8},{16,20},{20,16},{24,28},{28,24},{1,5},{5... | collective-permute-start | bytes 1179656 | tf_op jit(solution)/shard_map/ppermute | solution.py:681
  190.4 12.1 %collective-permute-start.3 = (bf16[128,1536]{1,0:T(8,128)(2,1)S(1)}, bf16[128,1536]{1,0:T(8,128)(2,1)S(1)}, u32[]{:S(2)}, u32[]{:S(2)}) collective-permute-start(bf16[128,1536]{1,0:T(8,128)(2,1)S(1)} %get-tuple-element.33), channel_id=1, source_target_pairs={{0,8},{4,12},{8,0},{12,4},{16,24},{20,28},{24,16},{28,20},{1,9},{5... | collective-permute-start | bytes 1179656 | tf_op jit(solution)/shard_map/ppermute | solution.py:681
  191.1 23.1 %collective-permute-start.37 = (bf16[128,2304]{1,0:T(8,128)(2,1)S(1)}, bf16[128,2304]{1,0:T(8,128)(2,1)S(1)}, u32[]{:S(2)}, u32[]{:S(2)}) collective-permute-start(bf16[128,2304]{1,0:T(8,128)(2,1)S(1)} %get-tuple-element.45), channel_id=1, source_target_pairs={{0,8},{4,12},{8,0},{12,4},{16,24},{20,28},{24,16},{28,20},{1,9},{5... | collective-permute-start | bytes 1769480 | tf_op jit(solution)/shard_map/ppermute | solution.py:681
  192.5 12.0 %collective-permute-start.5 = (bf16[128,1536]{1,0:T(8,128)(2,1)S(1)}, bf16[128,1536]{1,0:T(8,128)(2,1)S(1)}, u32[]{:S(2)}, u32[]{:S(2)}) collective-permute-start(bf16[128,1536]{1,0:T(8,128)(2,1)S(1)} %get-tuple-element.34), channel_id=1, source_target_pairs={{0,16},{4,20},{8,24},{12,28},{16,0},{20,4},{24,8},{28,12},{1,17},{... | collective-permute-start | bytes 1179656 | tf_op jit(solution)/shard_map/ppermute | solution.py:681
  198.5 17.2 %collective-permute-start.38 = (bf16[128,2304]{1,0:T(8,128)(2,1)S(1)}, bf16[128,2304]{1,0:T(8,128)(2,1)S(1)}, u32[]{:S(2)}, u32[]{:S(2)}) collective-permute-start(bf16[128,2304]{1,0:T(8,128)(2,1)S(1)} %get-tuple-element.46), channel_id=1, source_target_pairs={{0,16},{4,20},{8,24},{12,28},{16,0},{20,4},{24,8},{28,12},{1,17},{... | collective-permute-start | bytes 1769480 | tf_op jit(solution)/shard_map/ppermute | solution.py:681
  202.5 14.2 %collective-permute-start.39 = (bf16[128,3072]{1,0:T(8,128)(2,1)S(1)}, bf16[128,3072]{1,0:T(8,128)(2,1)S(1)}, u32[]{:S(2)}, u32[]{:S(2)}) collective-permute-start(bf16[128,3072]{1,0:T(8,128)(2,1)S(1)} %get-tuple-element.44.refs_0_), channel_id=1, source_target_pairs={{0,4},{4,0},{8,12},{12,8},{16,20},{20,16},{24,28},{28,24},{1,5},{5... | collective-permute-start | bytes 2359304 | tf_op jit(solution)/shard_map/ppermute | solution.py:681
  204.5 11.6 %collective-permute-start.40 = (bf16[128,1536]{1,0:T(8,128)(2,1)S(1)}, bf16[128,1536]{1,0:T(8,128)(2,1)S(1)}, u32[]{:S(2)}, u32[]{:S(2)}) collective-permute-start(bf16[128,1536]{1,0:T(8,128)(2,1)S(1)} %collective-permute-done.3.refs_1_), channel_id=1, source_target_pairs={{0,4},{4,0},{8,12},{12,8},{16,20},{20,16},{24,28},{28,24},{1,5},{5... | collective-permute-start | bytes 1179656 | tf_op jit(solution)/shard_map/ppermute | solution.py:681
  215.7 10.1 %collective-permute-start.4 = (bf16[128,1536]{1,0:T(8,128)(2,1)S(1)}, bf16[128,1536]{1,0:T(8,128)(2,1)S(1)}, u32[]{:S(2)}, u32[]{:S(2)}) collective-permute-start(bf16[128,1536]{1,0:T(8,128)(2,1)S(1)} %collective-permute-done.3.refs_1_), channel_id=1, source_target_pairs={{0,16},{4,20},{8,24},{12,28},{16,0},{20,4},{24,8},{28,12},{1,17},{... | collective-permute-start | bytes 1179656 | tf_op jit(solution)/shard_map/ppermute | solution.py:681
  216.1 11.4 %collective-permute-start.6 = (bf16[128,1536]{1,0:T(8,128)(2,1)S(1)}, bf16[128,1536]{1,0:T(8,128)(2,1)S(1)}, u32[]{:S(2)}, u32[]{:S(2)}) collective-permute-start(bf16[128,1536]{1,0:T(8,128)(2,1)S(1)} %collective-permute-done.5.refs_3_), channel_id=1, source_target_pairs={{0,8},{4,12},{8,0},{12,4},{16,24},{20,28},{24,16},{28,20},{1,9},{5... | collective-permute-start | bytes 1179656 | tf_op jit(solution)/shard_map/ppermute | solution.py:681
  216.7 10.8 %collective-permute-start.41 = (bf16[128,2304]{1,0:T(8,128)(2,1)S(1)}, bf16[128,2304]{1,0:T(8,128)(2,1)S(1)}, u32[]{:S(2)}, u32[]{:S(2)}) collective-permute-start(bf16[128,2304]{1,0:T(8,128)(2,1)S(1)} %collective-permute-done.37.refs_2_), channel_id=1, source_target_pairs={{0,4},{4,0},{8,12},{12,8},{16,20},{20,16},{24,28},{28,24},{1,5},{5... | collective-permute-start | bytes 1769480 | tf_op jit(solution)/shard_map/ppermute | solution.py:681
  216.7 11.3 %collective-permute-start.43 = (bf16[128,2304]{1,0:T(8,128)(2,1)S(1)}, bf16[128,2304]{1,0:T(8,128)(2,1)S(1)}, u32[]{:S(2)}, u32[]{:S(2)}) collective-permute-start(bf16[128,2304]{1,0:T(8,128)(2,1)S(1)} %collective-permute-done.38.refs_4_), channel_id=1, source_target_pairs={{0,4},{4,0},{8,12},{12,8},{16,20},{20,16},{24,28},{28,24},{1,5},{5... | collective-permute-start | bytes 1769480 | tf_op jit(solution)/shard_map/ppermute | solution.py:681
  225.7 17.6 %collective-permute-start.15 = (bf16[768,512]{1,0:T(8,128)(2,1)S(1)}, bf16[768,512]{1,0:T(8,128)(2,1)S(1)}, u32[]{:S(2)}, u32[]{:S(2)}) collective-permute-start(bf16[768,512]{1,0:T(8,128)(2,1)S(1)} %get-tuple-element.40), channel_id=1, source_target_pairs={{0,3},{1,0},{2,1},{3,2},{4,7},{5,4},{6,5},{7,6},{8,11},{9,8},{10,9... | collective-permute-start | bytes 2359304 | tf_op jit(solution)/shard_map/ppermute | solution.py:678
  227.5 15.9 %collective-permute-start.22 = (bf16[768,512]{1,0:T(8,128)(2,1)S(1)}, bf16[768,512]{1,0:T(8,128)(2,1)S(1)}, u32[]{:S(2)}, u32[]{:S(2)}) collective-permute-start(bf16[768,512]{1,0:T(8,128)(2,1)S(1)} %collective-permute-done.21), channel_id=1, source_target_pairs={{0,4},{4,0},{8,12},{12,8},{16,20},{20,16},{24,28},{28,24},{1,5},{5... | collective-permute-start | bytes 2359304 | tf_op jit(solution)/shard_map/ppermute | solution.py:681
  228.0 15.3 %collective-permute-start.7 = (bf16[128,1536]{1,0:T(8,128)(2,1)S(1)}, bf16[128,1536]{1,0:T(8,128)(2,1)S(1)}, u32[]{:S(2)}, u32[]{:S(2)}) collective-permute-start(bf16[128,1536]{1,0:T(8,128)(2,1)S(1)} %collective-permute-done.4.refs_0_), channel_id=1, source_target_pairs={{0,4},{4,0},{8,12},{12,8},{16,20},{20,16},{24,28},{28,24},{1,5},{5... | collective-permute-start | bytes 1179656 | tf_op jit(solution)/shard_map/ppermute | solution.py:681
  228.1 15.3 %collective-permute-start.8 = (bf16[128,1536]{1,0:T(8,128)(2,1)S(1)}, bf16[128,1536]{1,0:T(8,128)(2,1)S(1)}, u32[]{:S(2)}, u32[]{:S(2)}) collective-permute-start(bf16[128,1536]{1,0:T(8,128)(2,1)S(1)} %collective-permute-done.6.refs_1_), channel_id=1, source_target_pairs={{0,4},{4,0},{8,12},{12,8},{16,20},{20,16},{24,28},{28,24},{1,5},{5... | collective-permute-start | bytes 1179656 | tf_op jit(solution)/shard_map/ppermute | solution.py:681
  (13 other events, 89.2 us)

commit v3 on v2

--- a/solution.py
+++ b/solution.py
@@ -395,8 +395,8 @@
         sources = refs[:8]
         near_ref = refs[8]
         outs = refs[9:14]
-        before_ref = refs[14]
-        x_ref, obs_ref, gap_ref, noise_ref, len_ref, amp_ref, decay_ref, map_ref, held, sems = refs[15:]
+        far_ref, near_cols_ref = refs[14:16]
+        x_ref, obs_ref, gap_ref, noise_ref, len_ref, amp_ref, decay_ref, map_ref, held, sems = refs[16:]
         targets = (x_ref, obs_ref, gap_ref, noise_ref, len_ref, amp_ref, decay_ref, map_ref)
         copies = [
             pltpu.make_async_copy(source, target, sems.at[k])
@@ -421,17 +421,17 @@
             return split_dot(near_ref[:block_rows, :], held[:, : count * size])
 
         cut_columns((per_row, per_col, own, cols_width // 2, col * per_col), fetch, row, outs)
-        before = jnp.where(col == 0, cols_axis - 1, col - 1)
-        before_ref[...] = fetch(before * per_col, per_col)
+        far_ref[...] = fetch(jnp.bitwise_xor(col, 3) * per_col, per_col)
+        near_cols_ref[...] = fetch(jnp.bitwise_xor(col, 2) * per_col, per_col)
 
     line = pltpu.VMEM((1, block_rows), F32)
     outs = [(block_rows + 8, block_rows, F32)]
-    outs += [(block_rows, w, BF16) for w in cut_widths(own, cols_width) + [cols_width]]
+    outs += [(block_rows, w, BF16) for w in cut_widths(own, cols_width) + [cols_width] * 2]
     return pl.pallas_call(
         kernel,
         name="head",
         in_specs=[SMEM] + [ANY] * 8,
-        out_specs=[VMEM] * 7,
+        out_specs=[VMEM] * 8,
         out_shape=[jax.ShapeDtypeStruct((h, w), t) for h, w, t in outs],
         scratch_shapes=[
             pltpu.VMEM((block_rows, columns), BF16),
@@ -450,22 +450,31 @@
     )(where, design, *[v.reshape(1, -1) for v in small], *tables, tile_map.reshape(1, -1))
 
 
-def pack_cut(chunk, near, tile_map, where, rows_axis, cols_axis):
-    block_rows, columns = chunk.shape
+def pack_cut(chunks, nears, tile_map, where, rows_axis, cols_axis):
+    block_rows, columns = chunks[0].shape
     tiles = tile_map.shape[0]
     size = columns // tiles
     per_row, per_col = tiles // rows_axis, tiles // cols_axis
     own, cols_width = per_row * size, per_col * size
-
-    def kernel(map_ref, where_ref, near_ref, x_ref, *refs):
-        outs, held = refs[:-1], refs[-1]
+    count = len(chunks)
+
+    def kernel(map_ref, where_ref, *refs):
+        near_refs, x_refs = refs[:count], refs[count : 2 * count]
+        outs, held = refs[2 * count : -1], refs[-1]
         row, col = where_ref[0], where_ref[1]
-        weight = near_ref[:block_rows, :]
+        at_end = where_ref[2] == 1
+
+        def choose(refs, rows, cols):
+            first = refs[0][rows, cols]
+            return first if count == 1 else jnp.where(at_end, refs[1][rows, cols], first)
+
+        everything = pl.ds(0, block_rows)
+        weight = choose(near_refs, everything, pl.ds(0, block_rows))
 
         def fetch(base, count):
             for j in range(count):
                 at = pl.multiple_of(map_ref[base + j] * size, size)
-                held[:, j * size : (j + 1) * size] = x_ref[:, pl.ds(at, size)]
+                held[:, j * size : (j + 1) * size] = choose(x_refs, everything, pl.ds(at, size))
             return split_dot(weight, held[:, : count * size])
 
         cut_columns((per_row, per_col, own, cols_width // 2, col * per_col), fetch, row, outs)
@@ -473,7 +482,7 @@
     return pl.pallas_call(
         kernel,
         name="pack_cut",
-        in_specs=[SMEM, SMEM, VMEM, VMEM],
+        in_specs=[SMEM, SMEM] + [VMEM] * (2 * count),
         out_specs=[VMEM] * 5,
         out_shape=[
             jax.ShapeDtypeStruct((block_rows, w), BF16) for w in cut_widths(own, cols_width)
@@ -481,7 +490,7 @@
         scratch_shapes=[pltpu.VMEM((block_rows, max(own, cols_width)), BF16)],
         cost_estimate=pl.CostEstimate(flops=10**9, bytes_accessed=5 * 10**6, transcendentals=0),
         compiler_params=pltpu.CompilerParams(vmem_limit_bytes=8 << 20),
-    )(tile_map, where, near, chunk)
+    )(tile_map, where, *nears, *chunks)
 
 
 def row_parts(keep, xb, yb, fa, fb, own):
@@ -515,16 +524,17 @@
             held[at : at + source.shape[0], :] = source[...]
             at += source.shape[0]
         at = 0
+        end = where_ref[2]
+        planes = (0, 1, 3 - end, 2 + end)
         for m, s in places:
-            line = m * cols_axis + s
             rows_ref[:, at : at + block_rows] = jnp.broadcast_to(
-                held[line : line + 1, :], (8, block_rows)
+                held[pl.ds(m * cols_axis + planes[s], 1), :], (8, block_rows)
             )
             at += block_rows
         from_row = lax.div(plan_ref[0], cols_axis)
         from_col = lax.rem(plan_ref[0], cols_axis)
         mask = jnp.bitwise_xor(from_row, where_ref[0])
-        step = lax.rem(where_ref[1] - from_col + cols_axis, cols_axis)
+        step = jnp.bitwise_xor(where_ref[1], from_col)
         picked_ref[...] = held[pl.ds(mask * cols_axis + step, 1), :]
 
     return pl.pallas_call(
@@ -671,18 +681,24 @@
     cols_width = (tiles // cols_axis) * size
     half = cols_width // 2
     row, col = lax.axis_index("row"), lax.axis_index("col")
-    where = jnp.stack([row, col]).astype(jnp.int32)
     last = cols_axis - 1
-
-    def ring(x, shift):
-        return lax.ppermute(x, "col", [(c, (c + shift) % cols_axis) for c in range(cols_axis)])
+    at_end = jnp.logical_or(col == 0, col == last)
+    where = jnp.stack([row, col, at_end.astype(jnp.int32)]).astype(jnp.int32)
+
+    def hop(x, pairs):
+        return lax.ppermute(x, "col", pairs)
+
+    def cross(x, mask):
+        return hop(x, [(c, c ^ mask) for c in range(cols_axis)])
 
     def swap(x, mask):
         return lax.ppermute(x, "row", [(r, r ^ mask) for r in range(rows_axis)])
 
-    chunks = [design]
-    for _ in range(1, last):
-        chunks.append(ring(chunks[-1], 1))
+    outward = [(1, 0), (last - 1, last)]
+    inward = [(last, 1), (0, last - 1)]
+    beside = cross(design, 1)
+    inner = hop(design, [(1, last - 1), (last - 1, 1)])
+    outer = hop(inner, outward)
     near, *parts = head(
         design,
         (observations, gaps, noise_var),
@@ -692,7 +708,7 @@
         rows_axis,
         cols_axis,
     )
-    line = [near] + [ring(near, s) for s in range(1, cols_axis)]
+    line = [near] + [cross(near, s) for s in range(1, cols_axis)]
     line_obs = jnp.stack([part[block_rows] for part in line])
     obs = [line_obs] + [swap(line_obs, m) for m in range(1, rows_axis)]
 
@@ -702,15 +718,20 @@
         return keep, xa, xb, ya, yb, swap(xa, 4), swap(ya, 2)
 
     traded = [trade(*parts[:5])]
-    for s in range(1, last):
-        cut = pack_cut(chunks[s], line[s], tile_map, where, rows_axis, cols_axis)
+    sources = ([beside], [line[1]]), ([inner, outer], [line[3], line[2]])
+    for s, (raw, nears) in enumerate(sources, 1):
+        cut = pack_cut(raw, nears, tile_map, where, rows_axis, cols_axis)
         traded.append(trade(*cut))
 
     keep, _, xb, _, yb, fa, fb = traded[0]
     lead, rest = row_parts(keep, xb, yb, fa, fb, own)
-    far_cols = ring(parts[5], last)
-    far_rest = ring(rest, last)
-    far_lead = ring(lead, last)
+    far_ends = hop(parts[5], [(last, 0), (0, last)])
+    far_inner = hop(parts[6], inward)
+    far_cols = jnp.where(at_end, far_ends, far_inner)
+    rest_inner = hop(rest, inward)
+    lead_inner = hop(lead, inward)
+    far_rest = jnp.where(at_end, hop(rest_inner, outward), rest_inner)
+    far_lead = jnp.where(at_end, hop(lead_inner, outward), lead_inner)
     x3, y3 = swap(far_cols, 2), swap(far_cols, 4)
     fa3 = swap(x3[:, :half], 4)
     fb3 = swap(y3[:, half:], 2)
@@ -804,7 +825,7 @@
         P(),
     )
     rows_axis, cols_axis = mesh.shape["row"], mesh.shape["col"]
-    square = rows_axis == 2**3 and cols_axis > 2
+    square = rows_axis == 2**3 and cols_axis == 2**2
 
     def body(*args):
         if not square:

time: 252 us -> 265 us (1.052)
  starting transfers between devices: 46.6 us -> 76.1 us
  waiting for transfers between devices: 172 us -> 154 us
    ppermute x8 -> x12, waiting for transfers between devices: 85.7 us -> 64.7 us  [hop(): return lax.ppermute(x, 'col', pairs)]
    ppermute x8 -> x12, starting transfers between devices: 16.1 us -> 32.7 us  [hop(): return lax.ppermute(x, 'col', pairs)]
    ppermute x44, starting transfers between devices: 30.5 us -> 43.4 us  [swap(): return lax.ppermute(x, 'row', [(r, r ^ mask) for r in range(rows_axis)])]
    unnamed x18 -> x22, local copies, waits for them, and re-layouts: 5.99 us -> 6.66 us
  transfers between devices with their start and end apart: 52 -> 56, of which waited for: 23 -> 23; matrix products, arithmetic and copies ran while one was open for 0% -> 0% of each run, Pallas kernels for 5% -> 7%
where the time goes in v3:
time: 265 us; the launch traced here: 264 us
  waiting for transfers between devices  154 us (58%)
  starting transfers between devices  76.1 us (29%)
  Pallas kernels  25 us (9%)
  local copies, waits for them, and re-layouts  7.3 us (3%)
    ppermute x44, waiting for transfers between devices, swap(): return lax.ppermute(x, 'row', [(r, r ^ mask) for r in range(rows_axis)])  89.1 us
    ppermute x12, waiting for transfers between devices, hop(): return lax.ppermute(x, 'col', pairs)  64.7 us
    ppermute x44, starting transfers between devices, swap(): return lax.ppermute(x, 'row', [(r, r ^ mask) for r in range(rows_axis)])  43.4 us
    ppermute x12, starting transfers between devices, hop(): return lax.ppermute(x, 'col', pairs)  32.7 us
    pallas_call x3, Pallas kernels, gram_direct(): pl.pallas_call(kernel, in_specs=[VMEM] * (count + 1 + len(before)), out_s...  15.2 us
    unnamed x22, local copies, waits for them, and re-layouts  6.66 us
  transfers between devices with their start and end apart: 56, of which 23 were waited for; matrix products, arithmetic and copies ran while one was open for 0% of the time, Pallas kernels for 7%

profile of v3, /device:TPU:0, one launch (start us, length us, event | category | flops | bytes accessed | tf_op | source)
XLA Modules:
  0.0 264.2 jit_solution(17512151322651034618)
XLA Ops:
  0.6 3.1 %collective-permute-start.47 = (bf16[128,6144]{1,0:T(8,128)(2,1)}, bf16[128,6144]{1,0:T(8,128)(2,1)S(1)}, u32[]{:S(2)}, u32[]{:S(2)}) collective-permute-start(bf16[128,6144]{1,0:T(8,128)(2,1)} %refs_0_.1), channel_id=1, source_target_pairs={{0,1},{1,0},{2,3},{3,2},{4,5},{5,4},{6,7},{7,6},{8,9},{9,8},{10,11... | collective-permute-start | bytes 4718600 | tf_op jit(solution)/shard_map/ppermute | solution.py:689
  3.8 1.4 copy-done
  9.8 3.9 %head.1 = (f32[136,128]{1,0:T(8,128)S(1)}, bf16[128,1536]{1,0:T(8,128)(2,1)S(1)}, bf16[128,2304]{1,0:T(8,128)(2,1)S(1)}, bf16[128,1536]{1,0:T(8,128)(2,1)S(1)}, ...) custom-call(s32[3]{0:T(128)S(1)} %pad_add_fusion.where_ref, ...), custom_call_target="tpu_custom_call" | custom-call | flops 1000000000 | bytes 5000000 | tf_op jit(solution)/shard_map/head/pallas_call | solution.py:430
  13.8 1.6 collective-permute-start.12
  15.8 2.6 collective-permute-start.1
  19.7 21.6 %collective-permute-done.32.refs_0_ = f32[136,128]{1,0:T(8,128)S(1)} collective-permute-done((f32[136,128]{1,0:T(8,128)S(1)}, f32[136,128]{1,0:T(8,128)S(1)}, u32[]{:S(2)}, u32[]{:S(2)}) %collective-permute-start.32) | collective-permute-done | bytes 69664 | tf_op jit(solution)/shard_map/ppermute | solution.py:689
  41.3 1.7 collective-permute-start.10
  43.0 2.0 collective-permute-done.refs_0_
  45.1 1.6 collective-permute-start.34
  47.5 8.4 %collective-permute-done.34.refs_2_ = f32[4,128]{1,0:T(4,128)S(1)} collective-permute-done((f32[4,128]{1,0:T(4,128)S(1)}, f32[4,128]{1,0:T(4,128)S(1)}, u32[]{:S(2)}, u32[]{:S(2)}) %collective-permute-start.34) | collective-permute-done | bytes 2080 | tf_op jit(solution)/shard_map/ppermute | solution.py:695
  55.9 1.4 collective-permute-start.36
  57.3 2.2 collective-permute-done.36.refs_4_
  59.5 2.3 collective-permute-start.38
  62.3 1.7 collective-permute-done.38.refs_6_
  64.1 1.4 collective-permute-start.14
  66.8 1.9 pack_cut.3
  68.7 1.4 collective-permute-done.39.refs_7_
  71.5 15.0 %collective-permute-done.14.refs_3_ = bf16[128,1536]{1,0:T(8,128)(2,1)S(1)} collective-permute-done((bf16[128,1536]{1,0:T(8,128)(2,1)S(1)}, bf16[128,1536]{1,0:T(8,128)(2,1)S(1)}, u32[]{:S(2)}, u32[]{:S(2)}) %collective-permute-start.14) | collective-permute-done | bytes 393248 | tf_op jit(solution)/shard_map/ppermute | solution.py:695
  89.0 5.9 %collective-permute-done.13.fa_ref.refs_5_ = bf16[128,1536]{1,0:T(8,128)(2,1)S(1)} collective-permute-done((bf16[128,1536]{1,0:T(8,128)(2,1)S(1)}, bf16[128,1536]{1,0:T(8,128)(2,1)S(1)}, u32[]{:S(2)}, u32[]{:S(2)}) %collective-permute-start.13) | collective-permute-done | bytes 393248 | tf_op jit(solution)/shard_map/ppermute | solution.py:695
  95.4 1.5 collective-permute-start.52
  96.9 6.4 %collective-permute-done.50.refs_10_ = bf16[128,1536]{1,0:T(8,128)(2,1)S(1)} collective-permute-done((bf16[128,1536]{1,0:T(8,128)(2,1)S(1)}, bf16[128,1536]{1,0:T(8,128)(2,1)S(1)}, u32[]{:S(2)}, u32[]{:S(2)}) %collective-permute-start.50) | collective-permute-done | bytes 393248 | tf_op jit(solution)/shard_map/ppermute | solution.py:695
  106.4 4.4 %collective-permute-done.49.refs_9_ = bf16[128,2304]{1,0:T(8,128)(2,1)S(1)} collective-permute-done((bf16[128,2304]{1,0:T(8,128)(2,1)S(1)}, bf16[128,2304]{1,0:T(8,128)(2,1)S(1)}, u32[]{:S(2)}, u32[]{:S(2)}) %collective-permute-start.49) | collective-permute-done | bytes 589856 | tf_op jit(solution)/shard_map/ppermute | solution.py:695
  110.7 5.3 %collective-permute-done.51.refs_11_ = bf16[128,2304]{1,0:T(8,128)(2,1)S(1)} collective-permute-done((bf16[128,2304]{1,0:T(8,128)(2,1)S(1)}, bf16[128,2304]{1,0:T(8,128)(2,1)S(1)}, u32[]{:S(2)}, u32[]{:S(2)}) %collective-permute-start.51) | collective-permute-done | bytes 589856 | tf_op jit(solution)/shard_map/ppermute | solution.py:695
  116.0 5.8 %collective-permute-done.52.refs_12_ = bf16[128,1536]{1,0:T(8,128)(2,1)S(1)} collective-permute-done((bf16[128,1536]{1,0:T(8,128)(2,1)S(1)}, bf16[128,1536]{1,0:T(8,128)(2,1)S(1)}, u32[]{:S(2)}, u32[]{:S(2)}) %collective-permute-start.52) | collective-permute-done | bytes 393248 | tf_op jit(solution)/shard_map/ppermute | solution.py:695
  121.7 5.6 %shard_map.112 = (f32[768,1536]{1,0:T(8,128)S(1)}, f32[768,1536]{1,0:T(8,128)S(1)}, f32[8,768]{1,0:T(8,128)S(1)}, f32[8,768]{1,0:T(8,128)S(1)}) custom-call(bf16[128,3072]{1,0:T(8,128)(2,1)S(1)} %get-tuple-element.36.keep_ref.refs_0_, bf16[128,1536]{1,0:T(8,128)(2,1)S(1)} %collective-permute-done.12.refs_1_, ...), custom_call_target="tpu_custom_call" | custom-call | flops 4831838208 | bytes 20000000 | tf_op jit(solution)/shard_map/pallas_call | solution.py:647
  127.4 5.7 %collective-permute-start.18 = (bf16[128,1536]{1,0:T(8,128)(2,1)S(1)}, bf16[128,1536]{1,0:T(8,128)(2,1)S(1)}, u32[]{:S(2)}, u32[]{:S(2)}) collective-permute-start(bf16[128,1536]{1,0:T(8,128)(2,1)S(1)} %get-tuple-element.42), channel_id=1, source_target_pairs={{3,0},{0,3},{7,4},{4,7},{11,8},{8,11},{15,12},{12,15},{19,16},{16,... | collective-permute-start | bytes 1179656 | tf_op jit(solution)/shard_map/ppermute | solution.py:689
  135.8 7.5 %collective-permute-done.18 = bf16[128,1536]{1,0:T(8,128)(2,1)S(1)} collective-permute-done((bf16[128,1536]{1,0:T(8,128)(2,1)S(1)}, bf16[128,1536]{1,0:T(8,128)(2,1)S(1)}, u32[]{:S(2)}, u32[]{:S(2)}) %collective-permute-start.18) | collective-permute-done | bytes 393248 | tf_op jit(solution)/shard_map/ppermute | solution.py:689
  143.3 7.4 %collective-permute-done.19 = bf16[128,1536]{1,0:T(8,128)(2,1)S(1)} collective-permute-done((bf16[128,1536]{1,0:T(8,128)(2,1)S(1)}, bf16[128,1536]{1,0:T(8,128)(2,1)S(1)}, u32[]{:S(2)}, u32[]{:S(2)}) %collective-permute-start.19) | collective-permute-done | bytes 393248 | tf_op jit(solution)/shard_map/ppermute | solution.py:689
  151.7 1.5 collective-permute-start.21
  153.7 8.9 %collective-permute-start.24 = (bf16[768,512]{1,0:T(8,128)(2,1)S(1)}, bf16[768,512]{1,0:T(8,128)(2,1)S(1)}, u32[]{:S(2)}, u32[]{:S(2)}) collective-permute-start(bf16[768,512]{1,0:T(8,128)(2,1)S(1)} %get-tuple-element.44), channel_id=1, source_target_pairs={{3,1},{0,2},{7,5},{4,6},{11,9},{8,10},{15,13},{12,14},{19,17},{16,... | collective-permute-start | bytes 2359304 | tf_op jit(solution)/shard_map/ppermute | solution.py:689
  162.5 4.5 %collective-permute-start.16 = (bf16[768,512]{1,0:T(8,128)(2,1)S(1)}, bf16[768,512]{1,0:T(8,128)(2,1)S(1)}, u32[]{:S(2)}, u32[]{:S(2)}) collective-permute-start(bf16[768,512]{1,0:T(8,128)(2,1)S(1)} %get-tuple-element.41), channel_id=1, source_target_pairs={{3,1},{0,2},{7,5},{4,6},{11,9},{8,10},{15,13},{12,14},{19,17},{16,... | collective-permute-start | bytes 2359304 | tf_op jit(solution)/shard_map/ppermute | solution.py:689
  167.2 1.7 collective-permute-done.27.refs_11_
  168.9 2.5 collective-permute-start.22
  171.3 9.1 %collective-permute-done.24 = bf16[768,512]{1,0:T(8,128)(2,1)S(1)} collective-permute-done((bf16[768,512]{1,0:T(8,128)(2,1)S(1)}, bf16[768,512]{1,0:T(8,128)(2,1)S(1)}, u32[]{:S(2)}, u32[]{:S(2)}) %collective-permute-start.24) | collective-permute-done | bytes 786464 | tf_op jit(solution)/shard_map/ppermute | solution.py:689
  181.7 10.1 %collective-permute-done.16 = bf16[768,512]{1,0:T(8,128)(2,1)S(1)} collective-permute-done((bf16[768,512]{1,0:T(8,128)(2,1)S(1)}, bf16[768,512]{1,0:T(8,128)(2,1)S(1)}, u32[]{:S(2)}, u32[]{:S(2)}) %collective-permute-start.16) | collective-permute-done | bytes 786464 | tf_op jit(solution)/shard_map/ppermute | solution.py:689
  191.8 1.5 collective-permute-start.17
  193.9 5.2 %collective-permute-done.23.refs_9_ = bf16[128,768]{1,0:T(8,128)(2,1)S(1)} collective-permute-done((bf16[128,768]{1,0:T(8,128)(2,1)S(1)}, bf16[128,768]{1,0:T(8,128)(2,1)S(1)}, u32[]{:S(2)}, u32[]{:S(2)}) %collective-permute-start.23) | collective-permute-done | bytes 196640 | tf_op jit(solution)/shard_map/ppermute | solution.py:695
  199.6 2.4 pack_cut.2
  202.6 1.5 collective-permute-start.40
  204.1 7.0 %collective-permute-done.17 = bf16[768,512]{1,0:T(8,128)(2,1)S(1)} collective-permute-done((bf16[768,512]{1,0:T(8,128)(2,1)S(1)}, bf16[768,512]{1,0:T(8,128)(2,1)S(1)}, u32[]{:S(2)}, u32[]{:S(2)}) %collective-permute-start.17) | collective-permute-done | bytes 786464 | tf_op jit(solution)/shard_map/ppermute | solution.py:689
  211.1 12.1 %collective-permute-start.6 = (bf16[128,1536]{1,0:T(8,128)(2,1)S(1)}, bf16[128,1536]{1,0:T(8,128)(2,1)S(1)}, u32[]{:S(2)}, u32[]{:S(2)}) collective-permute-start(bf16[128,1536]{1,0:T(8,128)(2,1)S(1)} %get-tuple-element.35), channel_id=1, source_target_pairs={{0,16},{4,20},{8,24},{12,28},{16,0},{20,4},{24,8},{28,12},{1,17},{... | collective-permute-start | bytes 1179656 | tf_op jit(solution)/shard_map/ppermute | solution.py:695
  223.3 9.4 %collective-permute-done.6.refs_3_ = bf16[128,1536]{1,0:T(8,128)(2,1)S(1)} collective-permute-done((bf16[128,1536]{1,0:T(8,128)(2,1)S(1)}, bf16[128,1536]{1,0:T(8,128)(2,1)S(1)}, u32[]{:S(2)}, u32[]{:S(2)}) %collective-permute-start.6) | collective-permute-done | bytes 393248 | tf_op jit(solution)/shard_map/ppermute | solution.py:695
  233.2 9.2 %collective-permute-done.41.refs_4_ = bf16[128,2304]{1,0:T(8,128)(2,1)S(1)} collective-permute-done((bf16[128,2304]{1,0:T(8,128)(2,1)S(1)}, bf16[128,2304]{1,0:T(8,128)(2,1)S(1)}, u32[]{:S(2)}, u32[]{:S(2)}) %collective-permute-start.41) | collective-permute-done | bytes 589856 | tf_op jit(solution)/shard_map/ppermute | solution.py:695
  242.5 2.5 collective-permute-start.5
  245.7 5.1 %collective-permute-done.5.refs_0_ = bf16[128,1536]{1,0:T(8,128)(2,1)S(1)} collective-permute-done((bf16[128,1536]{1,0:T(8,128)(2,1)S(1)}, bf16[128,1536]{1,0:T(8,128)(2,1)S(1)}, u32[]{:S(2)}, u32[]{:S(2)}) %collective-permute-start.5) | collective-permute-done | bytes 393248 | tf_op jit(solution)/shard_map/ppermute | solution.py:695
  250.7 2.0 collective-permute-done.7.refs_1_
  253.9 2.2 shard_map.113
  256.2 7.4 %shard_map.114 = (f32[768,1536]{1,0:T(8,128)}, f32[8,768]{1,0:T(8,128)S(1)}) custom-call(bf16[128,1536]{1,0:T(8,128)(2,1)S(1)} %collective-permute-done.5.refs_0_, bf16[128,1536]{1,0:T(8,128)(2,1)S(1)} %collective-permute-done.7.refs_1_, bf16[128,1536]{1,0:T(8,128)(2,1)S(1)} %collective-permute-done.8.refs_2_, ...), custom_call_target="tpu_custom_call" | custom-call | flops 3019898880 | bytes 20000000 | tf_op jit(solution)/shard_map/pallas_call | solution.py:647
  (106 shorter events, 26.1 us)
Async XLA Ops:
  0.6 65.5 %collective-permute-start.47 = (bf16[128,6144]{1,0:T(8,128)(2,1)}, bf16[128,6144]{1,0:T(8,128)(2,1)S(1)}, u32[]{:S(2)}, u32[]{:S(2)}) collective-permute-start(bf16[128,6144]{1,0:T(8,128)(2,1)} %refs_0_.1), channel_id=1, source_target_pairs={{0,1},{1,0},{2,3},{3,2},{4,5},{5,4},{6,7},{7,6},{8,9},{9,8},{10,11... | collective-permute-start | bytes 4718600 | tf_op jit(solution)/shard_map/ppermute | solution.py:689
  13.8 51.7 %collective-permute-start.12 = (bf16[128,1536]{1,0:T(8,128)(2,1)S(1)}, bf16[128,1536]{1,0:T(8,128)(2,1)S(1)}, u32[]{:S(2)}, u32[]{:S(2)}) collective-permute-start(bf16[128,1536]{1,0:T(8,128)(2,1)S(1)} %get-tuple-element.39), channel_id=1, source_target_pairs={{0,8},{4,12},{8,0},{12,4},{16,24},{20,28},{24,16},{28,20},{1,9},{5... | collective-permute-start | bytes 1179656 | tf_op jit(solution)/shard_map/ppermute | solution.py:695
  15.3 26.0 %collective-permute-start.32 = (f32[136,128]{1,0:T(8,128)S(1)}, f32[136,128]{1,0:T(8,128)S(1)}, u32[]{:S(2)}, u32[]{:S(2)}) collective-permute-start(f32[136,128]{1,0:T(8,128)S(1)} %get-tuple-element.33), channel_id=1, source_target_pairs={{0,1},{1,0},{2,3},{3,2},{4,5},{5,4},{6,7},{7,6},{8,9},{9,8},{10,11... | collective-permute-start | bytes 208904 | tf_op jit(solution)/shard_map/ppermute | solution.py:689
  15.8 27.2 %collective-permute-start.1 = (f32[136,128]{1,0:T(8,128)S(1)}, f32[136,128]{1,0:T(8,128)S(1)}, u32[]{:S(2)}, u32[]{:S(2)}) collective-permute-start(f32[136,128]{1,0:T(8,128)S(1)} %get-tuple-element.33), channel_id=1, source_target_pairs={{0,2},{1,3},{2,0},{3,1},{4,6},{5,7},{6,4},{7,5},{8,10},{9,11},{10,... | collective-permute-start | bytes 208904 | tf_op jit(solution)/shard_map/ppermute | solution.py:689
  18.4 26.6 %collective-permute-start = (f32[136,128]{1,0:T(8,128)S(1)}, f32[136,128]{1,0:T(8,128)S(1)}, u32[]{:S(2)}, u32[]{:S(2)}) collective-permute-start(f32[136,128]{1,0:T(8,128)S(1)} %get-tuple-element.33), channel_id=1, source_target_pairs={{0,3},{1,2},{2,1},{3,0},{4,7},{5,6},{6,5},{7,4},{8,11},{9,10},{10,... | collective-permute-start | bytes 208904 | tf_op jit(solution)/shard_map/ppermute | solution.py:689
  41.3 45.7 %collective-permute-start.10 = (bf16[128,2304]{1,0:T(8,128)(2,1)S(1)}, bf16[128,2304]{1,0:T(8,128)(2,1)S(1)}, u32[]{:S(2)}, u32[]{:S(2)}) collective-permute-start(bf16[128,2304]{1,0:T(8,128)(2,1)S(1)} %get-tuple-element.37), channel_id=1, source_target_pairs={{0,8},{4,12},{8,0},{12,4},{16,24},{20,28},{24,16},{28,20},{1,9},{5... | collective-permute-start | bytes 1769480 | tf_op jit(solution)/shard_map/ppermute | solution.py:695
  45.1 10.8 %collective-permute-start.34 = (f32[4,128]{1,0:T(4,128)S(1)}, f32[4,128]{1,0:T(4,128)S(1)}, u32[]{:S(2)}, u32[]{:S(2)}) collective-permute-start(f32[4,128]{1,0:T(4,128)S(1)} %pad_maximum_fusion.refs_0_), channel_id=1, source_target_pairs={{0,8},{4,12},{8,0},{12,4},{16,24},{20,28},{24,16},{28,20},{1,9},{5... | collective-permute-start | bytes 6152 | tf_op jit(solution)/shard_map/ppermute | solution.py:695
  46.7 10.6 %collective-permute-start.35 = (f32[4,128]{1,0:T(4,128)S(1)}, f32[4,128]{1,0:T(4,128)S(1)}, u32[]{:S(2)}, u32[]{:S(2)}) collective-permute-start(f32[4,128]{1,0:T(4,128)S(1)} %pad_maximum_fusion.refs_0_), channel_id=1, source_target_pairs={{0,12},{4,8},{8,4},{12,0},{16,28},{20,24},{24,20},{28,16},{1,13},{... | collective-permute-start | bytes 6152 | tf_op jit(solution)/shard_map/ppermute | solution.py:695
  55.9 3.6 %collective-permute-start.36 = (f32[4,128]{1,0:T(4,128)S(1)}, f32[4,128]{1,0:T(4,128)S(1)}, u32[]{:S(2)}, u32[]{:S(2)}) collective-permute-start(f32[4,128]{1,0:T(4,128)S(1)} %pad_maximum_fusion.refs_0_), channel_id=1, source_target_pairs={{0,16},{4,20},{8,24},{12,28},{16,0},{20,4},{24,8},{28,12},{1,17},{... | collective-permute-start | bytes 6152 | tf_op jit(solution)/shard_map/ppermute | solution.py:695
  57.3 4.5 %collective-permute-start.37 = (f32[4,128]{1,0:T(4,128)S(1)}, f32[4,128]{1,0:T(4,128)S(1)}, u32[]{:S(2)}, u32[]{:S(2)}) collective-permute-start(f32[4,128]{1,0:T(4,128)S(1)} %pad_maximum_fusion.refs_0_), channel_id=1, source_target_pairs={{0,20},{4,16},{8,28},{12,24},{16,4},{20,0},{24,12},{28,8},{1,21},{... | collective-permute-start | bytes 6152 | tf_op jit(solution)/shard_map/ppermute | solution.py:695
  59.5 4.6 %collective-permute-start.38 = (f32[4,128]{1,0:T(4,128)S(1)}, f32[4,128]{1,0:T(4,128)S(1)}, u32[]{:S(2)}, u32[]{:S(2)}) collective-permute-start(f32[4,128]{1,0:T(4,128)S(1)} %pad_maximum_fusion.refs_0_), channel_id=1, source_target_pairs={{0,24},{4,28},{8,16},{12,20},{16,8},{20,12},{24,0},{28,4},{1,25},{... | collective-permute-start | bytes 6152 | tf_op jit(solution)/shard_map/ppermute | solution.py:695
  61.8 25.9 %collective-permute-start.11 = (bf16[128,2304]{1,0:T(8,128)(2,1)S(1)}, bf16[128,2304]{1,0:T(8,128)(2,1)S(1)}, u32[]{:S(2)}, u32[]{:S(2)}) collective-permute-start(bf16[128,2304]{1,0:T(8,128)(2,1)S(1)} %get-tuple-element.38), channel_id=1, source_target_pairs={{0,16},{4,20},{8,24},{12,28},{16,0},{20,4},{24,8},{28,12},{1,17},{... | collective-permute-start | bytes 1769480 | tf_op jit(solution)/shard_map/ppermute | solution.py:695
  64.1 22.4 %collective-permute-start.14 = (bf16[128,1536]{1,0:T(8,128)(2,1)S(1)}, bf16[128,1536]{1,0:T(8,128)(2,1)S(1)}, u32[]{:S(2)}, u32[]{:S(2)}) collective-permute-start(bf16[128,1536]{1,0:T(8,128)(2,1)S(1)} %get-tuple-element.40), channel_id=1, source_target_pairs={{0,16},{4,20},{8,24},{12,28},{16,0},{20,4},{24,8},{28,12},{1,17},{... | collective-permute-start | bytes 1179656 | tf_op jit(solution)/shard_map/ppermute | solution.py:695
  65.5 29.4 %collective-permute-start.13 = (bf16[128,1536]{1,0:T(8,128)(2,1)S(1)}, bf16[128,1536]{1,0:T(8,128)(2,1)S(1)}, u32[]{:S(2)}, u32[]{:S(2)}) collective-permute-start(bf16[128,1536]{1,0:T(8,128)(2,1)S(1)} %collective-permute-done.12.refs_1_), channel_id=1, source_target_pairs={{0,16},{4,20},{8,24},{12,28},{16,0},{20,4},{24,8},{28,12},{1,17},{... | collective-permute-start | bytes 1179656 | tf_op jit(solution)/shard_map/ppermute | solution.py:695
  66.1 4.0 %collective-permute-start.39 = (f32[4,128]{1,0:T(4,128)S(1)}, f32[4,128]{1,0:T(4,128)S(1)}, u32[]{:S(2)}, u32[]{:S(2)}) collective-permute-start(f32[4,128]{1,0:T(4,128)S(1)} %pad_maximum_fusion.refs_0_), channel_id=1, source_target_pairs={{0,28},{4,24},{8,20},{12,16},{16,12},{20,8},{24,4},{28,0},{1,29},{... | collective-permute-start | bytes 6152 | tf_op jit(solution)/shard_map/ppermute | solution.py:695
  70.1 25.3 %collective-permute-start.48 = (bf16[128,1536]{1,0:T(8,128)(2,1)S(1)}, bf16[128,1536]{1,0:T(8,128)(2,1)S(1)}, u32[]{:S(2)}, u32[]{:S(2)}) collective-permute-start(bf16[128,1536]{1,0:T(8,128)(2,1)S(1)} %get-tuple-element.50), channel_id=1, source_target_pairs={{0,8},{4,12},{8,0},{12,4},{16,24},{20,28},{24,16},{28,20},{1,9},{5... | collective-permute-start | bytes 1179656 | tf_op jit(solution)/shard_map/ppermute | solution.py:695
  86.5 16.9 %collective-permute-start.50 = (bf16[128,1536]{1,0:T(8,128)(2,1)S(1)}, bf16[128,1536]{1,0:T(8,128)(2,1)S(1)}, u32[]{:S(2)}, u32[]{:S(2)}) collective-permute-start(bf16[128,1536]{1,0:T(8,128)(2,1)S(1)} %get-tuple-element.52), channel_id=1, source_target_pairs={{0,16},{4,20},{8,24},{12,28},{16,0},{20,4},{24,8},{28,12},{1,17},{... | collective-permute-start | bytes 1179656 | tf_op jit(solution)/shard_map/ppermute | solution.py:695
  87.0 16.9 %collective-permute-start.15 = (bf16[128,1536]{1,0:T(8,128)(2,1)S(1)}, bf16[128,1536]{1,0:T(8,128)(2,1)S(1)}, u32[]{:S(2)}, u32[]{:S(2)}) collective-permute-start(bf16[128,1536]{1,0:T(8,128)(2,1)S(1)} %collective-permute-done.14.refs_3_), channel_id=1, source_target_pairs={{0,8},{4,12},{8,0},{12,4},{16,24},{20,28},{24,16},{28,20},{1,9},{5... | collective-permute-start | bytes 1179656 | tf_op jit(solution)/shard_map/ppermute | solution.py:695
  87.7 23.0 %collective-permute-start.49 = (bf16[128,2304]{1,0:T(8,128)(2,1)S(1)}, bf16[128,2304]{1,0:T(8,128)(2,1)S(1)}, u32[]{:S(2)}, u32[]{:S(2)}) collective-permute-start(bf16[128,2304]{1,0:T(8,128)(2,1)S(1)} %get-tuple-element.51), channel_id=1, source_target_pairs={{0,8},{4,12},{8,0},{12,4},{16,24},{20,28},{24,16},{28,20},{1,9},{5... | collective-permute-start | bytes 1769480 | tf_op jit(solution)/shard_map/ppermute | solution.py:695
  94.9 21.1 %collective-permute-start.51 = (bf16[128,2304]{1,0:T(8,128)(2,1)S(1)}, bf16[128,2304]{1,0:T(8,128)(2,1)S(1)}, u32[]{:S(2)}, u32[]{:S(2)}) collective-permute-start(bf16[128,2304]{1,0:T(8,128)(2,1)S(1)} %get-tuple-element.53), channel_id=1, source_target_pairs={{0,16},{4,20},{8,24},{12,28},{16,0},{20,4},{24,8},{28,12},{1,17},{... | collective-permute-start | bytes 1769480 | tf_op jit(solution)/shard_map/ppermute | solution.py:695
  95.4 26.3 %collective-permute-start.52 = (bf16[128,1536]{1,0:T(8,128)(2,1)S(1)}, bf16[128,1536]{1,0:T(8,128)(2,1)S(1)}, u32[]{:S(2)}, u32[]{:S(2)}) collective-permute-start(bf16[128,1536]{1,0:T(8,128)(2,1)S(1)} %collective-permute-done.48.refs_8_), channel_id=1, source_target_pairs={{0,16},{4,20},{8,24},{12,28},{16,0},{20,4},{24,8},{28,12},{1,17},{... | collective-permute-start | bytes 1179656 | tf_op jit(solution)/shard_map/ppermute | solution.py:695
  103.3 18.4 %collective-permute-start.53 = (bf16[128,1536]{1,0:T(8,128)(2,1)S(1)}, bf16[128,1536]{1,0:T(8,128)(2,1)S(1)}, u32[]{:S(2)}, u32[]{:S(2)}) collective-permute-start(bf16[128,1536]{1,0:T(8,128)(2,1)S(1)} %collective-permute-done.50.refs_10_), channel_id=1, source_target_pairs={{0,8},{4,12},{8,0},{12,4},{16,24},{20,28},{24,16},{28,20},{1,9},{5... | collective-permute-start | bytes 1179656 | tf_op jit(solution)/shard_map/ppermute | solution.py:695
  103.9 30.6 %collective-permute-start.2 = (bf16[128,6144]{1,0:T(8,128)(2,1)S(1)}, bf16[128,6144]{1,0:T(8,128)(2,1)S(1)}, u32[]{:S(2)}, u32[]{:S(2)}) collective-permute-start(bf16[128,6144]{1,0:T(8,128)(2,1)S(1)} %copy-done.1), channel_id=1, source_target_pairs={{1,2},{2,1},{5,6},{6,5},{9,10},{10,9},{13,14},{14,13},{17,18},{18,... | collective-permute-start | bytes 4718600 | tf_op jit(solution)/shard_map/ppermute | solution.py:689
  127.4 126.0 %collective-permute-start.54 = (f32[768,1536]{1,0:T(8,128)S(1)}, f32[768,1536]{1,0:T(8,128)S(1)}, u32[]{:S(2)}, u32[]{:S(2)}) collective-permute-start(f32[768,1536]{1,0:T(8,128)S(1)} %get-tuple-element.55), channel_id=1, source_target_pairs={{0,4},{4,0},{8,12},{12,8},{16,20},{20,16},{24,28},{28,24},{1,5},{5... | collective-permute-start | bytes 14155784 | tf_op jit(solution)/shard_map/ppermute | solution.py:695
  127.4 15.8 %collective-permute-start.18 = (bf16[128,1536]{1,0:T(8,128)(2,1)S(1)}, bf16[128,1536]{1,0:T(8,128)(2,1)S(1)}, u32[]{:S(2)}, u32[]{:S(2)}) collective-permute-start(bf16[128,1536]{1,0:T(8,128)(2,1)S(1)} %get-tuple-element.42), channel_id=1, source_target_pairs={{3,0},{0,3},{7,4},{4,7},{11,8},{8,11},{15,12},{12,15},{19,16},{16,... | collective-permute-start | bytes 1179656 | tf_op jit(solution)/shard_map/ppermute | solution.py:689
  133.2 17.5 %collective-permute-start.19 = (bf16[128,1536]{1,0:T(8,128)(2,1)S(1)}, bf16[128,1536]{1,0:T(8,128)(2,1)S(1)}, u32[]{:S(2)}, u32[]{:S(2)}) collective-permute-start(bf16[128,1536]{1,0:T(8,128)(2,1)S(1)} %get-tuple-element.43), channel_id=1, source_target_pairs={{3,1},{0,2},{7,5},{4,6},{11,9},{8,10},{15,13},{12,14},{19,17},{16,... | collective-permute-start | bytes 1179656 | tf_op jit(solution)/shard_map/ppermute | solution.py:689
  134.5 64.5 %collective-permute-start.3 = (bf16[128,6144]{1,0:T(8,128)(2,1)S(1)}, bf16[128,6144]{1,0:T(8,128)(2,1)S(1)}, u32[]{:S(2)}, u32[]{:S(2)}) collective-permute-start(bf16[128,6144]{1,0:T(8,128)(2,1)S(1)} %collective-permute-done.2.refs_2_), channel_id=1, source_target_pairs={{1,0},{2,3},{5,4},{6,7},{9,8},{10,11},{13,12},{14,15},{17,16},{18,... | collective-permute-start | bytes 4718600 | tf_op jit(solution)/shard_map/ppermute | solution.py:689
  150.8 11.8 %collective-permute-start.20 = (bf16[128,1536]{1,0:T(8,128)(2,1)S(1)}, bf16[128,1536]{1,0:T(8,128)(2,1)S(1)}, u32[]{:S(2)}, u32[]{:S(2)}) collective-permute-start(bf16[128,1536]{1,0:T(8,128)(2,1)S(1)} %broadcast_select_fusion.2.refs_5_), channel_id=1, source_target_pairs={{0,8},{4,12},{8,0},{12,4},{16,24},{20,28},{24,16},{28,20},{1,9},{5... | collective-permute-start | bytes 1179656 | tf_op jit(solution)/shard_map/ppermute | solution.py:695
  151.7 15.4 %collective-permute-start.21 = (bf16[128,1536]{1,0:T(8,128)(2,1)S(1)}, bf16[128,1536]{1,0:T(8,128)(2,1)S(1)}, u32[]{:S(2)}, u32[]{:S(2)}) collective-permute-start(bf16[128,1536]{1,0:T(8,128)(2,1)S(1)} %broadcast_select_fusion.2.refs_5_), channel_id=1, source_target_pairs={{0,16},{4,20},{8,24},{12,28},{16,0},{20,4},{24,8},{28,12},{1,17},{... | collective-permute-start | bytes 1179656 | tf_op jit(solution)/shard_map/ppermute | solution.py:695
  153.7 26.7 %collective-permute-start.24 = (bf16[768,512]{1,0:T(8,128)(2,1)S(1)}, bf16[768,512]{1,0:T(8,128)(2,1)S(1)}, u32[]{:S(2)}, u32[]{:S(2)}) collective-permute-start(bf16[768,512]{1,0:T(8,128)(2,1)S(1)} %get-tuple-element.44), channel_id=1, source_target_pairs={{3,1},{0,2},{7,5},{4,6},{11,9},{8,10},{15,13},{12,14},{19,17},{16,... | collective-permute-start | bytes 2359304 | tf_op jit(solution)/shard_map/ppermute | solution.py:689
  162.5 29.3 %collective-permute-start.16 = (bf16[768,512]{1,0:T(8,128)(2,1)S(1)}, bf16[768,512]{1,0:T(8,128)(2,1)S(1)}, u32[]{:S(2)}, u32[]{:S(2)}) collective-permute-start(bf16[768,512]{1,0:T(8,128)(2,1)S(1)} %get-tuple-element.41), channel_id=1, source_target_pairs={{3,1},{0,2},{7,5},{4,6},{11,9},{8,10},{15,13},{12,14},{19,17},{16,... | collective-permute-start | bytes 2359304 | tf_op jit(solution)/shard_map/ppermute | solution.py:689
  168.9 24.5 %collective-permute-start.22 = (bf16[128,768]{1,0:T(8,128)(2,1)S(1)}, bf16[128,768]{1,0:T(8,128)(2,1)S(1)}, u32[]{:S(2)}, u32[]{:S(2)}) collective-permute-start(bf16[128,768]{1,0:T(8,128)(2,1)S(1)} %slice.28), channel_id=1, source_target_pairs={{0,16},{4,20},{8,24},{12,28},{16,0},{20,4},{24,8},{28,12},{1,17},{... | collective-permute-start | bytes 589832 | tf_op jit(solution)/shard_map/ppermute | solution.py:695
  180.4 23.7 %collective-permute-start.25 = (bf16[768,512]{1,0:T(8,128)(2,1)S(1)}, bf16[768,512]{1,0:T(8,128)(2,1)S(1)}, u32[]{:S(2)}, u32[]{:S(2)}) collective-permute-start(bf16[768,512]{1,0:T(8,128)(2,1)S(1)} %collective-permute-done.24), channel_id=1, source_target_pairs={{1,0},{2,3},{5,4},{6,7},{9,8},{10,11},{13,12},{14,15},{17,16},{18,... | collective-permute-start | bytes 2359304 | tf_op jit(solution)/shard_map/ppermute | solution.py:689
  191.8 19.3 %collective-permute-start.17 = (bf16[768,512]{1,0:T(8,128)(2,1)S(1)}, bf16[768,512]{1,0:T(8,128)(2,1)S(1)}, u32[]{:S(2)}, u32[]{:S(2)}) collective-permute-start(bf16[768,512]{1,0:T(8,128)(2,1)S(1)} %collective-permute-done.16), channel_id=1, source_target_pairs={{1,0},{2,3},{5,4},{6,7},{9,8},{10,11},{13,12},{14,15},{17,16},{18,... | collective-permute-start | bytes 2359304 | tf_op jit(solution)/shard_map/ppermute | solution.py:689
  193.3 5.7 %collective-permute-start.23 = (bf16[128,768]{1,0:T(8,128)(2,1)S(1)}, bf16[128,768]{1,0:T(8,128)(2,1)S(1)}, u32[]{:S(2)}, u32[]{:S(2)}) collective-permute-start(bf16[128,768]{1,0:T(8,128)(2,1)S(1)} %slice.29), channel_id=1, source_target_pairs={{0,8},{4,12},{8,0},{12,4},{16,24},{20,28},{24,16},{28,20},{1,9},{5... | collective-permute-start | bytes 589832 | tf_op jit(solution)/shard_map/ppermute | solution.py:695
  202.0 21.2 %collective-permute-start.4 = (bf16[128,1536]{1,0:T(8,128)(2,1)S(1)}, bf16[128,1536]{1,0:T(8,128)(2,1)S(1)}, u32[]{:S(2)}, u32[]{:S(2)}) collective-permute-start(bf16[128,1536]{1,0:T(8,128)(2,1)S(1)} %get-tuple-element.34), channel_id=1, source_target_pairs={{0,8},{4,12},{8,0},{12,4},{16,24},{20,28},{24,16},{28,20},{1,9},{5... | collective-permute-start | bytes 1179656 | tf_op jit(solution)/shard_map/ppermute | solution.py:695
  202.6 30.2 %collective-permute-start.40 = (bf16[128,2304]{1,0:T(8,128)(2,1)S(1)}, bf16[128,2304]{1,0:T(8,128)(2,1)S(1)}, u32[]{:S(2)}, u32[]{:S(2)}) collective-permute-start(bf16[128,2304]{1,0:T(8,128)(2,1)S(1)} %get-tuple-element.47), channel_id=1, source_target_pairs={{0,8},{4,12},{8,0},{12,4},{16,24},{20,28},{24,16},{28,20},{1,9},{5... | collective-permute-start | bytes 1769480 | tf_op jit(solution)/shard_map/ppermute | solution.py:695
  204.1 19.1 %collective-permute-start.55 = (f32[8,768]{1,0:T(8,128)S(1)}, f32[8,768]{1,0:T(8,128)S(1)}, u32[]{:S(2)}, u32[]{:S(2)}) collective-permute-start(f32[8,768]{1,0:T(8,128)S(1)} %get-tuple-element.57), channel_id=1, source_target_pairs={{0,4},{4,0},{8,12},{12,8},{16,20},{20,16},{24,28},{28,24},{1,5},{5... | collective-permute-start | bytes 73736 | tf_op jit(solution)/shard_map/ppermute | solution.py:695
  211.1 21.6 %collective-permute-start.6 = (bf16[128,1536]{1,0:T(8,128)(2,1)S(1)}, bf16[128,1536]{1,0:T(8,128)(2,1)S(1)}, u32[]{:S(2)}, u32[]{:S(2)}) collective-permute-start(bf16[128,1536]{1,0:T(8,128)(2,1)S(1)} %get-tuple-element.35), channel_id=1, source_target_pairs={{0,16},{4,20},{8,24},{12,28},{16,0},{20,4},{24,8},{28,12},{1,17},{... | collective-permute-start | bytes 1179656 | tf_op jit(solution)/shard_map/ppermute | solution.py:695
  223.2 21.8 %collective-permute-start.42 = (bf16[128,3072]{1,0:T(8,128)(2,1)S(1)}, bf16[128,3072]{1,0:T(8,128)(2,1)S(1)}, u32[]{:S(2)}, u32[]{:S(2)}) collective-permute-start(bf16[128,3072]{1,0:T(8,128)(2,1)S(1)} %get-tuple-element.46.refs_0_), channel_id=1, source_target_pairs={{0,4},{4,0},{8,12},{12,8},{16,20},{20,16},{24,28},{28,24},{1,5},{5... | collective-permute-start | bytes 2359304 | tf_op jit(solution)/shard_map/ppermute | solution.py:695
  223.2 19.3 %collective-permute-start.41 = (bf16[128,2304]{1,0:T(8,128)(2,1)S(1)}, bf16[128,2304]{1,0:T(8,128)(2,1)S(1)}, u32[]{:S(2)}, u32[]{:S(2)}) collective-permute-start(bf16[128,2304]{1,0:T(8,128)(2,1)S(1)} %get-tuple-element.48), channel_id=1, source_target_pairs={{0,16},{4,20},{8,24},{12,28},{16,0},{20,4},{24,8},{28,12},{1,17},{... | collective-permute-start | bytes 1769480 | tf_op jit(solution)/shard_map/ppermute | solution.py:695
  232.7 12.2 %collective-permute-start.43 = (bf16[128,1536]{1,0:T(8,128)(2,1)S(1)}, bf16[128,1536]{1,0:T(8,128)(2,1)S(1)}, u32[]{:S(2)}, u32[]{:S(2)}) collective-permute-start(bf16[128,1536]{1,0:T(8,128)(2,1)S(1)} %collective-permute-done.4.refs_1_), channel_id=1, source_target_pairs={{0,4},{4,0},{8,12},{12,8},{16,20},{20,16},{24,28},{28,24},{1,5},{5... | collective-permute-start | bytes 1179656 | tf_op jit(solution)/shard_map/ppermute | solution.py:695
  232.7 12.2 %collective-permute-start.45 = (bf16[128,1536]{1,0:T(8,128)(2,1)S(1)}, bf16[128,1536]{1,0:T(8,128)(2,1)S(1)}, u32[]{:S(2)}, u32[]{:S(2)}) collective-permute-start(bf16[128,1536]{1,0:T(8,128)(2,1)S(1)} %collective-permute-done.6.refs_3_), channel_id=1, source_target_pairs={{0,4},{4,0},{8,12},{12,8},{16,20},{20,16},{24,28},{28,24},{1,5},{5... | collective-permute-start | bytes 1179656 | tf_op jit(solution)/shard_map/ppermute | solution.py:695
  242.5 8.2 %collective-permute-start.5 = (bf16[128,1536]{1,0:T(8,128)(2,1)S(1)}, bf16[128,1536]{1,0:T(8,128)(2,1)S(1)}, u32[]{:S(2)}, u32[]{:S(2)}) collective-permute-start(bf16[128,1536]{1,0:T(8,128)(2,1)S(1)} %collective-permute-done.4.refs_1_), channel_id=1, source_target_pairs={{0,16},{4,20},{8,24},{12,28},{16,0},{20,4},{24,8},{28,12},{1,17},{... | collective-permute-start | bytes 1179656 | tf_op jit(solution)/shard_map/ppermute | solution.py:695
  245.0 7.8 %collective-permute-start.7 = (bf16[128,1536]{1,0:T(8,128)(2,1)S(1)}, bf16[128,1536]{1,0:T(8,128)(2,1)S(1)}, u32[]{:S(2)}, u32[]{:S(2)}) collective-permute-start(bf16[128,1536]{1,0:T(8,128)(2,1)S(1)} %collective-permute-done.6.refs_3_), channel_id=1, source_target_pairs={{0,8},{4,12},{8,0},{12,4},{16,24},{20,28},{24,16},{28,20},{1,9},{5... | collective-permute-start | bytes 1179656 | tf_op jit(solution)/shard_map/ppermute | solution.py:695
  245.0 7.8 %collective-permute-start.44 = (bf16[128,2304]{1,0:T(8,128)(2,1)S(1)}, bf16[128,2304]{1,0:T(8,128)(2,1)S(1)}, u32[]{:S(2)}, u32[]{:S(2)}) collective-permute-start(bf16[128,2304]{1,0:T(8,128)(2,1)S(1)} %collective-permute-done.40.refs_2_), channel_id=1, source_target_pairs={{0,4},{4,0},{8,12},{12,8},{16,20},{20,16},{24,28},{28,24},{1,5},{5... | collective-permute-start | bytes 1769480 | tf_op jit(solution)/shard_map/ppermute | solution.py:695
  245.1 8.2 %collective-permute-start.46 = (bf16[128,2304]{1,0:T(8,128)(2,1)S(1)}, bf16[128,2304]{1,0:T(8,128)(2,1)S(1)}, u32[]{:S(2)}, u32[]{:S(2)}) collective-permute-start(bf16[128,2304]{1,0:T(8,128)(2,1)S(1)} %collective-permute-done.41.refs_4_), channel_id=1, source_target_pairs={{0,4},{4,0},{8,12},{12,8},{16,20},{20,16},{24,28},{28,24},{1,5},{5... | collective-permute-start | bytes 1769480 | tf_op jit(solution)/shard_map/ppermute | solution.py:695
  250.7 5.4 %collective-permute-start.26 = (bf16[768,512]{1,0:T(8,128)(2,1)S(1)}, bf16[768,512]{1,0:T(8,128)(2,1)S(1)}, u32[]{:S(2)}, u32[]{:S(2)}) collective-permute-start(bf16[768,512]{1,0:T(8,128)(2,1)S(1)} %broadcast_select_fusion), channel_id=1, source_target_pairs={{0,4},{4,0},{8,12},{12,8},{16,20},{20,16},{24,28},{28,24},{1,5},{5... | collective-permute-start | bytes 2359304 | tf_op jit(solution)/shard_map/ppermute | solution.py:695
  (19 other events, 195.3 us)

commit v4 on v3

--- a/solution.py
+++ b/solution.py
@@ -514,7 +514,7 @@
     )(keep, xb, yb, fa, fb)
 
 
-def obs_rows(obs, places, plan, where, cols_axis):
+def obs_rows(obs, places, plan, where, cols_axis, pick):
     block_rows = obs[0].shape[1]
 
     def kernel(plan_ref, where_ref, *refs):
@@ -527,15 +527,20 @@
         end = where_ref[2]
         planes = (0, 1, 3 - end, 2 + end)
         for m, s in places:
+            line = (m % 2 * 4 + m // 2) * cols_axis + planes[s]
             rows_ref[:, at : at + block_rows] = jnp.broadcast_to(
-                held[pl.ds(m * cols_axis + planes[s], 1), :], (8, block_rows)
+                held[pl.ds(line, 1), :], (8, block_rows)
             )
             at += block_rows
-        from_row = lax.div(plan_ref[0], cols_axis)
-        from_col = lax.rem(plan_ref[0], cols_axis)
-        mask = jnp.bitwise_xor(from_row, where_ref[0])
-        step = jnp.bitwise_xor(where_ref[1], from_col)
-        picked_ref[...] = held[pl.ds(mask * cols_axis + step, 1), :]
+        if pick:
+            from_row = lax.div(plan_ref[0], cols_axis)
+            from_col = lax.rem(plan_ref[0], cols_axis)
+            mask = jnp.bitwise_xor(from_row, where_ref[0])
+            line = lax.rem(mask, 2) * 4 + lax.div(mask, 2)
+            step = jnp.bitwise_xor(where_ref[1], from_col)
+            picked_ref[...] = held[pl.ds(line * cols_axis + step, 1), :]
+        else:
+            picked_ref[...] = held[:1, :]
 
     return pl.pallas_call(
         kernel,
@@ -656,7 +661,9 @@
             bytes_accessed=2 * 10**7,
             transcendentals=0,
         ),
-        compiler_params=pltpu.CompilerParams(vmem_limit_bytes=scratch_bytes + (4 << 20)),
+        compiler_params=pltpu.CompilerParams(
+            vmem_limit_bytes=max(scratch_bytes + (4 << 20), 9 << 20)
+        ),
     )(*operands, rows, *before)
 
 
@@ -710,7 +717,8 @@
     )
     line = [near] + [cross(near, s) for s in range(1, cols_axis)]
     line_obs = jnp.stack([part[block_rows] for part in line])
-    obs = [line_obs] + [swap(line_obs, m) for m in range(1, rows_axis)]
+    obs = [line_obs] + [swap(line_obs, 2 * n) for n in range(1, 4)]
+    obs_all = obs + [swap(jnp.concatenate(obs, axis=0), 1)]
 
     def trade(xa, xb, ya, yb, keep):
         xa, ya = swap(xa, 2), swap(ya, 4)
@@ -762,14 +770,15 @@
     mid = [(2 * n + core, last - 1) for core in (0, 1) for n in range(3)]
     late = [(6 + core, last - 1) for core in (0, 1)]
     late += [(2 * n + core, last) for core in (0, 1) for n in range(4)]
-    rows, balanced_obs = obs_rows(obs, early + mid + late, plan, where, cols_axis)
+    rows_early, _ = obs_rows(obs, early, plan, where, cols_axis, False)
+    rows, balanced_obs = obs_rows(obs_all, mid + late, plan, where, cols_axis, True)
 
     blocks, operands = [], []
     for s in range(last - 1):
         blocks += part_blocks(len(operands), block_rows, 0, True)
         operands += list(traded[s])
     keep, give, keep_rhs, give_rhs = gram_direct(
-        blocks, [], operands, rows, 0, wide, cols_width, (), 2, False
+        blocks, [], operands, rows_early, 0, wide, cols_width, (), 2, False
     )
     other = swap(give, 1)
     other_rhs = swap(give_rhs, 1)
@@ -777,20 +786,19 @@
     mine = list(traded[last - 1])
     theirs = [swap(v, 1) for v in mine]
     sides = [part_blocks(0, block_rows, 0, False), part_blocks(5, block_rows, 1, False)]
-    at_row = len(early) * block_rows
     most, most_rhs = gram_direct(
         sides[0][:3] + sides[1][:3],
         [],
         mine[:5] + theirs[:5],
         rows,
-        at_row,
+        0,
         own,
         cols_width,
         (keep, other, keep_rhs, other_rhs),
         1,
         False,
     )
-    at_row += len(mid) * block_rows
+    at_row = len(mid) * block_rows
     mine_far = [far_cols, x3, y3, fa3, fb3]
     theirs_far = [swap(v, 1) for v in mine_far]
     their_rest = swap(far_rest, 1)

time: 265 us -> 263 us (level)
  starting transfers between devices: 76.1 us -> 56.6 us
  local copies, waits for them, and re-layouts: 7.3 us -> 14 us
  Pallas kernels: 25 us -> 31.5 us
  waiting for transfers between devices: 154 us -> 158 us
    ppermute x44 -> x41, starting transfers between devices: 43.4 us -> 31.6 us  [swap(): return lax.ppermute(x, 'row', [(r, r ^ mask) for r in range(rows_axis)])]
    ppermute x12, waiting for transfers between devices: 64.7 us -> 73.1 us  [hop(): return lax.ppermute(x, 'col', pairs)]
    ppermute x12, starting transfers between devices: 32.7 us -> 25.1 us  [hop(): return lax.ppermute(x, 'col', pairs)]
    unnamed x22 -> x46, local copies, waits for them, and re-layouts: 6.66 us -> 11.4 us
    pallas_call x3, Pallas kernels: 15.2 us -> 19.8 us  [gram_direct(): pl.pallas_call(kernel, in_specs=[VMEM] * (count + 1 + len(before)), out_s...]
    ppermute x44 -> x41, waiting for transfers between devices: 89.1 us -> 85.1 us  [swap(): return lax.ppermute(x, 'row', [(r, r ^ mask) for r in range(rows_axis)])]
  transfers between devices with their start and end apart: 56 -> 53, of which waited for: 23 -> 22; matrix products, arithmetic and copies ran while one was open for 0% -> 1% of each run, Pallas kernels for 7% -> 9%
where the time goes in v4:
time: 263 us; the launch traced here: 262 us
  waiting for transfers between devices  158 us (60%)
  starting transfers between devices  56.6 us (22%)
  Pallas kernels  31.5 us (12%)
  local copies, waits for them, and re-layouts  14 us (5%)
    ppermute x41, waiting for transfers between devices, swap(): return lax.ppermute(x, 'row', [(r, r ^ mask) for r in range(rows_axis)])  85.1 us
    ppermute x12, waiting for transfers between devices, hop(): return lax.ppermute(x, 'col', pairs)  73.1 us
    ppermute x41, starting transfers between devices, swap(): return lax.ppermute(x, 'row', [(r, r ^ mask) for r in range(rows_axis)])  31.6 us
    ppermute x12, starting transfers between devices, hop(): return lax.ppermute(x, 'col', pairs)  25.1 us
    pallas_call x3, Pallas kernels, gram_direct(): pl.pallas_call(kernel, in_specs=[VMEM] * (count + 1 + len(before)), out_s...  19.8 us
    unnamed x46, local copies, waits for them, and re-layouts  11.4 us
  transfers between devices with their start and end apart: 53, of which 22 were waited for; matrix products, arithmetic and copies ran while one was open for 1% of the time, Pallas kernels for 9%

profile of v4, /device:TPU:0, one launch (start us, length us, event | category | flops | bytes accessed | tf_op | source)
XLA Modules:
  0.0 262.3 jit_solution(10831607906560971450)
XLA Ops:
  0.6 3.1 %collective-permute-start.44 = (bf16[128,6144]{1,0:T(8,128)(2,1)}, bf16[128,6144]{1,0:T(8,128)(2,1)S(1)}, u32[]{:S(2)}, u32[]{:S(2)}) collective-permute-start(bf16[128,6144]{1,0:T(8,128)(2,1)} %refs_0_.1), channel_id=1, source_target_pairs={{0,1},{1,0},{2,3},{3,2},{4,5},{5,4},{6,7},{7,6},{8,9},{9,8},{10,11... | collective-permute-start | bytes 4718600 | tf_op jit(solution)/shard_map/ppermute | solution.py:696
  3.8 1.4 copy-done.1
  9.8 4.0 %head.1 = (f32[136,128]{1,0:T(8,128)S(1)}, bf16[128,1536]{1,0:T(8,128)(2,1)S(1)}, bf16[128,2304]{1,0:T(8,128)(2,1)S(1)}, bf16[128,1536]{1,0:T(8,128)(2,1)S(1)}, ...) custom-call(s32[3]{0:T(128)S(1)} %pad_add_fusion.where_ref, ...), custom_call_target="tpu_custom_call" | custom-call | flops 1000000000 | bytes 5000000 | tf_op jit(solution)/shard_map/head/pallas_call | solution.py:430
  13.8 1.6 collective-permute-start.12
  15.8 2.6 collective-permute-start.1
  19.8 21.6 %collective-permute-done.32.refs_0_ = f32[136,128]{1,0:T(8,128)S(1)} collective-permute-done((f32[136,128]{1,0:T(8,128)S(1)}, f32[136,128]{1,0:T(8,128)S(1)}, u32[]{:S(2)}, u32[]{:S(2)}) %collective-permute-start.32) | collective-permute-done | bytes 69664 | tf_op jit(solution)/shard_map/ppermute | solution.py:696
  41.3 1.7 collective-permute-start.10
  43.0 2.0 collective-permute-done.refs_0_
  45.0 1.6 collective-permute-start.33
  46.6 1.5 collective-permute-start.34
  48.1 7.8 %collective-permute-done.33.refs_1_ = f32[4,128]{1,0:T(4,128)S(1)} collective-permute-done((f32[4,128]{1,0:T(4,128)S(1)}, f32[4,128]{1,0:T(4,128)S(1)}, u32[]{:S(2)}, u32[]{:S(2)}) %collective-permute-start.33) | collective-permute-done | bytes 2080 | tf_op jit(solution)/shard_map/ppermute | solution.py:702
  57.9 1.4 collective-permute-start.13
  59.3 1.4 collective-permute-start.35
  60.8 1.9 pack_cut.3
  63.8 1.5 collective-permute-start.45
  65.3 15.2 %collective-permute-done.14.refs_3_ = bf16[128,1536]{1,0:T(8,128)(2,1)S(1)} collective-permute-done((bf16[128,1536]{1,0:T(8,128)(2,1)S(1)}, bf16[128,1536]{1,0:T(8,128)(2,1)S(1)}, u32[]{:S(2)}, u32[]{:S(2)}) %collective-permute-start.14) | collective-permute-done | bytes 393248 | tf_op jit(solution)/shard_map/ppermute | solution.py:702
  82.0 1.5 collective-permute-start.15
  84.0 5.0 %collective-permute-done.13.fa_ref.refs_5_ = bf16[128,1536]{1,0:T(8,128)(2,1)S(1)} collective-permute-done((bf16[128,1536]{1,0:T(8,128)(2,1)S(1)}, bf16[128,1536]{1,0:T(8,128)(2,1)S(1)}, u32[]{:S(2)}, u32[]{:S(2)}) %collective-permute-start.13) | collective-permute-done | bytes 393248 | tf_op jit(solution)/shard_map/ppermute | solution.py:702
  91.0 6.4 %collective-permute-done.47.refs_10_ = bf16[128,1536]{1,0:T(8,128)(2,1)S(1)} collective-permute-done((bf16[128,1536]{1,0:T(8,128)(2,1)S(1)}, bf16[128,1536]{1,0:T(8,128)(2,1)S(1)}, u32[]{:S(2)}, u32[]{:S(2)}) %collective-permute-start.47) | collective-permute-done | bytes 393248 | tf_op jit(solution)/shard_map/ppermute | solution.py:702
  101.3 2.7 %collective-permute-done.46.refs_9_ = bf16[128,2304]{1,0:T(8,128)(2,1)S(1)} collective-permute-done((bf16[128,2304]{1,0:T(8,128)(2,1)S(1)}, bf16[128,2304]{1,0:T(8,128)(2,1)S(1)}, u32[]{:S(2)}, u32[]{:S(2)}) %collective-permute-start.46) | collective-permute-done | bytes 589856 | tf_op jit(solution)/shard_map/ppermute | solution.py:702
  104.0 6.1 %collective-permute-done.48.refs_11_ = bf16[128,2304]{1,0:T(8,128)(2,1)S(1)} collective-permute-done((bf16[128,2304]{1,0:T(8,128)(2,1)S(1)}, bf16[128,2304]{1,0:T(8,128)(2,1)S(1)}, u32[]{:S(2)}, u32[]{:S(2)}) %collective-permute-start.48) | collective-permute-done | bytes 589856 | tf_op jit(solution)/shard_map/ppermute | solution.py:702
  110.0 5.9 %collective-permute-done.49.refs_12_ = bf16[128,1536]{1,0:T(8,128)(2,1)S(1)} collective-permute-done((bf16[128,1536]{1,0:T(8,128)(2,1)S(1)}, bf16[128,1536]{1,0:T(8,128)(2,1)S(1)}, u32[]{:S(2)}, u32[]{:S(2)}) %collective-permute-start.49) | collective-permute-done | bytes 393248 | tf_op jit(solution)/shard_map/ppermute | solution.py:702
  115.9 7.7 %shard_map.112 = (f32[768,1536]{1,0:T(8,128)S(1)}, f32[768,1536]{1,0:T(8,128)}, f32[8,768]{1,0:T(8,128)S(1)}, f32[8,768]{1,0:T(8,128)S(1)}) custom-call(bf16[128,3072]{1,0:T(8,128)(2,1)S(1)} %get-tuple-element.37.keep_ref.refs_0_, bf16[128,1536]{1,0:T(8,128)(2,1)S(1)} %collective-permute-done.12.refs_1_, ...), custom_call_target="tpu_custom_call" | custom-call | flops 4831838208 | bytes 20000000 | tf_op jit(solution)/shard_map/pallas_call | solution.py:652
  123.7 2.2 copy-done
  125.9 4.2 %collective-permute-start.18 = (bf16[128,1536]{1,0:T(8,128)(2,1)S(1)}, bf16[128,1536]{1,0:T(8,128)(2,1)S(1)}, u32[]{:S(2)}, u32[]{:S(2)}) collective-permute-start(bf16[128,1536]{1,0:T(8,128)(2,1)S(1)} %get-tuple-element.43), channel_id=1, source_target_pairs={{3,0},{0,3},{7,4},{4,7},{11,8},{8,11},{15,12},{12,15},{19,16},{16,... | collective-permute-start | bytes 1179656 | tf_op jit(solution)/shard_map/ppermute | solution.py:696
  132.7 9.0 %collective-permute-done.18 = bf16[128,1536]{1,0:T(8,128)(2,1)S(1)} collective-permute-done((bf16[128,1536]{1,0:T(8,128)(2,1)S(1)}, bf16[128,1536]{1,0:T(8,128)(2,1)S(1)}, u32[]{:S(2)}, u32[]{:S(2)}) %collective-permute-start.18) | collective-permute-done | bytes 393248 | tf_op jit(solution)/shard_map/ppermute | solution.py:696
  141.7 5.7 %collective-permute-done.19 = bf16[128,1536]{1,0:T(8,128)(2,1)S(1)} collective-permute-done((bf16[128,1536]{1,0:T(8,128)(2,1)S(1)}, bf16[128,1536]{1,0:T(8,128)(2,1)S(1)}, u32[]{:S(2)}, u32[]{:S(2)}) %collective-permute-start.19) | collective-permute-done | bytes 393248 | tf_op jit(solution)/shard_map/ppermute | solution.py:696
  147.4 1.6 collective-permute-start.20
  149.0 1.9 concatenate.4
  150.9 1.5 collective-permute-start.21
  156.1 5.6 %collective-permute-start.24 = (bf16[768,512]{1,0:T(8,128)(2,1)S(1)}, bf16[768,512]{1,0:T(8,128)(2,1)S(1)}, u32[]{:S(2)}, u32[]{:S(2)}) collective-permute-start(bf16[768,512]{1,0:T(8,128)(2,1)S(1)} %get-tuple-element.45), channel_id=1, source_target_pairs={{3,1},{0,2},{7,5},{4,6},{11,9},{8,10},{15,13},{12,14},{19,17},{16,... | collective-permute-start | bytes 2359304 | tf_op jit(solution)/shard_map/ppermute | solution.py:696
  161.7 1.6 collective-permute-start.16
  163.5 1.7 collective-permute-done.27.refs_11_
  165.1 1.5 collective-permute-start.22
  166.7 12.9 %collective-permute-done.24 = bf16[768,512]{1,0:T(8,128)(2,1)S(1)} collective-permute-done((bf16[768,512]{1,0:T(8,128)(2,1)S(1)}, bf16[768,512]{1,0:T(8,128)(2,1)S(1)}, u32[]{:S(2)}, u32[]{:S(2)}) %collective-permute-start.24) | collective-permute-done | bytes 786464 | tf_op jit(solution)/shard_map/ppermute | solution.py:696
  180.9 14.8 %collective-permute-done.16 = bf16[768,512]{1,0:T(8,128)(2,1)S(1)} collective-permute-done((bf16[768,512]{1,0:T(8,128)(2,1)S(1)}, bf16[768,512]{1,0:T(8,128)(2,1)S(1)}, u32[]{:S(2)}, u32[]{:S(2)}) %collective-permute-start.16) | collective-permute-done | bytes 786464 | tf_op jit(solution)/shard_map/ppermute | solution.py:696
  195.7 1.5 collective-permute-start.17
  197.8 5.6 %collective-permute-done.23.refs_9_ = bf16[128,768]{1,0:T(8,128)(2,1)S(1)} collective-permute-done((bf16[128,768]{1,0:T(8,128)(2,1)S(1)}, bf16[128,768]{1,0:T(8,128)(2,1)S(1)}, u32[]{:S(2)}, u32[]{:S(2)}) %collective-permute-start.23) | collective-permute-done | bytes 196640 | tf_op jit(solution)/shard_map/ppermute | solution.py:702
  204.0 3.3 %pack_cut.2 = (bf16[128,1536]{1,0:T(8,128)(2,1)S(1)}, bf16[128,2304]{1,0:T(8,128)(2,1)S(1)}, bf16[128,1536]{1,0:T(8,128)(2,1)S(1)}, bf16[128,2304]{1,0:T(8,128)(2,1)S(1)}, bf16[128,3072]{1,0:T(8,128)(2,1)S(1)}) custom-call(s32[48]{0:T(128)S(1)} %copy-done.14, s32[3]{0:T(128)S(1)} %pad_add_fusion.where_ref, f32[136,128]{1,0:T(8,128)S(1)} %collective-permute-done.refs_0_, ...), custom_call_target="tpu_custom_call" | custom-call | flops 1000000000 | bytes 5000000 | tf_op jit(solution)/shard_map/pack_cut/pallas_call | solution.py:482
  207.8 1.5 collective-permute-start.37
  209.3 7.0 %collective-permute-done.17 = bf16[768,512]{1,0:T(8,128)(2,1)S(1)} collective-permute-done((bf16[768,512]{1,0:T(8,128)(2,1)S(1)}, bf16[768,512]{1,0:T(8,128)(2,1)S(1)}, u32[]{:S(2)}, u32[]{:S(2)}) %collective-permute-start.17) | collective-permute-done | bytes 786464 | tf_op jit(solution)/shard_map/ppermute | solution.py:696
  216.9 2.4 collective-permute-done.4.refs_1_
  219.8 8.6 %collective-permute-done.6.refs_3_ = bf16[128,1536]{1,0:T(8,128)(2,1)S(1)} collective-permute-done((bf16[128,1536]{1,0:T(8,128)(2,1)S(1)}, bf16[128,1536]{1,0:T(8,128)(2,1)S(1)}, u32[]{:S(2)}, u32[]{:S(2)}) %collective-permute-start.6) | collective-permute-done | bytes 393248 | tf_op jit(solution)/shard_map/ppermute | solution.py:702
  228.4 2.6 collective-permute-done.37.refs_2_
  230.9 7.6 %collective-permute-done.38.refs_4_ = bf16[128,2304]{1,0:T(8,128)(2,1)S(1)} collective-permute-done((bf16[128,2304]{1,0:T(8,128)(2,1)S(1)}, bf16[128,2304]{1,0:T(8,128)(2,1)S(1)}, u32[]{:S(2)}, u32[]{:S(2)}) %collective-permute-start.38) | collective-permute-done | bytes 589856 | tf_op jit(solution)/shard_map/ppermute | solution.py:702
  240.8 6.4 %collective-permute-done.5.refs_0_ = bf16[128,1536]{1,0:T(8,128)(2,1)S(1)} collective-permute-done((bf16[128,1536]{1,0:T(8,128)(2,1)S(1)}, bf16[128,1536]{1,0:T(8,128)(2,1)S(1)}, u32[]{:S(2)}, u32[]{:S(2)}) %collective-permute-start.5) | collective-permute-done | bytes 393248 | tf_op jit(solution)/shard_map/ppermute | solution.py:702
  249.5 4.7 %shard_map.113 = (f32[768,1536]{1,0:T(8,128)S(1)}, f32[8,768]{1,0:T(8,128)S(1)}) custom-call(bf16[128,3072]{1,0:T(8,128)(2,1)S(1)} %get-tuple-element.47.refs_0_, bf16[128,1536]{1,0:T(8,128)(2,1)S(1)} %collective-permute-done.4.refs_1_, bf16[128,2304]{1,0:T(8,128)(2,1)S(1)} %collective-permute-done.37.refs_2_, ...), custom_call_target="tpu_custom_call" | custom-call | flops 1811939328 | bytes 20000000 | tf_op jit(solution)/shard_map/pallas_call | solution.py:652
  254.3 7.3 %shard_map.114 = (f32[768,1536]{1,0:T(8,128)}, f32[8,768]{1,0:T(8,128)S(1)}) custom-call(bf16[128,1536]{1,0:T(8,128)(2,1)S(1)} %collective-permute-done.5.refs_0_, bf16[128,1536]{1,0:T(8,128)(2,1)S(1)} %collective-permute-done.7.refs_1_, bf16[128,1536]{1,0:T(8,128)(2,1)S(1)} %collective-permute-done.8.refs_2_, ...), custom_call_target="tpu_custom_call" | custom-call | flops 3019898880 | bytes 20000000 | tf_op jit(solution)/shard_map/pallas_call | solution.py:652
  (127 shorter events, 32.4 us)
Async XLA Ops:
  0.6 58.7 %collective-permute-start.44 = (bf16[128,6144]{1,0:T(8,128)(2,1)}, bf16[128,6144]{1,0:T(8,128)(2,1)S(1)}, u32[]{:S(2)}, u32[]{:S(2)}) collective-permute-start(bf16[128,6144]{1,0:T(8,128)(2,1)} %refs_0_.1), channel_id=1, source_target_pairs={{0,1},{1,0},{2,3},{3,2},{4,5},{5,4},{6,7},{7,6},{8,9},{9,8},{10,11... | collective-permute-start | bytes 4718600 | tf_op jit(solution)/shard_map/ppermute | solution.py:696
  13.8 44.1 %collective-permute-start.12 = (bf16[128,1536]{1,0:T(8,128)(2,1)S(1)}, bf16[128,1536]{1,0:T(8,128)(2,1)S(1)}, u32[]{:S(2)}, u32[]{:S(2)}) collective-permute-start(bf16[128,1536]{1,0:T(8,128)(2,1)S(1)} %get-tuple-element.40), channel_id=1, source_target_pairs={{0,8},{4,12},{8,0},{12,4},{16,24},{20,28},{24,16},{28,20},{1,9},{5... | collective-permute-start | bytes 1179656 | tf_op jit(solution)/shard_map/ppermute | solution.py:702
  15.4 26.0 %collective-permute-start.32 = (f32[136,128]{1,0:T(8,128)S(1)}, f32[136,128]{1,0:T(8,128)S(1)}, u32[]{:S(2)}, u32[]{:S(2)}) collective-permute-start(f32[136,128]{1,0:T(8,128)S(1)} %get-tuple-element.34), channel_id=1, source_target_pairs={{0,1},{1,0},{2,3},{3,2},{4,5},{5,4},{6,7},{7,6},{8,9},{9,8},{10,11... | collective-permute-start | bytes 208904 | tf_op jit(solution)/shard_map/ppermute | solution.py:696
  15.8 27.2 %collective-permute-start.1 = (f32[136,128]{1,0:T(8,128)S(1)}, f32[136,128]{1,0:T(8,128)S(1)}, u32[]{:S(2)}, u32[]{:S(2)}) collective-permute-start(f32[136,128]{1,0:T(8,128)S(1)} %get-tuple-element.34), channel_id=1, source_target_pairs={{0,2},{1,3},{2,0},{3,1},{4,6},{5,7},{6,4},{7,5},{8,10},{9,11},{10,... | collective-permute-start | bytes 208904 | tf_op jit(solution)/shard_map/ppermute | solution.py:696
  18.4 26.6 %collective-permute-start = (f32[136,128]{1,0:T(8,128)S(1)}, f32[136,128]{1,0:T(8,128)S(1)}, u32[]{:S(2)}, u32[]{:S(2)}) collective-permute-start(f32[136,128]{1,0:T(8,128)S(1)} %get-tuple-element.34), channel_id=1, source_target_pairs={{0,3},{1,2},{2,1},{3,0},{4,7},{5,6},{6,5},{7,4},{8,11},{9,10},{10,... | collective-permute-start | bytes 208904 | tf_op jit(solution)/shard_map/ppermute | solution.py:696
  41.3 40.6 %collective-permute-start.10 = (bf16[128,2304]{1,0:T(8,128)(2,1)S(1)}, bf16[128,2304]{1,0:T(8,128)(2,1)S(1)}, u32[]{:S(2)}, u32[]{:S(2)}) collective-permute-start(bf16[128,2304]{1,0:T(8,128)(2,1)S(1)} %get-tuple-element.38), channel_id=1, source_target_pairs={{0,8},{4,12},{8,0},{12,4},{16,24},{20,28},{24,16},{28,20},{1,9},{5... | collective-permute-start | bytes 1769480 | tf_op jit(solution)/shard_map/ppermute | solution.py:702
  45.0 10.8 %collective-permute-start.33 = (f32[4,128]{1,0:T(4,128)S(1)}, f32[4,128]{1,0:T(4,128)S(1)}, u32[]{:S(2)}, u32[]{:S(2)}) collective-permute-start(f32[4,128]{1,0:T(4,128)S(1)} %pad_maximum_fusion.refs_0_), channel_id=1, source_target_pairs={{0,8},{4,12},{8,0},{12,4},{16,24},{20,28},{24,16},{28,20},{1,9},{5... | collective-permute-start | bytes 6152 | tf_op jit(solution)/shard_map/ppermute | solution.py:702
  46.6 10.7 %collective-permute-start.34 = (f32[4,128]{1,0:T(4,128)S(1)}, f32[4,128]{1,0:T(4,128)S(1)}, u32[]{:S(2)}, u32[]{:S(2)}) collective-permute-start(f32[4,128]{1,0:T(4,128)S(1)} %pad_maximum_fusion.refs_0_), channel_id=1, source_target_pairs={{0,16},{4,20},{8,24},{12,28},{16,0},{20,4},{24,8},{28,12},{1,17},{... | collective-permute-start | bytes 6152 | tf_op jit(solution)/shard_map/ppermute | solution.py:702
  55.9 27.5 %collective-permute-start.11 = (bf16[128,2304]{1,0:T(8,128)(2,1)S(1)}, bf16[128,2304]{1,0:T(8,128)(2,1)S(1)}, u32[]{:S(2)}, u32[]{:S(2)}) collective-permute-start(bf16[128,2304]{1,0:T(8,128)(2,1)S(1)} %get-tuple-element.39), channel_id=1, source_target_pairs={{0,16},{4,20},{8,24},{12,28},{16,0},{20,4},{24,8},{28,12},{1,17},{... | collective-permute-start | bytes 1769480 | tf_op jit(solution)/shard_map/ppermute | solution.py:702
  57.3 23.3 %collective-permute-start.14 = (bf16[128,1536]{1,0:T(8,128)(2,1)S(1)}, bf16[128,1536]{1,0:T(8,128)(2,1)S(1)}, u32[]{:S(2)}, u32[]{:S(2)}) collective-permute-start(bf16[128,1536]{1,0:T(8,128)(2,1)S(1)} %get-tuple-element.41), channel_id=1, source_target_pairs={{0,16},{4,20},{8,24},{12,28},{16,0},{20,4},{24,8},{28,12},{1,17},{... | collective-permute-start | bytes 1179656 | tf_op jit(solution)/shard_map/ppermute | solution.py:702
  57.9 31.1 %collective-permute-start.13 = (bf16[128,1536]{1,0:T(8,128)(2,1)S(1)}, bf16[128,1536]{1,0:T(8,128)(2,1)S(1)}, u32[]{:S(2)}, u32[]{:S(2)}) collective-permute-start(bf16[128,1536]{1,0:T(8,128)(2,1)S(1)} %collective-permute-done.12.refs_1_), channel_id=1, source_target_pairs={{0,16},{4,20},{8,24},{12,28},{16,0},{20,4},{24,8},{28,12},{1,17},{... | collective-permute-start | bytes 1179656 | tf_op jit(solution)/shard_map/ppermute | solution.py:702
  63.8 26.5 %collective-permute-start.45 = (bf16[128,1536]{1,0:T(8,128)(2,1)S(1)}, bf16[128,1536]{1,0:T(8,128)(2,1)S(1)}, u32[]{:S(2)}, u32[]{:S(2)}) collective-permute-start(bf16[128,1536]{1,0:T(8,128)(2,1)S(1)} %get-tuple-element.51), channel_id=1, source_target_pairs={{0,8},{4,12},{8,0},{12,4},{16,24},{20,28},{24,16},{28,20},{1,9},{5... | collective-permute-start | bytes 1179656 | tf_op jit(solution)/shard_map/ppermute | solution.py:702
  80.5 16.9 %collective-permute-start.47 = (bf16[128,1536]{1,0:T(8,128)(2,1)S(1)}, bf16[128,1536]{1,0:T(8,128)(2,1)S(1)}, u32[]{:S(2)}, u32[]{:S(2)}) collective-permute-start(bf16[128,1536]{1,0:T(8,128)(2,1)S(1)} %get-tuple-element.53), channel_id=1, source_target_pairs={{0,16},{4,20},{8,24},{12,28},{16,0},{20,4},{24,8},{28,12},{1,17},{... | collective-permute-start | bytes 1179656 | tf_op jit(solution)/shard_map/ppermute | solution.py:702
  82.0 16.8 %collective-permute-start.15 = (bf16[128,1536]{1,0:T(8,128)(2,1)S(1)}, bf16[128,1536]{1,0:T(8,128)(2,1)S(1)}, u32[]{:S(2)}, u32[]{:S(2)}) collective-permute-start(bf16[128,1536]{1,0:T(8,128)(2,1)S(1)} %collective-permute-done.14.refs_3_), channel_id=1, source_target_pairs={{0,8},{4,12},{8,0},{12,4},{16,24},{20,28},{24,16},{28,20},{1,9},{5... | collective-permute-start | bytes 1179656 | tf_op jit(solution)/shard_map/ppermute | solution.py:702
  83.4 20.5 %collective-permute-start.46 = (bf16[128,2304]{1,0:T(8,128)(2,1)S(1)}, bf16[128,2304]{1,0:T(8,128)(2,1)S(1)}, u32[]{:S(2)}, u32[]{:S(2)}) collective-permute-start(bf16[128,2304]{1,0:T(8,128)(2,1)S(1)} %get-tuple-element.52), channel_id=1, source_target_pairs={{0,8},{4,12},{8,0},{12,4},{16,24},{20,28},{24,16},{28,20},{1,9},{5... | collective-permute-start | bytes 1769480 | tf_op jit(solution)/shard_map/ppermute | solution.py:702
  89.0 21.1 %collective-permute-start.48 = (bf16[128,2304]{1,0:T(8,128)(2,1)S(1)}, bf16[128,2304]{1,0:T(8,128)(2,1)S(1)}, u32[]{:S(2)}, u32[]{:S(2)}) collective-permute-start(bf16[128,2304]{1,0:T(8,128)(2,1)S(1)} %get-tuple-element.54), channel_id=1, source_target_pairs={{0,16},{4,20},{8,24},{12,28},{16,0},{20,4},{24,8},{28,12},{1,17},{... | collective-permute-start | bytes 1769480 | tf_op jit(solution)/shard_map/ppermute | solution.py:702
  90.4 25.5 %collective-permute-start.49 = (bf16[128,1536]{1,0:T(8,128)(2,1)S(1)}, bf16[128,1536]{1,0:T(8,128)(2,1)S(1)}, u32[]{:S(2)}, u32[]{:S(2)}) collective-permute-start(bf16[128,1536]{1,0:T(8,128)(2,1)S(1)} %collective-permute-done.45.refs_8_), channel_id=1, source_target_pairs={{0,16},{4,20},{8,24},{12,28},{16,0},{20,4},{24,8},{28,12},{1,17},{... | collective-permute-start | bytes 1179656 | tf_op jit(solution)/shard_map/ppermute | solution.py:702
  97.4 18.5 %collective-permute-start.50 = (bf16[128,1536]{1,0:T(8,128)(2,1)S(1)}, bf16[128,1536]{1,0:T(8,128)(2,1)S(1)}, u32[]{:S(2)}, u32[]{:S(2)}) collective-permute-start(bf16[128,1536]{1,0:T(8,128)(2,1)S(1)} %collective-permute-done.47.refs_10_), channel_id=1, source_target_pairs={{0,8},{4,12},{8,0},{12,4},{16,24},{20,28},{24,16},{28,20},{1,9},{5... | collective-permute-start | bytes 1179656 | tf_op jit(solution)/shard_map/ppermute | solution.py:702
  98.8 32.6 %collective-permute-start.2 = (bf16[128,6144]{1,0:T(8,128)(2,1)S(1)}, bf16[128,6144]{1,0:T(8,128)(2,1)S(1)}, u32[]{:S(2)}, u32[]{:S(2)}) collective-permute-start(bf16[128,6144]{1,0:T(8,128)(2,1)S(1)} %copy-done.2), channel_id=1, source_target_pairs={{1,2},{2,1},{5,6},{6,5},{9,10},{10,9},{13,14},{14,13},{17,18},{18,... | collective-permute-start | bytes 4718600 | tf_op jit(solution)/shard_map/ppermute | solution.py:696
  125.8 123.5 %collective-permute-start.51 = (f32[768,1536]{1,0:T(8,128)}, f32[768,1536]{1,0:T(8,128)}, u32[]{:S(2)}, u32[]{:S(2)}) collective-permute-start(f32[768,1536]{1,0:T(8,128)} %get-tuple-element.57), channel_id=1, source_target_pairs={{0,4},{4,0},{8,12},{12,8},{16,20},{20,16},{24,28},{28,24},{1,5},{5... | collective-permute-start | bytes 14155784 | tf_op jit(solution)/shard_map/ppermute | solution.py:702
  125.9 15.8 %collective-permute-start.18 = (bf16[128,1536]{1,0:T(8,128)(2,1)S(1)}, bf16[128,1536]{1,0:T(8,128)(2,1)S(1)}, u32[]{:S(2)}, u32[]{:S(2)}) collective-permute-start(bf16[128,1536]{1,0:T(8,128)(2,1)S(1)} %get-tuple-element.43), channel_id=1, source_target_pairs={{3,0},{0,3},{7,4},{4,7},{11,8},{8,11},{15,12},{12,15},{19,16},{16,... | collective-permute-start | bytes 1179656 | tf_op jit(solution)/shard_map/ppermute | solution.py:696
  130.0 17.3 %collective-permute-start.19 = (bf16[128,1536]{1,0:T(8,128)(2,1)S(1)}, bf16[128,1536]{1,0:T(8,128)(2,1)S(1)}, u32[]{:S(2)}, u32[]{:S(2)}) collective-permute-start(bf16[128,1536]{1,0:T(8,128)(2,1)S(1)} %get-tuple-element.44), channel_id=1, source_target_pairs={{3,1},{0,2},{7,5},{4,6},{11,9},{8,10},{15,13},{12,14},{19,17},{16,... | collective-permute-start | bytes 1179656 | tf_op jit(solution)/shard_map/ppermute | solution.py:696
  131.4 72.1 %collective-permute-start.3 = (bf16[128,6144]{1,0:T(8,128)(2,1)S(1)}, bf16[128,6144]{1,0:T(8,128)(2,1)}, u32[]{:S(2)}, u32[]{:S(2)}) collective-permute-start(bf16[128,6144]{1,0:T(8,128)(2,1)S(1)} %collective-permute-done.2.refs_2_), channel_id=1, source_target_pairs={{1,0},{2,3},{5,4},{6,7},{9,8},{10,11},{13,12},{14,15},{17,16},{18,... | collective-permute-start | bytes 4718600 | tf_op jit(solution)/shard_map/ppermute | solution.py:696
  147.4 14.3 %collective-permute-start.20 = (bf16[128,1536]{1,0:T(8,128)(2,1)S(1)}, bf16[128,1536]{1,0:T(8,128)(2,1)S(1)}, u32[]{:S(2)}, u32[]{:S(2)}) collective-permute-start(bf16[128,1536]{1,0:T(8,128)(2,1)S(1)} %broadcast_select_fusion.2.refs_5_), channel_id=1, source_target_pairs={{0,8},{4,12},{8,0},{12,4},{16,24},{20,28},{24,16},{28,20},{1,9},{5... | collective-permute-start | bytes 1179656 | tf_op jit(solution)/shard_map/ppermute | solution.py:702
  150.9 5.2 %collective-permute-start.36 = (f32[16,128]{1,0:T(8,128)}, f32[16,128]{1,0:T(8,128)S(1)}, u32[]{:S(2)}, u32[]{:S(2)}) collective-permute-start(f32[16,128]{1,0:T(8,128)} %concatenate.4), channel_id=1, source_target_pairs={{0,4},{4,0},{8,12},{12,8},{16,20},{20,16},{24,28},{28,24},{1,5},{5... | collective-permute-start | bytes 24584 | tf_op jit(solution)/shard_map/ppermute | solution.py:702
  150.9 12.5 %collective-permute-start.21 = (bf16[128,1536]{1,0:T(8,128)(2,1)S(1)}, bf16[128,1536]{1,0:T(8,128)(2,1)S(1)}, u32[]{:S(2)}, u32[]{:S(2)}) collective-permute-start(bf16[128,1536]{1,0:T(8,128)(2,1)S(1)} %broadcast_select_fusion.2.refs_5_), channel_id=1, source_target_pairs={{0,16},{4,20},{8,24},{12,28},{16,0},{20,4},{24,8},{28,12},{1,17},{... | collective-permute-start | bytes 1179656 | tf_op jit(solution)/shard_map/ppermute | solution.py:702
  156.1 23.5 %collective-permute-start.24 = (bf16[768,512]{1,0:T(8,128)(2,1)S(1)}, bf16[768,512]{1,0:T(8,128)(2,1)S(1)}, u32[]{:S(2)}, u32[]{:S(2)}) collective-permute-start(bf16[768,512]{1,0:T(8,128)(2,1)S(1)} %get-tuple-element.45), channel_id=1, source_target_pairs={{3,1},{0,2},{7,5},{4,6},{11,9},{8,10},{15,13},{12,14},{19,17},{16,... | collective-permute-start | bytes 2359304 | tf_op jit(solution)/shard_map/ppermute | solution.py:696
  161.7 34.0 %collective-permute-start.16 = (bf16[768,512]{1,0:T(8,128)(2,1)S(1)}, bf16[768,512]{1,0:T(8,128)(2,1)S(1)}, u32[]{:S(2)}, u32[]{:S(2)}) collective-permute-start(bf16[768,512]{1,0:T(8,128)(2,1)S(1)} %get-tuple-element.42), channel_id=1, source_target_pairs={{3,1},{0,2},{7,5},{4,6},{11,9},{8,10},{15,13},{12,14},{19,17},{16,... | collective-permute-start | bytes 2359304 | tf_op jit(solution)/shard_map/ppermute | solution.py:696
  165.1 32.0 %collective-permute-start.22 = (bf16[128,768]{1,0:T(8,128)(2,1)S(1)}, bf16[128,768]{1,0:T(8,128)(2,1)S(1)}, u32[]{:S(2)}, u32[]{:S(2)}) collective-permute-start(bf16[128,768]{1,0:T(8,128)(2,1)S(1)} %slice.28), channel_id=1, source_target_pairs={{0,16},{4,20},{8,24},{12,28},{16,0},{20,4},{24,8},{28,12},{1,17},{... | collective-permute-start | bytes 589832 | tf_op jit(solution)/shard_map/ppermute | solution.py:702
  179.6 29.8 %collective-permute-start.25 = (bf16[768,512]{1,0:T(8,128)(2,1)S(1)}, bf16[768,512]{1,0:T(8,128)(2,1)S(1)}, u32[]{:S(2)}, u32[]{:S(2)}) collective-permute-start(bf16[768,512]{1,0:T(8,128)(2,1)S(1)} %collective-permute-done.24), channel_id=1, source_target_pairs={{1,0},{2,3},{5,4},{6,7},{9,8},{10,11},{13,12},{14,15},{17,16},{18,... | collective-permute-start | bytes 2359304 | tf_op jit(solution)/shard_map/ppermute | solution.py:696
  195.7 20.7 %collective-permute-start.17 = (bf16[768,512]{1,0:T(8,128)(2,1)S(1)}, bf16[768,512]{1,0:T(8,128)(2,1)S(1)}, u32[]{:S(2)}, u32[]{:S(2)}) collective-permute-start(bf16[768,512]{1,0:T(8,128)(2,1)S(1)} %collective-permute-done.16), channel_id=1, source_target_pairs={{1,0},{2,3},{5,4},{6,7},{9,8},{10,11},{13,12},{14,15},{17,16},{18,... | collective-permute-start | bytes 2359304 | tf_op jit(solution)/shard_map/ppermute | solution.py:696
  197.2 6.2 %collective-permute-start.23 = (bf16[128,768]{1,0:T(8,128)(2,1)S(1)}, bf16[128,768]{1,0:T(8,128)(2,1)S(1)}, u32[]{:S(2)}, u32[]{:S(2)}) collective-permute-start(bf16[128,768]{1,0:T(8,128)(2,1)S(1)} %slice.29), channel_id=1, source_target_pairs={{0,8},{4,12},{8,0},{12,4},{16,24},{20,28},{24,16},{28,20},{1,9},{5... | collective-permute-start | bytes 589832 | tf_op jit(solution)/shard_map/ppermute | solution.py:702
  207.2 12.1 %collective-permute-start.4 = (bf16[128,1536]{1,0:T(8,128)(2,1)S(1)}, bf16[128,1536]{1,0:T(8,128)(2,1)S(1)}, u32[]{:S(2)}, u32[]{:S(2)}) collective-permute-start(bf16[128,1536]{1,0:T(8,128)(2,1)S(1)} %get-tuple-element.35), channel_id=1, source_target_pairs={{0,8},{4,12},{8,0},{12,4},{16,24},{20,28},{24,16},{28,20},{1,9},{5... | collective-permute-start | bytes 1179656 | tf_op jit(solution)/shard_map/ppermute | solution.py:702
  207.8 23.1 %collective-permute-start.37 = (bf16[128,2304]{1,0:T(8,128)(2,1)S(1)}, bf16[128,2304]{1,0:T(8,128)(2,1)S(1)}, u32[]{:S(2)}, u32[]{:S(2)}) collective-permute-start(bf16[128,2304]{1,0:T(8,128)(2,1)S(1)} %get-tuple-element.48), channel_id=1, source_target_pairs={{0,8},{4,12},{8,0},{12,4},{16,24},{20,28},{24,16},{28,20},{1,9},{5... | collective-permute-start | bytes 1769480 | tf_op jit(solution)/shard_map/ppermute | solution.py:702
  209.3 7.6 %collective-permute-start.52 = (f32[8,768]{1,0:T(8,128)S(1)}, f32[8,768]{1,0:T(8,128)S(1)}, u32[]{:S(2)}, u32[]{:S(2)}) collective-permute-start(f32[8,768]{1,0:T(8,128)S(1)} %get-tuple-element.59), channel_id=1, source_target_pairs={{0,4},{4,0},{8,12},{12,8},{16,20},{20,16},{24,28},{28,24},{1,5},{5... | collective-permute-start | bytes 73736 | tf_op jit(solution)/shard_map/ppermute | solution.py:702
  216.4 12.0 %collective-permute-start.6 = (bf16[128,1536]{1,0:T(8,128)(2,1)S(1)}, bf16[128,1536]{1,0:T(8,128)(2,1)S(1)}, u32[]{:S(2)}, u32[]{:S(2)}) collective-permute-start(bf16[128,1536]{1,0:T(8,128)(2,1)S(1)} %get-tuple-element.36), channel_id=1, source_target_pairs={{0,16},{4,20},{8,24},{12,28},{16,0},{20,4},{24,8},{28,12},{1,17},{... | collective-permute-start | bytes 1179656 | tf_op jit(solution)/shard_map/ppermute | solution.py:702
  216.9 23.3 %collective-permute-start.39 = (bf16[128,3072]{1,0:T(8,128)(2,1)S(1)}, bf16[128,3072]{1,0:T(8,128)(2,1)S(1)}, u32[]{:S(2)}, u32[]{:S(2)}) collective-permute-start(bf16[128,3072]{1,0:T(8,128)(2,1)S(1)} %get-tuple-element.47.refs_0_), channel_id=1, source_target_pairs={{0,4},{4,0},{8,12},{12,8},{16,20},{20,16},{24,28},{28,24},{1,5},{5... | collective-permute-start | bytes 2359304 | tf_op jit(solution)/shard_map/ppermute | solution.py:702
  219.3 19.3 %collective-permute-start.38 = (bf16[128,2304]{1,0:T(8,128)(2,1)S(1)}, bf16[128,2304]{1,0:T(8,128)(2,1)S(1)}, u32[]{:S(2)}, u32[]{:S(2)}) collective-permute-start(bf16[128,2304]{1,0:T(8,128)(2,1)S(1)} %get-tuple-element.49), channel_id=1, source_target_pairs={{0,16},{4,20},{8,24},{12,28},{16,0},{20,4},{24,8},{28,12},{1,17},{... | collective-permute-start | bytes 1769480 | tf_op jit(solution)/shard_map/ppermute | solution.py:702
  228.4 10.7 %collective-permute-start.40 = (bf16[128,1536]{1,0:T(8,128)(2,1)S(1)}, bf16[128,1536]{1,0:T(8,128)(2,1)S(1)}, u32[]{:S(2)}, u32[]{:S(2)}) collective-permute-start(bf16[128,1536]{1,0:T(8,128)(2,1)S(1)} %collective-permute-done.4.refs_1_), channel_id=1, source_target_pairs={{0,4},{4,0},{8,12},{12,8},{16,20},{20,16},{24,28},{28,24},{1,5},{5... | collective-permute-start | bytes 1179656 | tf_op jit(solution)/shard_map/ppermute | solution.py:702
  230.9 9.3 %collective-permute-start.42 = (bf16[128,1536]{1,0:T(8,128)(2,1)S(1)}, bf16[128,1536]{1,0:T(8,128)(2,1)S(1)}, u32[]{:S(2)}, u32[]{:S(2)}) collective-permute-start(bf16[128,1536]{1,0:T(8,128)(2,1)S(1)} %collective-permute-done.6.refs_3_), channel_id=1, source_target_pairs={{0,4},{4,0},{8,12},{12,8},{16,20},{20,16},{24,28},{28,24},{1,5},{5... | collective-permute-start | bytes 1179656 | tf_op jit(solution)/shard_map/ppermute | solution.py:702
  238.6 8.7 %collective-permute-start.5 = (bf16[128,1536]{1,0:T(8,128)(2,1)S(1)}, bf16[128,1536]{1,0:T(8,128)(2,1)S(1)}, u32[]{:S(2)}, u32[]{:S(2)}) collective-permute-start(bf16[128,1536]{1,0:T(8,128)(2,1)S(1)} %collective-permute-done.4.refs_1_), channel_id=1, source_target_pairs={{0,16},{4,20},{8,24},{12,28},{16,0},{20,4},{24,8},{28,12},{1,17},{... | collective-permute-start | bytes 1179656 | tf_op jit(solution)/shard_map/ppermute | solution.py:702
  239.1 9.2 %collective-permute-start.7 = (bf16[128,1536]{1,0:T(8,128)(2,1)S(1)}, bf16[128,1536]{1,0:T(8,128)(2,1)S(1)}, u32[]{:S(2)}, u32[]{:S(2)}) collective-permute-start(bf16[128,1536]{1,0:T(8,128)(2,1)S(1)} %collective-permute-done.6.refs_3_), channel_id=1, source_target_pairs={{0,8},{4,12},{8,0},{12,4},{16,24},{20,28},{24,16},{28,20},{1,9},{5... | collective-permute-start | bytes 1179656 | tf_op jit(solution)/shard_map/ppermute | solution.py:702
  240.2 8.6 %collective-permute-start.41 = (bf16[128,2304]{1,0:T(8,128)(2,1)S(1)}, bf16[128,2304]{1,0:T(8,128)(2,1)S(1)}, u32[]{:S(2)}, u32[]{:S(2)}) collective-permute-start(bf16[128,2304]{1,0:T(8,128)(2,1)S(1)} %collective-permute-done.37.refs_2_), channel_id=1, source_target_pairs={{0,4},{4,0},{8,12},{12,8},{16,20},{20,16},{24,28},{28,24},{1,5},{5... | collective-permute-start | bytes 1769480 | tf_op jit(solution)/shard_map/ppermute | solution.py:702
  240.2 8.7 %collective-permute-start.43 = (bf16[128,2304]{1,0:T(8,128)(2,1)S(1)}, bf16[128,2304]{1,0:T(8,128)(2,1)S(1)}, u32[]{:S(2)}, u32[]{:S(2)}) collective-permute-start(bf16[128,2304]{1,0:T(8,128)(2,1)S(1)} %collective-permute-done.38.refs_4_), channel_id=1, source_target_pairs={{0,4},{4,0},{8,12},{12,8},{16,20},{20,16},{24,28},{28,24},{1,5},{5... | collective-permute-start | bytes 1769480 | tf_op jit(solution)/shard_map/ppermute | solution.py:702
  247.2 7.0 %collective-permute-start.26 = (bf16[768,512]{1,0:T(8,128)(2,1)S(1)}, bf16[768,512]{1,0:T(8,128)(2,1)S(1)}, u32[]{:S(2)}, u32[]{:S(2)}) collective-permute-start(bf16[768,512]{1,0:T(8,128)(2,1)S(1)} %broadcast_select_fusion), channel_id=1, source_target_pairs={{0,4},{4,0},{8,12},{12,8},{16,20},{20,16},{24,28},{28,24},{1,5},{5... | collective-permute-start | bytes 2359304 | tf_op jit(solution)/shard_map/ppermute | solution.py:702
  248.3 5.9 %collective-permute-start.28 = (bf16[128,1536]{1,0:T(8,128)(2,1)S(1)}, bf16[128,1536]{1,0:T(8,128)(2,1)S(1)}, u32[]{:S(2)}, u32[]{:S(2)}) collective-permute-start(bf16[128,1536]{1,0:T(8,128)(2,1)S(1)} %collective-permute-done.20.refs_6_), channel_id=1, source_target_pairs={{0,4},{4,0},{8,12},{12,8},{16,20},{20,16},{24,28},{28,24},{1,5},{5... | collective-permute-start | bytes 1179656 | tf_op jit(solution)/shard_map/ppermute | solution.py:702
  248.8 5.4 %collective-permute-start.29 = (bf16[128,1536]{1,0:T(8,128)(2,1)S(1)}, bf16[128,1536]{1,0:T(8,128)(2,1)S(1)}, u32[]{:S(2)}, u32[]{:S(2)}) collective-permute-start(bf16[128,1536]{1,0:T(8,128)(2,1)S(1)} %collective-permute-done.21.refs_7_), channel_id=1, source_target_pairs={{0,4},{4,0},{8,12},{12,8},{16,20},{20,16},{24,28},{28,24},{1,5},{5... | collective-permute-start | bytes 1179656 | tf_op jit(solution)/shard_map/ppermute | solution.py:702
  248.9 5.4 %collective-permute-start.8 = (bf16[128,1536]{1,0:T(8,128)(2,1)S(1)}, bf16[128,1536]{1,0:T(8,128)(2,1)S(1)}, u32[]{:S(2)}, u32[]{:S(2)}) collective-permute-start(bf16[128,1536]{1,0:T(8,128)(2,1)S(1)} %collective-permute-done.5.refs_0_), channel_id=1, source_target_pairs={{0,4},{4,0},{8,12},{12,8},{16,20},{20,16},{24,28},{28,24},{1,5},{5... | collective-permute-start | bytes 1179656 | tf_op jit(solution)/shard_map/ppermute | solution.py:702
  (28 other events, 633.6 us)
